TPU v7x, 256 devices: a whole 4x4x8 slice. The times are simulated.
256 devices in a mesh: dp: 32 (over y, z), group: 8 (over x, core).
Axes of the slice: x: 4, y: 4, z: 8, core: 2. Of those that a mesh axis runs over, the one named last changes fastest.
Arguments:
- keys: int32 [131072], P(('dp', 'group')), may hold values from 0 to 1073741823
- cut: int32 [1], replicated, may hold values from 256 to 1023
- owner: int32 [131072, 1], P(('dp', 'group')), may hold values from 0 to 31; in each aligned block of 512 rows (0 to 511, 512 to 1023, ...) at most 32 rows name the same one
- tokens: int32 [131072, 2048], P(('dp', 'group')), may hold values from 0 to 128255
Outputs:
- histogram: int32 [4096], replicated
- packed_rows: int32 [262144, 2048], P(('dp', 'group'))
- packed_weights: float32 [262144], P(('dp', 'group'))
Inputs may be any that keep to these rules, and one draw needn't show every extreme that they name: Among the examples of one device, at most 32 have the same owner, and some owner has exactly 32.
All inputs are finite; a program needn't handle non-finite values.
Results may differ from a plain program's by a relative error of at most 0.0003.
Values sent between devices are 32-bit elements; how exact they have to be, the bound alone decides.
No kernel may reach another device: no remote copies, remote signals or barrier semaphores. Data moves between devices by JAX's collectives and lax.ppermute only.
A program may use at most 128 MiB of HBM per device.

v0:
```python
import jax
import jax.numpy as jnp
from jax import lax
from jax.sharding import Mesh
from jax.sharding import PartitionSpec as P

BINS = 4096
BIN_WIDTH = 262144
DP = ("dp_0", "dp_1")
GROUP = ("group_0", "group_1")
DP_GROUP = ("dp_0", "dp_1", "group_0", "group_1")


def neutral_like(value, identity):
    return jnp.broadcast_to(jnp.asarray(identity, value.dtype), value.shape)


def prefix_by_axis(value, axes, combine, identity):
    before = start = neutral_like(value, identity)
    so_far = value
    for axis in reversed(axes):
        count, index = (lax.axis_size(axis), lax.axis_index(axis))
        pieces = lax.all_gather(so_far, axis)
        inside, so_far = (start, start)
        for k in range(count):
            passed = k < index
            so_far = combine(so_far, pieces[k])
            inside = jnp.where(passed, so_far, inside)
        before = combine(inside, before)
    return before


def split_up(value, dim, count):
    before, after = (value.shape[:dim], value.shape[dim + 1 :])
    return jnp.moveaxis(value.reshape(*before, count, -1, *after), dim, 0)


def laid_out(tiles, dim):
    tiles = jnp.moveaxis(tiles, 0, dim)
    dims = tiles.shape
    return tiles.reshape(*dims[:dim], dims[dim] * dims[dim + 1], *dims[dim + 2 :])


def exchange_both(value, axis, axes, splits, concats):
    sizes = [lax.axis_size(a) for a in axes]
    tiles = split_up(value, splits[0], sizes[0])
    tiles = jnp.moveaxis(split_up(tiles, splits[1] + 1, sizes[1]), 0, 1)
    inside = tiles.shape[2:]
    tiles = tiles.reshape(-1, *inside)
    tiles = lax.all_to_all(tiles, axis, split_axis=0, concat_axis=0, tiled=True)
    tiles = laid_out(tiles.reshape(*sizes, *inside), concats[0] + 1)
    return laid_out(tiles, concats[1])


def add_counts(earlier, later):
    return earlier + later


def body(keys, cut, owner, tokens):
    examples = keys.shape[0]
    width = tokens.shape[1]
    n_owner = lax.axis_size(DP)
    n_member = lax.axis_size(GROUP)
    slots = 2 * examples // (n_owner * n_member)
    capacity = 2 * examples
    bins_of = keys // BIN_WIDTH
    local_hist = jnp.zeros((BINS,), jnp.float32).at[bins_of].add(1.0)
    kept = bins_of >= cut[0]
    dest = owner[:, 0]
    onehot = (
        (dest[:, None] == jnp.arange(n_owner, dtype=jnp.int32)[None, :]) & kept[:, None]
    ).astype(jnp.int32)
    counts = jnp.sum(onehot, axis=0).astype(jnp.float32)
    before = prefix_by_axis(counts, DP_GROUP, add_counts, jnp.zeros_like(counts))
    hist = lax.psum(local_hist, DP_GROUP)
    running = jnp.cumsum(onehot, axis=0) - onehot
    local_rank = jnp.sum(running * onehot, axis=1)
    offset = jnp.sum(before.astype(jnp.int32)[None, :] * onehot, axis=1)
    rank = offset + local_rank
    member = rank % n_member
    outside = n_owner * n_member * slots
    position_send = jnp.where(
        kept, (dest * n_member + member) * slots + local_rank // n_member, outside
    )
    send_rows = jnp.zeros((outside, width), jnp.int32).at[position_send].set(tokens, mode="drop")
    details = jnp.stack([rank // n_member, keys], axis=1)
    send_meta = jnp.full((outside, 2), -1, jnp.int32).at[position_send].set(details, mode="drop")
    send_rows = send_rows.reshape(n_owner, n_member, slots, width)
    send_meta = send_meta.reshape(n_owner, n_member, slots, 2)
    got_rows, got_meta = (
        exchange_both(send_rows, DP_GROUP, (DP, GROUP), (0, 1), (0, 1)),
        exchange_both(send_meta, DP_GROUP, (DP, GROUP), (0, 1), (0, 1)),
    )
    got_rows = got_rows.reshape(-1, width)
    got_meta = got_meta.reshape(-1, 2)
    slot = got_meta[:, 0]
    valid = slot >= 0
    target = jnp.where(valid, slot, capacity)
    suffix = jnp.cumsum(hist[::-1])[::-1]
    total = jnp.maximum(suffix[cut[0]], 1.0)
    got_bins = jnp.clip(got_meta[:, 1] // BIN_WIDTH, 0, BINS - 1)
    weight = jnp.where(valid, suffix[got_bins] / total, 0.0)
    packed_rows = jnp.zeros((capacity, width), jnp.int32).at[target].set(got_rows, mode="drop")
    packed_weights = jnp.zeros((capacity,), jnp.float32).at[target].set(weight, mode="drop")
    return (hist.astype(jnp.int32), packed_rows, packed_weights)


def solution(mesh):
    torus = Mesh(mesh.devices.reshape(4, 8, 4, 2), ("dp_0", "dp_1", "group_0", "group_1"))
    placed = (P(DP_GROUP), P(), P(DP_GROUP, None), P(DP_GROUP, None))
    return jax.shard_map(
        body,
        mesh=torus,
        in_specs=placed,
        out_specs=(P(), P(DP_GROUP, None), P(DP_GROUP)),
        check_vma=False,
    )
```

profile of v0, /device:TPU:1, one launch (start us, length us, event | category | flops | bytes accessed | tf_op | source)
XLA Modules:
  0.0 360.7 jit_solution(18366167405808590215)
XLA Ops:
  1.3 0.7 broadcast_compare_fusion
  2.0 0.8 convert_reduce_fusion
  2.8 1.3 dynamic-slice
  4.8 5.3 %all-reduce = f32[64]{0:T(128)S(1)} all-reduce(f32[64]{0:T(128)S(1)} %convert_dynamic-update-slice_fusion), channel_id=2, replica_groups=mesh['dp_0'=4,'dp_1'=8,'group_0'=4,'group_1'=2] {'group_1'}, use_global_device_ids=true, to_apply=%add | all-reduce | flops 64 | bytes 512
  10.1 1.3 dynamic-slice.1
  12.1 0.2 fusion.35
  12.2 6.7 %all-reduce.1 = f32[128]{0:T(128)S(1)} all-reduce(f32[128]{0:T(128)S(1)} %fusion.35), channel_id=3, replica_groups=mesh['dp_0'=4,'dp_1'=8,'group_0'=4,'group_1'=2] {'group_0'}, use_global_device_ids=true, to_apply=%add.1 | all-reduce | flops 128 | bytes 1024
  19.0 15.4 %all-gather.2 = f32[8,1,32]{2,1,0:T(1,128)S(1)} all-gather(f32[1,1,32]{2,1,0:T(1,128)S(1)} %fusion.37), channel_id=1, replica_groups=mesh['dp_0'=4,'dp_1'=8,'group_0'=4,'group_1'=2] {'dp_1'}, dimensions={0}, use_global_device_ids=true | all-gather | bytes 1152 | tf_op jit(solution)/shard_map/all_gather | solution.py:23
  34.4 7.9 %all-gather.3 = f32[4,1,32]{2,1,0:T(1,128)S(1)} all-gather(f32[1,1,32]{2,1,0:T(1,128)S(1)} %bitcast.115), channel_id=1, replica_groups=mesh['dp_0'=4,'dp_1'=8,'group_0'=4,'group_1'=2] {'dp_0'}, dimensions={0}, use_global_device_ids=true | all-gather | bytes 640 | tf_op jit(solution)/shard_map/all_gather | solution.py:23
  42.4 0.7 fusion.10
  43.1 1.2 reduce-window.15
  44.2 0.2 slice_reduce_fusion
  44.6 0.8 select_reduce_fusion
  45.4 0.7 compare_select_fusion.6
  46.1 0.7 pad_add_fusion
  46.8 0.1 copy.12
  47.0 1.8 scatter_custom_fusion.1
  48.8 2.3 copy.14
  51.1 13.2 %all-to-all-start = ((s32[256,1,1,4,2]{3,4,2,1,0:T(2,128)}), s32[256,1,1,4,2]{3,4,2,1,0:T(2,128)S(1)}, u32[]{:S(2)}, u32[]{:S(2)}) async-start(s32[256,1,1,4,2]{3,4,2,1,0:T(2,128)} %copy.14), calls=%async_computation | async-start | bytes 524288 | tf_op jit(solution)/shard_map/all_to_all | solution.py:50
  64.3 8.6 %scatter_custom_fusion.2 = s32[1024,2048]{1,0:T(8,128)} fusion(s32[512]{0:T(512)S(1)} %get-tuple-element.5, s32[512,2048]{1,0:T(8,128)} %param.7, s32[]{:T(128)} %constant.97.clone.1), kind=kCustom, calls=%fused_computation.8 | custom fusion | bytes 8389120 | tf_op jit(solution)/shard_map/scatter | solution.py:85
  72.9 9.8 %reshape_transpose_transpose_reshape_reshape_reshape.7 = s32[256,1,1,4,2048]{4,3,0,2,1:T(4,128)} reshape(s32[1024,2048]{1,0:T(8,128)} %scatter_custom_fusion.2) | data formatting | bytes 16777216 | tf_op jit(solution)/shard_map/reshape;transpose;transpose;reshape;reshape;reshape | solution.py:49
  82.7 14.9 %all-to-all-start.1 = ((s32[256,1,1,4,2048]{4,3,2,1,0:T(4,128)}), s32[256,1,1,4,2048]{4,3,2,1,0:T(4,128)}, u32[]{:S(2)}, u32[]{:S(2)}) async-start(s32[256,1,1,4,2048]{4,3,2,1,0:T(4,128)} %bitcast.102), calls=%async_computation.1 | async-start | bytes 16777216 | tf_op jit(solution)/shard_map/all_to_all | solution.py:50
  97.6 3.3 scatter_custom_fusion
  100.8 222.9 %psum.7 = f32[4096]{0:T(1024)S(1)} all-reduce(f32[4096]{0:T(1024)S(1)} %scatter_custom_fusion), channel_id=1, replica_groups=mesh['dp_0'=4,'dp_1'=8,'group_0'=4,'group_1'=2] {'dp_0','dp_1','group_0'..., use_global_device_ids=true, to_apply=%region_1.2 | all-reduce | flops 4096 | bytes 32768 | tf_op jit(solution)/shard_map/psum | solution.py:75
  323.8 0.6 convert_element_type.27
  324.4 0.3 reduce-window.19
  325.1 0.6 dynamic_slice.3
  326.4 0.2 reshape_reshape.6
  326.6 6.2 %gather_fusion = f32[1024]{0:T(1024)S(1)} fusion(f32[4096]{0:T(1024)S(1)} %rev.7, s32[1024]{0:T(1024)S(1)} %broadcast_clamp_fusion), kind=kCustom, calls=%fused_computation | custom fusion | bytes 12288 | tf_op jit(solution)/shard_map/gather | solution.py:102
  332.8 4.9 %scatter_custom_fusion.4 = f32[1024]{0:T(1024)} fusion(s32[1024]{0:T(1024)S(1)} %bitcast.116, f32[1024]{0:T(1024)S(1)} %divide_select_fusion, f32[]{:T(128)} %constant.95.clone.1), kind=kCustom, calls=%fused_computation.65 | custom fusion | bytes 4100 | tf_op jit(solution)/shard_map/scatter | solution.py:104
  337.7 10.0 %reshape.165 = s32[1024,2048]{1,0:T(8,128)} reshape(s32[32,8,1,4,2048]{4,3,1,0,2:T(4,128)} %bitcast.31) | data formatting | bytes 16777216 | tf_op jit(solution)/shard_map/reshape;reshape | solution.py:94
  347.7 13.0 %scatter_custom_fusion.3 = s32[1024,2048]{1,0:T(8,128)} fusion(s32[1024]{0:T(1024)S(1)} %bitcast.117, s32[1024,2048]{1,0:T(8,128)} %reshape.165, s32[]{:T(128)} %constant.97.clone.1), kind=kCustom, calls=%fused_computation.6 | custom fusion | bytes 8389120 | tf_op jit(solution)/shard_map/scatter | solution.py:103
  (24 shorter events, 0.9 us)
Async XLA Ops:
  51.1 31.6 %all-to-all-start = ((s32[256,1,1,4,2]{3,4,2,1,0:T(2,128)}), s32[256,1,1,4,2]{3,4,2,1,0:T(2,128)S(1)}, u32[]{:S(2)}, u32[]{:S(2)}) async-start(s32[256,1,1,4,2]{3,4,2,1,0:T(2,128)} %copy.14), calls=%async_computation | async-start | bytes 524288 | tf_op jit(solution)/shard_map/all_to_all | solution.py:50
  82.7 255.0 %all-to-all-start.1 = ((s32[256,1,1,4,2048]{4,3,2,1,0:T(4,128)}), s32[256,1,1,4,2048]{4,3,2,1,0:T(4,128)}, u32[]{:S(2)}, u32[]{:S(2)}) async-start(s32[256,1,1,4,2048]{4,3,2,1,0:T(4,128)} %bitcast.102), calls=%async_computation.1 | async-start | bytes 16777216 | tf_op jit(solution)/shard_map/all_to_all | solution.py:50
where the time goes:
time: 362 us; the launch traced here: 361 us
  blocking collectives  258 us (71%)
  local copies, waits for them, and re-layouts  60.7 us (17%)
  starting transfers between devices  28 us (8%)
  other arithmetic  10.4 us (3%)
    psum x1, blocking collectives, body(): hist = lax.psum(local_hist, DP_GROUP)  223 us
    all_to_all x2, starting transfers between devices, exchange_both(): tiles = lax.all_to_all(tiles, axis, split_axis=0, concat_axis=0, tiled=True)  28 us
    all_gather x2, blocking collectives, prefix_by_axis(): pieces = lax.all_gather(so_far, axis)  23.3 us
    scatter x1, local copies, waits for them, and re-layouts, body(): jnp.zeros((capacity, width), jnp.int32).at[target]  13 us
    another operation x2, local copies, waits for them, and re-layouts, exchange_both(): tiles = tiles.reshape(-1, *inside)  12.1 us
    unnamed x2, blocking collectives  12 us
    another operation x1, local copies, waits for them, and re-layouts, body(): got_rows = got_rows.reshape(-1, width)  10 us
    scatter x1, local copies, waits for them, and re-layouts, body(): jnp.zeros((outside, width), jnp.int32).at[position_send]  8.6 us
  transfers between devices with their start and end apart: 2, of which 0 were waited for; matrix products, arithmetic and copies ran while one was open for 10% of the time, Pallas kernels for 0%

commit v1 on v0

v1 whole, which is shorter than its diff:
```python
import jax
import jax.numpy as jnp
from jax import lax
from jax.experimental import pallas as pl
from jax.experimental.pallas import tpu as pltpu
from jax.sharding import Mesh
from jax.sharding import PartitionSpec as P

BINS = 4096
KEY_SHIFT = 18
DP = ("dp_0", "dp_1")
GROUP = ("group_0", "group_1")
DP_GROUP = ("dp_0", "dp_1", "group_0", "group_1")
LANES = 128
STEP = 64

SMEM = pltpu.MemorySpace.SMEM
VMEM = pltpu.MemorySpace.VMEM


def smem_spec():
    return pl.BlockSpec(memory_space=SMEM)


def any_spec():
    return pl.BlockSpec(memory_space=pl.MemorySpace.ANY)


def pack_rows(keys, dest, info, tokens, n_dev, n_member, slots):
    examples, width = tokens.shape
    tiles = width // LANES
    steps = examples // STEP
    n_owner = n_dev // n_member

    def kernel(keys_ref, dest_ref, info_ref, tok_ref, rows_ref, meta_ref, buf, seen, sent, sem):
        g = pl.program_id(0)

        @pl.when(g == 0)
        def _():
            sent[0] = 0
            for o in range(n_owner):
                seen[o] = 0

        @pl.when(g < steps)
        def _():
            for r in range(STEP // 8):
                for k in range(tiles):
                    at = (g * STEP + r * 8) * tiles + k
                    buf[pl.ds(at, 8, stride=tiles), :] = tok_ref[r * 8 : r * 8 + 8, k * LANES : (k + 1) * LANES]

        @pl.when(g > 0)
        def _():
            lowest = info_ref[0] << KEY_SHIFT

            def row(i, total):
                key = keys_ref[i]
                kept = key >= lowest

                @pl.when(kept)
                def _():
                    o = dest_ref[i]
                    local = seen[o]
                    seen[o] = local + 1
                    member = (info_ref[1 + o] + local) & (n_member - 1)
                    to = (o * n_member + member) * slots + local // n_member
                    meta_ref[to] = key
                    pltpu.make_async_copy(
                        buf.at[pl.ds(pl.multiple_of(i * tiles, tiles), tiles)],
                        rows_ref.at[pl.ds(pl.multiple_of(to * tiles, tiles), tiles)],
                        sem,
                    ).start()

                return total + kept.astype(jnp.int32)

            start = (g - 1) * STEP
            sent[0] = lax.fori_loop(start, start + STEP, row, sent[0])

        @pl.when(g == steps)
        def _():
            def drain(i, carry):
                pltpu.make_async_copy(buf.at[pl.ds(0, tiles)], rows_ref.at[pl.ds(0, tiles)], sem).wait()
                return carry

            lax.fori_loop(0, sent[0], drain, 0)

    return pl.pallas_call(
        kernel,
        grid=(steps + 1,),
        in_specs=[
            smem_spec(),
            smem_spec(),
            smem_spec(),
            pl.BlockSpec((STEP, width), lambda g: (jnp.minimum(g, steps - 1), 0)),
        ],
        out_specs=[any_spec(), smem_spec()],
        out_shape=[
            jax.ShapeDtypeStruct((n_dev * slots * tiles, LANES), tokens.dtype),
            jax.ShapeDtypeStruct((n_dev * slots,), keys.dtype),
        ],
        scratch_shapes=[
            pltpu.VMEM((examples * tiles, LANES), tokens.dtype),
            pltpu.SMEM((n_owner,), jnp.int32),
            pltpu.SMEM((1,), jnp.int32),
            pltpu.SemaphoreType.DMA,
        ],
        name="pack_rows",
    )(keys, dest, info, tokens)


def incoming(counts_ref, member, n_dev, n_member, visit, carry):
    def source(s, state):
        before, carry = state
        count = counts_ref[s]
        first = (member - before) & (n_member - 1)
        rows = (count - first + n_member - 1) >> 3
        carry = visit(s, (before + first) >> 3, rows, carry)
        return before + count, carry

    return lax.fori_loop(0, n_dev, source, (0, carry))


def place_weights(counts, member, got_keys, suffix, n_dev, n_member, slots, capacity):
    def kernel(counts_ref, member_ref, keys_ref, suffix_ref, out_ref):
        def clear(i, carry):
            for j in range(8):
                out_ref[i * 8 + j] = 0.0
            return carry

        lax.fori_loop(0, capacity // 8, clear, 0)

        def visit(s, slot, rows, carry):
            def one(q, c):
                out_ref[slot + q] = suffix_ref[keys_ref[s * slots + q] >> KEY_SHIFT]
                return c

            return lax.fori_loop(0, rows, one, carry)

        incoming(counts_ref, member_ref[0], n_dev, n_member, visit, 0)

    return pl.pallas_call(
        kernel,
        in_specs=[smem_spec()] * 4,
        out_specs=smem_spec(),
        out_shape=jax.ShapeDtypeStruct((capacity,), jnp.float32),
        name="place_weights",
    )(counts, member, got_keys, suffix)


def unpack_rows(counts, member, got, n_dev, n_member, slots, capacity, width):
    tiles = width // LANES
    steps = capacity // STEP

    def kernel(counts_ref, member_ref, got_ref, out_ref, buf, pending, filled, sems):
        g = pl.program_id(0)

        @pl.when(g == 0)
        def _():
            for b in range(steps):
                pending[b] = 0

            def visit(s, slot, rows, carry):
                b = slot // STEP

                @pl.when(rows > 0)
                def _():
                    pending[b] = pending[b] + rows

                for n in range(1, slots + 1):

                    @pl.when(rows == n)
                    def _(n=n):
                        pltpu.make_async_copy(
                            got_ref.at[pl.ds(pl.multiple_of(s * (slots * tiles), tiles), n * tiles)],
                            buf.at[pl.ds(pl.multiple_of(slot * tiles, tiles), n * tiles)],
                            sems.at[b],
                        ).start()

                return carry

            total, _ = incoming(counts_ref, member_ref[0], n_dev, n_member, visit, 0)
            filled[0] = (total - member_ref[0] + n_member - 1) >> 3

        def drain(i, carry):
            pltpu.make_async_copy(got_ref.at[pl.ds(0, tiles)], buf.at[pl.ds(0, tiles)], sems.at[g]).wait()
            return carry

        lax.fori_loop(0, pending[g], drain, 0)
        index = g * STEP + lax.broadcasted_iota(jnp.int32, (8, LANES), 0)
        for r in range(STEP // 8):
            real = index + r * 8 < filled[0]
            for k in range(tiles):
                at = (g * STEP + r * 8) * tiles + k
                rows = buf[pl.ds(at, 8, stride=tiles), :]
                out_ref[r * 8 : r * 8 + 8, k * LANES : (k + 1) * LANES] = jnp.where(real, rows, 0)

    return pl.pallas_call(
        kernel,
        grid=(steps,),
        in_specs=[smem_spec(), smem_spec(), any_spec()],
        out_specs=pl.BlockSpec((STEP, width), lambda g: (g, 0)),
        out_shape=jax.ShapeDtypeStruct((capacity, width), got.dtype),
        scratch_shapes=[
            pltpu.VMEM((capacity * tiles, LANES), got.dtype),
            pltpu.SMEM((steps,), jnp.int32),
            pltpu.SMEM((1,), jnp.int32),
            pltpu.SemaphoreType.DMA((steps,)),
        ],
        name="unpack_rows",
    )(counts, member, got)


def exchange(value):
    return lax.all_to_all(value, DP_GROUP, split_axis=0, concat_axis=0, tiled=True)


def body(keys, cut, owner, tokens):
    examples = keys.shape[0]
    width = tokens.shape[1]
    n_owner = lax.axis_size(DP)
    n_member = lax.axis_size(GROUP)
    n_dev = n_owner * n_member
    slots = 2 * examples // n_dev
    capacity = 2 * examples
    piece = BINS // n_dev
    me = lax.axis_index(DP_GROUP)
    member = lax.axis_index(GROUP)
    bins_of = keys >> KEY_SHIFT
    dest = owner[:, 0]
    kept = bins_of >= cut[0]
    owners = jnp.arange(n_owner, dtype=jnp.int32)
    counts = jnp.sum(((dest[:, None] == owners[None, :]) & kept[:, None]).astype(jnp.int32), axis=0)
    local_hist = jnp.zeros((BINS,), jnp.int32).at[bins_of].add(1)
    first = jnp.concatenate(
        [local_hist.reshape(n_dev, piece), jnp.broadcast_to(counts[None, :], (n_dev, n_owner))], axis=1
    )
    first = exchange(first)
    piece_sum = jnp.sum(first[:, :piece], axis=0)
    table = first[:, piece:]
    earlier = jnp.arange(n_dev, dtype=jnp.int32)[:, None] < me
    before = jnp.sum(jnp.where(earlier, table, 0), axis=0)
    mine = lax.dynamic_slice_in_dim(table, me // n_member, 1, axis=1)[:, 0]
    info = jnp.concatenate([cut, before])
    send_rows, send_keys = pack_rows(keys, dest, info, tokens, n_dev, n_member, slots)
    second = jnp.concatenate(
        [send_keys.reshape(n_dev, slots), jnp.broadcast_to(piece_sum[None, :], (n_dev, piece))], axis=1
    )
    second = exchange(second)
    got_keys = second[:, :slots].reshape(-1)
    hist = second[:, slots:].reshape(-1)
    got = exchange(send_rows.reshape(n_dev, slots, width // LANES, LANES)).reshape(-1, LANES)
    suffix = jnp.cumsum(hist.astype(jnp.float32)[::-1])[::-1]
    total = jnp.maximum(suffix[cut[0]], 1.0)
    member = member[None].astype(jnp.int32)
    weights = place_weights(mine, member, got_keys, suffix, n_dev, n_member, slots, capacity) / total
    packed = unpack_rows(mine, member, got, n_dev, n_member, slots, capacity, width)
    return (hist, packed, weights)


def solution(mesh):
    torus = Mesh(mesh.devices.reshape(4, 8, 4, 2), ("dp_0", "dp_1", "group_0", "group_1"))
    placed = (P(DP_GROUP), P(), P(DP_GROUP, None), P(DP_GROUP, None))
    return jax.shard_map(
        body,
        mesh=torus,
        in_specs=placed,
        out_specs=(P(), P(DP_GROUP, None), P(DP_GROUP)),
        check_vma=False,
    )
```

time: 362 us -> 285 us (0.79)
  blocking collectives: 258 us -> 18.1 us
  waiting for transfers between devices: 0.01 us -> 186 us
  local copies, waits for them, and re-layouts: 60.7 us -> 3.6 us
  Pallas kernels: 0 us -> 42.8 us
  starting transfers between devices: 28 us -> 22.9 us
    psum x1 -> x0, blocking collectives: 223 us -> none  [body(): hist = lax.psum(local_hist, DP_GROUP)]
    all_to_all x2, waiting for transfers between devices: 0.01 us -> 186 us  [exchange(): lax.all_to_all(value, DP_GROUP, split_axis=0, concat_axis=0, tiled=True)]
    pallas_call x0 -> x3, Pallas kernels: none -> 42.8 us  [the longest x1 18.3 us: pack_rows(): pl.pallas_call(kernel, grid=(steps + 1,), in_specs=[smem_spec(), smem_spe...]
    scatter x4 -> x0, local copies, waits for them, and re-layouts: 28.4 us -> none  [the longest x1 13 us: body(): jnp.zeros((capacity, width), jnp.int32).at[target]]
    all_gather x2 -> x0, blocking collectives: 23.3 us -> none  [prefix_by_axis(): pieces = lax.all_gather(so_far, axis)]
    another operation x8 -> x1, local copies, waits for them, and re-layouts: 22.6 us -> 0.11 us  [the longest x2 12.1 us: exchange_both(): tiles = tiles.reshape(-1, *inside)]
    all_to_all x0 -> x1, blocking collectives: none -> 18.1 us  [exchange(): lax.all_to_all(value, DP_GROUP, split_axis=0, concat_axis=0, tiled=True)]
    unnamed x2 -> x0, blocking collectives: 12 us -> none
  transfers between devices with their start and end apart: 2 -> 2, of which waited for: 0 -> 2; matrix products, arithmetic and copies ran while one was open for 10% -> 1% of each run, Pallas kernels for 0% -> 3%
where the time goes in v1:
time: 285 us; the launch traced here: 284 us
  waiting for transfers between devices  186 us (65%)
  Pallas kernels  42.8 us (15%)
  starting transfers between devices  22.9 us (8%)
  blocking collectives  18.1 us (6%)
  other arithmetic  8.7 us (3%)
  local copies, waits for them, and re-layouts  3.6 us (1%)
    all_to_all x2, waiting for transfers between devices, exchange(): lax.all_to_all(value, DP_GROUP, split_axis=0, concat_axis=0, tiled=True)  186 us
    all_to_all x2, starting transfers between devices, exchange(): lax.all_to_all(value, DP_GROUP, split_axis=0, concat_axis=0, tiled=True)  22.9 us
    pallas_call x1, Pallas kernels, pack_rows(): pl.pallas_call(kernel, grid=(steps + 1,), in_specs=[smem_spec(), smem_spe...  18.3 us
    all_to_all x1, blocking collectives, exchange(): lax.all_to_all(value, DP_GROUP, split_axis=0, concat_axis=0, tiled=True)  18.1 us
    pallas_call x1, Pallas kernels, unpack_rows(): pl.pallas_call(kernel, grid=(steps,), in_specs=[smem_spec(), smem_spec(),...  15.3 us
    pallas_call x1, Pallas kernels, place_weights(): pl.pallas_call(kernel, in_specs=[smem_spec()] * 4, out_specs=smem_spec(),...  9.22 us
  transfers between devices with their start and end apart: 2, of which 2 were waited for; matrix products, arithmetic and copies ran while one was open for 1% of the time, Pallas kernels for 3%

profile of v1, /device:TPU:1, one launch (start us, length us, event | category | flops | bytes accessed | tf_op | source)
XLA Modules:
  0.0 284.4 jit_solution(7601716730290090100)
XLA Ops:
  1.3 0.7 compare_select_fusion
  2.0 0.7 shift-right-arithmetic_compare_fusion
  2.7 0.8 convert_reduce_fusion
  3.5 0.1 pad.5.clone
  3.5 3.3 %scatter_custom_fusion = s32[4096]{0:T(1024)S(1)} fusion(s32[512]{0:T(512)S(1)} %compare_select_fusion, s32[512]{0:T(512)S(1)} %broadcast.14, s32[]{:T(128)} %constant.45.clone.1), kind=kCustom, calls=%fused_computation.11 | custom fusion | flops 512 | bytes 16388 | tf_op jit(solution)/shard_map/scatter-add | solution.py:232
  6.8 0.1 reshape.52
  6.9 0.7 pad_add_fusion
  7.6 15.6 %all-to-all-start = ((s32[256,1,48]{2,1,0:T(1,128)}), s32[256,1,48]{2,1,0:T(1,128)S(1)}, u32[]{:S(2)}, u32[]{:S(2)}) async-start(s32[256,1,48]{2,1,0:T(1,128)} %bitcast.2), calls=%async_computation | async-start | bytes 262144 | tf_op jit(solution)/shard_map/all_to_all | solution.py:213
  23.2 12.7 %all-to-all-done = s32[256,1,48]{2,1,0:T(1,128)S(1)} async-done(((s32[256,1,48]{2,1,0:T(1,128)}), s32[256,1,48]{2,1,0:T(1,128)S(1)}, u32[]{:S(2)}, u32[]{:S(2)}) %all-to-all-start) | async-done | bytes 49184 | tf_op jit(solution)/shard_map/all_to_all | solution.py:213
  36.0 0.1 pad.1.clone
  36.1 0.1 fusion.3
  36.2 0.7 pad_add_fusion.2.info_ref
  36.9 18.3 %pack_rows.1 = (s32[16384,128]{1,0:T(8,128)}, s32[1024]{0:T(1024)}) custom-call(s32[512]{0:T(512)} %keys_ref.1, s32[512]{0:T(512)} %bitcast.26, s32[33]{0:T(128)} %pad_add_fusion.2.info_ref, s32[512,2048]{1,0:T(8,128)} %tok_ref.1), custom_call_target="tpu_custom_call" | custom-call | tf_op jit(solution)/shard_map/pack_rows/pallas_call | solution.py:86
  55.2 0.8 reshape.53
  56.0 18.1 %all_to_all.29 = s32[256,1,20]{2,1,0:T(1,128)S(1)} all-to-all(s32[256,1,20]{2,1,0:T(1,128)S(1)} %bitcast.23), channel_id=1, replica_groups=mesh['dp_0'=4,'dp_1'=8,'group_0'=4,'group_1'=2] {'dp_0','dp_1','group_0'..., dimensions={0} | all-to-all | bytes 40960 | tf_op jit(solution)/shard_map/all_to_all | solution.py:213
  74.2 7.2 %all-to-all-start.2 = ((s32[256,4,16,128]{3,2,1,0:T(8,128)}), s32[256,4,16,128]{3,2,1,0:T(8,128)}, u32[]{:S(2)}, u32[]{:S(2)}) async-start(s32[256,4,16,128]{3,2,1,0:T(8,128)} %bitcast.18), calls=%async_computation.2 | async-start | bytes 16777216 | tf_op jit(solution)/shard_map/all_to_all | solution.py:213
  81.4 0.7 dynamic-slice_reduce_fusion.counts_ref
  82.2 0.1 slice.27
  82.2 0.7 reshape.57.keys_ref
  83.0 0.1 reshape.54
  83.1 0.1 rev.6
  83.2 0.3 reduce-window.9
  83.5 0.1 slice.29
  83.5 0.1 reduce-window.12
  83.6 0.1 slice_reduce_fusion.1
  83.7 0.1 add_bitcast_fusion
  83.8 0.1 rev.7.suffix_ref
  83.9 0.6 dynamic_slice.7
  85.0 9.2 %place_weights.1 = f32[1024]{0:T(1024)} custom-call(s32[256]{0:T(256)} %dynamic-slice_reduce_fusion.counts_ref, s32[1]{0:T(128)} %bitcast.6.member_ref, s32[1024]{0:T(1024)} %reshape.57.keys_ref, f32[4096]{0:T(1024)} %copy-done.1), custom_call_target="tpu_custom_call" | custom-call | tf_op jit(solution)/shard_map/place_weights/pallas_call | solution.py:140
  94.2 1.3 broadcast_divide_fusion
  95.5 173.6 %all-to-all-done.2 = s32[256,4,16,128]{3,2,1,0:T(8,128)} async-done(((s32[256,4,16,128]{3,2,1,0:T(8,128)}), s32[256,4,16,128]{3,2,1,0:T(8,128)}, u32[]{:S(2)}, u32[]{:S(2)}) %all-to-all-start.2) | async-done | bytes 8388640 | tf_op jit(solution)/shard_map/all_to_all | solution.py:213
  269.1 15.3 %unpack_rows.1 = s32[1024,2048]{1,0:T(8,128)} custom-call(s32[256]{0:T(256)} %dynamic-slice_reduce_fusion.counts_ref, s32[1]{0:T(128)} %bitcast.6.member_ref, s32[16384,128]{1,0:T(8,128)} %bitcast.8.got_ref), custom_call_target="tpu_custom_call" | custom-call | tf_op jit(solution)/shard_map/unpack_rows/pallas_call | solution.py:196
  (9 shorter events, 0.1 us)
Async XLA Ops:
  7.6 28.4 %all-to-all-start = ((s32[256,1,48]{2,1,0:T(1,128)}), s32[256,1,48]{2,1,0:T(1,128)S(1)}, u32[]{:S(2)}, u32[]{:S(2)}) async-start(s32[256,1,48]{2,1,0:T(1,128)} %bitcast.2), calls=%async_computation | async-start | bytes 262144 | tf_op jit(solution)/shard_map/all_to_all | solution.py:213
  74.2 194.9 %all-to-all-start.2 = ((s32[256,4,16,128]{3,2,1,0:T(8,128)}), s32[256,4,16,128]{3,2,1,0:T(8,128)}, u32[]{:S(2)}, u32[]{:S(2)}) async-start(s32[256,4,16,128]{3,2,1,0:T(8,128)} %bitcast.18), calls=%async_computation.2 | async-start | bytes 16777216 | tf_op jit(solution)/shard_map/all_to_all | solution.py:213
  83.1 201.3 %copy-start = (s32[4096]{0:T(1024)}, s32[4096]{0:T(1024)S(1)}, u32[]{:S(2)}) copy-start(s32[4096]{0:T(1024)S(1)} %reshape.54) | copy-start | bytes 49156
  83.9 1.1 copy-start.1

commit v2 on v1

--- a/solution.py
+++ b/solution.py
@@ -6,6 +6,7 @@
 from jax.sharding import Mesh
 from jax.sharding import PartitionSpec as P
 
+
 BINS = 4096
 KEY_SHIFT = 18
 DP = ("dp_0", "dp_1")
@@ -15,7 +16,6 @@
 STEP = 64
 
 SMEM = pltpu.MemorySpace.SMEM
-VMEM = pltpu.MemorySpace.VMEM
 
 
 def smem_spec():
@@ -23,7 +23,7 @@
 
 
 def any_spec():
-    return pl.BlockSpec(memory_space=pl.MemorySpace.ANY)
+    return pl.BlockSpec(memory_space=pltpu.MemorySpace.HBM)
 
 
 def pack_rows(keys, dest, info, tokens, n_dev, n_member, slots):
@@ -209,13 +209,292 @@
     )(counts, member, got)
 
 
-def exchange(value):
-    return lax.all_to_all(value, DP_GROUP, split_axis=0, concat_axis=0, tiled=True)
-
-
-def body(keys, cut, owner, tokens):
+CAPS = (288, 216, 144, 56)
+OWN = 128
+
+
+def segments(k):
+    edges = (0,) + CAPS[::-1]
+    return [(edges[j], edges[j + 1] - edges[j]) for j in range(5 - k)]
+
+
+def pack_relay(source, tokens):
+    examples, width = tokens.shape
+    tiles = width // LANES
+    steps = examples // STEP
+    sizes = [n for _, n in segments(1)] * 2 + [OWN]
+
+    def kernel(source_ref, tok_ref, *rest):
+        outs, (buf, sem) = rest[: len(sizes)], rest[len(sizes) :]
+        g = pl.program_id(0)
+
+        @pl.when(g < steps)
+        def _():
+            for r in range(STEP // 8):
+                for k in range(tiles):
+                    at = (g * STEP + r * 8) * tiles + k
+                    buf[pl.ds(at, 8, stride=tiles), :] = tok_ref[r * 8 : r * 8 + 8, k * LANES : (k + 1) * LANES]
+
+        @pl.when(g == steps)
+        def _():
+            start = 0
+            for out, size in zip(outs, sizes):
+
+                def some(i, carry, out=out, start=start):
+                    for j in range(8):
+                        p = i * 8 + j
+                        row = source_ref[start + p]
+                        pltpu.make_async_copy(
+                            buf.at[pl.ds(pl.multiple_of(row * tiles, tiles), tiles)],
+                            out.at[pl.ds(pl.multiple_of(p * tiles, tiles), tiles)],
+                            sem,
+                        ).start()
+                    return carry
+
+                lax.fori_loop(0, size // 8, some, 0)
+                start += size
+            for out, size in zip(outs, sizes):
+                pltpu.make_async_copy(buf.at[pl.ds(0, size * tiles)], out, sem).wait()
+
+    return pl.pallas_call(
+        kernel,
+        grid=(steps + 1,),
+        in_specs=[smem_spec(), pl.BlockSpec((STEP, width), lambda g: (jnp.minimum(g, steps - 1), 0))],
+        out_specs=[any_spec()] * len(sizes),
+        out_shape=[jax.ShapeDtypeStruct((n * tiles, LANES), tokens.dtype) for n in sizes],
+        scratch_shapes=[pltpu.VMEM((examples * tiles, LANES), tokens.dtype), pltpu.SemaphoreType.DMA],
+        name="pack_relay",
+    )(source, tokens)
+
+
+ROUNDS = ((0, 1), (2,), (3, 4))
+
+
+def lanes_of(hop):
+    if hop == 0:
+        return [((0,), 4)]
+    if hop == 4:
+        return [((0, 1), 4)]
+    return [((0,), 4), ((1,), 4)]
+
+
+def slot_map():
+    found = {}
+    for n, hops in enumerate(ROUNDS):
+        skip = 0
+        for hop in hops:
+            for sides, slots in lanes_of(hop):
+                for side in sides:
+                    found[hop if side == 0 else (8 - hop) % 8] = (n, skip)
+                skip += slots
+        for d, (m, at) in list(found.items()):
+            if m == n and not isinstance(at, tuple):
+                found[d] = (m, (at, skip))
+    return {d: (n, rows, at) for d, (n, (at, rows)) in found.items()}
+
+
+def spread(n, place, counts, befores, pieces, n_member, tiles):
+    slots = slot_map()
+    width = next(rows for m, rows, _ in slots.values() if m == n)
+    total = 4 * n_member * width * tiles
+    origins, held = {}, 0
+    for hop, side, start, rows, _ in pieces:
+        if (hop, side) not in origins:
+            rows_in = OWN if hop == 0 else CAPS[hop - 1]
+            origins[hop, side] = (held, rows_in)
+            held += rows_in + 32
+    arrays = [array for *_, array in pieces]
+
+    def kernel(place_ref, counts_ref, befores_ref, *rest):
+        ins, (out, buf, sem_in, sem_out) = rest[: len(pieces)], rest[len(pieces) :]
+        loads = []
+        for (hop, side, start, rows, _), ref in zip(pieces, ins):
+            at = (origins[hop, side][0] + start) * tiles
+            loads.append(pltpu.make_async_copy(ref, buf.at[pl.ds(at, rows * tiles)], sem_in))
+        for load in loads:
+            load.start()
+        z = place_ref[0]
+        todo = []
+        for (hop, side), (base, rows_in) in origins.items():
+            sign = 1 - 2 * side
+            origin = (z - sign * hop) & 7
+
+            def share(y, k, origin=origin, sign=sign, side=side):
+                count = counts_ref[origin * 32 + y * 8 + ((origin + sign * k) & 7)]
+                return (count + 1 - side) >> 1 if k == 4 else count
+
+            at = 0
+            if hop > 0:
+                for k in range(hop + 1, 5):
+                    for y in range(4):
+                        at += share(y, k)
+            for y in range(4):
+                todo.append((hop, side, y, base + jnp.minimum(at, rows_in), befores_ref[origin * 32 + y * 8 + z]))
+                at += share(y, hop)
+        for load in loads:
+            load.wait()
+        for hop, side, y, first, before in todo:
+            skip = slots[hop if side == 0 else (8 - hop) % 8][2]
+            for j in range(16 if hop == 4 else 32):
+                local = 2 * j + side if hop == 4 else j
+                member = (before + local) & (n_member - 1)
+                to = (y * n_member + member) * width + skip + local // n_member
+                pltpu.make_async_copy(
+                    buf.at[pl.ds(pl.multiple_of((first + j) * tiles, tiles), tiles)],
+                    out.at[pl.ds(pl.multiple_of(to * tiles, tiles), tiles)],
+                    sem_out,
+                ).start()
+        pltpu.make_async_copy(buf.at[pl.ds(0, total)], out, sem_out).wait()
+
+    return pl.pallas_call(
+        kernel,
+        in_specs=[smem_spec()] * 3 + [any_spec()] * len(pieces),
+        out_specs=any_spec(),
+        out_shape=jax.ShapeDtypeStruct((total, LANES), arrays[0].dtype),
+        scratch_shapes=[
+            pltpu.VMEM((max(held * tiles, total), LANES), arrays[0].dtype),
+            pltpu.SemaphoreType.DMA,
+            pltpu.SemaphoreType.DMA,
+        ],
+    )(place, counts, befores, *arrays)
+
+
+def unpack_relay(place, counts, befores, got, n_member, capacity, width):
+    tiles = width // LANES
+    steps = capacity // STEP
+    slots = 4
+    where = slot_map()
+
+    def kernel(place_ref, counts_ref, befores_ref, *rest):
+        ins, (out_ref, buf, pending, sems) = rest[: len(got)], rest[len(got) :]
+        g = pl.program_id(0)
+        z, member = place_ref[0], place_ref[1]
+        last = 32 * n_member - 1
+        filled = (befores_ref[last] + counts_ref[last] - member + n_member - 1) >> 3
+
+        @pl.when(g == 0)
+        def _():
+            for b in range(steps):
+                pending[b] = 0
+            for d in range(8):
+                n, rows_each, skip = where[d]
+                ref = ins[n]
+                origin = (z - d) & 7
+
+                def sender(i, carry, ref=ref, rows_each=rows_each, skip=skip, origin=origin):
+                    s = ((i >> 3) * 8 + origin) * n_member + (i & 7)
+                    before = befores_ref[s]
+                    first = (member - before) & (n_member - 1)
+                    rows = (counts_ref[s] - first + n_member - 1) >> 3
+                    slot = (before + first) >> 3
+                    b = slot // STEP
+                    at = i * rows_each + skip
+
+                    @pl.when(rows > 0)
+                    def _():
+                        pending[b] = pending[b] + rows
+
+                    for n in range(1, slots + 1):
+
+                        @pl.when(rows == n)
+                        def _(n=n):
+                            pltpu.make_async_copy(
+                                ref.at[pl.ds(pl.multiple_of(at * tiles, tiles), n * tiles)],
+                                buf.at[pl.ds(pl.multiple_of(slot * tiles, tiles), n * tiles)],
+                                sems.at[b],
+                            ).start()
+
+                    return carry
+
+                lax.fori_loop(0, 4 * n_member, sender, 0)
+
+        def drain(i, carry):
+            pltpu.make_async_copy(ins[0].at[pl.ds(0, tiles)], buf.at[pl.ds(0, tiles)], sems.at[g]).wait()
+            return carry
+
+        lax.fori_loop(0, pending[g], drain, 0)
+        index = g * STEP + lax.broadcasted_iota(jnp.int32, (8, LANES), 0)
+        for r in range(STEP // 8):
+            real = index + r * 8 < filled
+            for k in range(tiles):
+                at = (g * STEP + r * 8) * tiles + k
+                rows = buf[pl.ds(at, 8, stride=tiles), :]
+                out_ref[r * 8 : r * 8 + 8, k * LANES : (k + 1) * LANES] = jnp.where(real, rows, 0)
+
+    return pl.pallas_call(
+        kernel,
+        grid=(steps,),
+        in_specs=[smem_spec()] * 3 + [any_spec()] * len(got),
+        out_specs=pl.BlockSpec((STEP, width), lambda g: (g, 0)),
+        out_shape=jax.ShapeDtypeStruct((capacity, width), got[0].dtype),
+        scratch_shapes=[
+            pltpu.VMEM((capacity * tiles, LANES), got[0].dtype),
+            pltpu.SMEM((steps,), jnp.int32),
+            pltpu.SemaphoreType.DMA((steps,)),
+        ],
+        name="unpack_relay",
+    )(place, counts, befores, *got)
+
+
+def relay_source(counts, local_rank, onehot, z):
+    owner = jnp.arange(32, dtype=jnp.int32)
+    y, d = owner // 8, (owner - z) % 8
+    dist = jnp.minimum(d, 8 - d)
+    order = (4 - dist) * 4 + y
+    plus = (d >= 1) & (d <= 4)
+    minus = d >= 4
+    own = d == 0
+    size_plus = jnp.where(d == 4, (counts + 1) >> 1, counts)
+    size_minus = jnp.where(d == 4, counts >> 1, counts)
+    earlier = order[None, :] < order[:, None]
+
+    def start(members, sizes):
+        return jnp.sum(jnp.where(earlier & members[None, :], sizes[None, :], 0), axis=1)
+
+    side = CAPS[0]
+    base = jnp.where(own, 2 * side + start(own, counts), jnp.where(plus, start(plus, size_plus), side + start(minus, size_minus)))
+    other = side + start(minus, size_minus)
+    limit = jnp.where(own, 2 * side + OWN, jnp.where(plus, side, 2 * side))
+
+    def pick(values):
+        return jnp.sum(onehot * values[None, :], axis=1)
+
+    four = pick((d == 4).astype(jnp.int32)) == 1
+    odd = four & ((local_rank & 1) == 1)
+    position = jnp.where(odd, pick(other), pick(base)) + jnp.where(four, local_rank >> 1, local_rank)
+    bound = jnp.where(odd, 2 * side, pick(limit))
+    position = jnp.where((jnp.sum(onehot, axis=1) == 1) & (position < bound), position, -1)
+    example = jnp.arange(onehot.shape[0], dtype=jnp.int32)
+    places = jnp.arange(2 * side + OWN, dtype=jnp.int32)
+    return jnp.sum(jnp.where(position[None, :] == places[:, None], example[None, :], 0), axis=1)
+
+
+def relay_fits(table):
+    n_dev = table.shape[0]
+    z = (jnp.arange(n_dev, dtype=jnp.int32)[:, None] // 8) % 8
+    d = (jnp.arange(32, dtype=jnp.int32)[None, :] - z) % 8
+    plus = jnp.where(d == 4, (table + 1) >> 1, table)
+    over = jnp.zeros((), jnp.int32)
+    for k, cap in enumerate(CAPS, 1):
+        ahead = jnp.sum(jnp.where((d >= k) & (d <= 4), plus, 0), axis=1)
+        behind = jnp.sum(jnp.where((d <= 8 - k) & (d >= 4), jnp.where(d == 4, table >> 1, table), 0), axis=1)
+        over = jnp.maximum(over, jnp.max(jnp.maximum(ahead, behind)) - cap)
+    return over <= 0
+
+
+def exchange(value, axes=DP_GROUP):
+    return lax.all_to_all(value, axes, split_axis=0, concat_axis=0, tiled=True)
+
+
+def hop_on(value, step):
+    count = lax.axis_size("dp_1")
+    return lax.ppermute(value, "dp_1", [(i, (i + step) % count) for i in range(count)])
+
+
+def program(keys, cut, owner, tokens):
     examples = keys.shape[0]
     width = tokens.shape[1]
+    tiles = width // LANES
     n_owner = lax.axis_size(DP)
     n_member = lax.axis_size(GROUP)
     n_dev = n_owner * n_member
@@ -224,35 +503,86 @@
     piece = BINS // n_dev
     me = lax.axis_index(DP_GROUP)
     member = lax.axis_index(GROUP)
+    y, z = lax.axis_index("dp_0"), lax.axis_index("dp_1")
     bins_of = keys >> KEY_SHIFT
     dest = owner[:, 0]
     kept = bins_of >= cut[0]
     owners = jnp.arange(n_owner, dtype=jnp.int32)
-    counts = jnp.sum(((dest[:, None] == owners[None, :]) & kept[:, None]).astype(jnp.int32), axis=0)
+    onehot = ((dest[:, None] == owners[None, :]) & kept[:, None]).astype(jnp.int32)
+    counts = jnp.sum(onehot, axis=0)
+    index = jnp.arange(examples, dtype=jnp.int32)
+    lower = (index[None, :] < index[:, None]).astype(jnp.bfloat16)
+    running = jnp.dot(lower, onehot.astype(jnp.bfloat16), preferred_element_type=jnp.float32).astype(jnp.int32)
+    local_rank = jnp.sum(running * onehot, axis=1)
+    source = relay_source(counts, local_rank, onehot, z)
+    *pieces, own = pack_relay(source, tokens)
+    plus, minus = pieces[:4], pieces[4:]
+
     local_hist = jnp.zeros((BINS,), jnp.int32).at[bins_of].add(1)
     first = jnp.concatenate(
         [local_hist.reshape(n_dev, piece), jnp.broadcast_to(counts[None, :], (n_dev, n_owner))], axis=1
     )
+    first, _ = lax.optimization_barrier((first, source))
     first = exchange(first)
     piece_sum = jnp.sum(first[:, :piece], axis=0)
     table = first[:, piece:]
-    earlier = jnp.arange(n_dev, dtype=jnp.int32)[:, None] < me
-    before = jnp.sum(jnp.where(earlier, table, 0), axis=0)
-    mine = lax.dynamic_slice_in_dim(table, me // n_member, 1, axis=1)[:, 0]
-    info = jnp.concatenate([cut, before])
-    send_rows, send_keys = pack_rows(keys, dest, info, tokens, n_dev, n_member, slots)
+    device = jnp.arange(n_dev, dtype=jnp.int32)
+    below = (device[None, :] < device[:, None]).astype(jnp.bfloat16)
+    befores = jnp.dot(below, table.astype(jnp.bfloat16), preferred_element_type=jnp.float32).astype(jnp.int32)
+    before = lax.dynamic_slice_in_dim(befores, me, 1, axis=0)[0]
+
+    def column(values):
+        return lax.dynamic_slice_in_dim(values, me // n_member, 1, axis=1)[:, 0]
+
+    def line(values):
+        return lax.dynamic_slice(values.reshape(4, 8, n_member, n_owner), (y, 0, member, 0), (1, 8, 1, n_owner)).reshape(-1)
+
+    mine, mine_before = column(table), column(befores)
+    line_counts, line_befores = line(table), line(befores)
+    fits = relay_fits(table)
+    place = jnp.stack([z, member]).astype(jnp.int32)
+
+    late_keys, late_dest, before = lax.optimization_barrier((keys, dest, before))
+    late_kept = late_keys >> KEY_SHIFT >= cut[0]
+    late = (late_dest[:, None] == owners[None, :]) & late_kept[:, None]
+    rank = jnp.sum(jnp.where(late, before[None, :], 0), axis=1) + local_rank
+    to = jnp.where(late_kept, (dest * n_member + rank % n_member) * slots + local_rank // n_member, n_dev * slots)
+    send_keys = jnp.zeros((n_dev * slots,), jnp.int32).at[to].set(keys, mode="drop")
     second = jnp.concatenate(
         [send_keys.reshape(n_dev, slots), jnp.broadcast_to(piece_sum[None, :], (n_dev, piece))], axis=1
     )
     second = exchange(second)
+    arrived = {0: [(0, 0, 0, OWN, own)]}
+    for k in range(1, 5):
+        plus = [hop_on(v, 1) for v in plus[: 5 - k]]
+        minus = [hop_on(v, -1) for v in minus[: 5 - k]]
+        arrived[k] = [(k, i, *span, v) for i, side in enumerate((plus, minus)) for span, v in zip(segments(k), side)]
+    got = []
+    for n, hops in enumerate(ROUNDS):
+        laid = spread(n, place, line_counts, line_befores, [p for k in hops for p in arrived[k]], n_member, tiles)
+        laid = laid.reshape(n_owner, -1, tiles, LANES)
+        if n == 0:
+            laid, second = lax.optimization_barrier((laid, second))
+        else:
+            laid, got[-1] = lax.optimization_barrier((laid, got[-1]))
+        got.append(exchange(laid, ("dp_0",) + GROUP).reshape(-1, LANES))
+
     got_keys = second[:, :slots].reshape(-1)
     hist = second[:, slots:].reshape(-1)
-    got = exchange(send_rows.reshape(n_dev, slots, width // LANES, LANES)).reshape(-1, LANES)
     suffix = jnp.cumsum(hist.astype(jnp.float32)[::-1])[::-1]
     total = jnp.maximum(suffix[cut[0]], 1.0)
-    member = member[None].astype(jnp.int32)
-    weights = place_weights(mine, member, got_keys, suffix, n_dev, n_member, slots, capacity) / total
-    packed = unpack_rows(mine, member, got, n_dev, n_member, slots, capacity, width)
+    weights = place_weights(mine, member[None], got_keys, suffix, n_dev, n_member, slots, capacity) / total
+
+    def relayed(got):
+        return unpack_relay(place, mine, mine_before, got, n_member, capacity, width)
+
+    def direct(got):
+        info = jnp.concatenate([cut, before])
+        send_rows, _ = pack_rows(keys, dest, info, tokens, n_dev, n_member, slots)
+        rows = exchange(send_rows.reshape(n_dev, slots, tiles, LANES)).reshape(-1, LANES)
+        return unpack_rows(mine, member[None], rows, n_dev, n_member, slots, capacity, width)
+
+    packed = lax.cond(fits, relayed, direct, got)
     return (hist, packed, weights)
 
 
@@ -260,7 +590,7 @@
     torus = Mesh(mesh.devices.reshape(4, 8, 4, 2), ("dp_0", "dp_1", "group_0", "group_1"))
     placed = (P(DP_GROUP), P(), P(DP_GROUP, None), P(DP_GROUP, None))
     return jax.shard_map(
-        body,
+        program,
         mesh=torus,
         in_specs=placed,
         out_specs=(P(), P(DP_GROUP, None), P(DP_GROUP)),

time: 285 us -> 280 us (0.982)
  waiting for transfers between devices: 186 us -> 116 us
  starting transfers between devices: 22.9 us -> 78.8 us
  blocking collectives: 18.1 us -> 0 us
  local copies, waits for them, and re-layouts: 3.6 us -> 13 us
  Pallas kernels: 42.8 us -> 50.4 us
  other arithmetic: 8.7 us -> 11.9 us
  between operations: 2 us -> 5.14 us
    all_to_all x2 -> x5, waiting for transfers between devices: 186 us -> 25.2 us  [exchange(): return lax.all_to_all(value, axes, split_axis=0, concat_axis=0, tiled=True)]
    ppermute x0 -> x20, waiting for transfers between devices: none -> 91.1 us  [hop_on(): lax.ppermute(value, 'dp_1', [(i, (i + step) % count) for i in range(count)])]
    all_to_all x2 -> x5, starting transfers between devices: 22.9 us -> 52.2 us  [exchange(): return lax.all_to_all(value, axes, split_axis=0, concat_axis=0, tiled=True)]
    ppermute x0 -> x20, starting transfers between devices: none -> 26.6 us  [hop_on(): lax.ppermute(value, 'dp_1', [(i, (i + step) % count) for i in range(count)])]
    all_to_all x1 -> x0, blocking collectives: 18.1 us -> none  [exchange(): lax.all_to_all(value, DP_GROUP, split_axis=0, concat_axis=0, tiled=True)]
    pallas_call x2 -> x5, Pallas kernels: 33.6 us -> 41.7 us  [the longest x1 19.1 us: unpack_relay(): pl.pallas_call(kernel, grid=(steps,), in_specs=[smem_spec()] * 3 + [any_s...]
    unnamed x4 -> x28, local copies, waits for them, and re-layouts: 0.01 us -> 5.13 us
  transfers between devices with their start and end apart: 2 -> 25, of which waited for: 2 -> 9; matrix products, arithmetic and copies ran while one was open for 1% -> 4% of each run, Pallas kernels for 3% -> 11%
where the time goes in v2:
time: 280 us; the launch traced here: 277 us
  waiting for transfers between devices  116 us (41%)
  starting transfers between devices  78.8 us (28%)
  Pallas kernels  50.4 us (18%)
  local copies, waits for them, and re-layouts  13 us (5%)
  other arithmetic  11.9 us (4%)
  between operations  5.14 us (2%)
    ppermute x20, waiting for transfers between devices, hop_on(): lax.ppermute(value, 'dp_1', [(i, (i + step) % count) for i in range(count)])  91.1 us
    all_to_all x5, starting transfers between devices, exchange(): return lax.all_to_all(value, axes, split_axis=0, concat_axis=0, tiled=True)  52.2 us
    ppermute x20, starting transfers between devices, hop_on(): lax.ppermute(value, 'dp_1', [(i, (i + step) % count) for i in range(count)])  26.6 us
    all_to_all x5, waiting for transfers between devices, exchange(): return lax.all_to_all(value, axes, split_axis=0, concat_axis=0, tiled=True)  25.2 us
    pallas_call x1, Pallas kernels, unpack_relay(): pl.pallas_call(kernel, grid=(steps,), in_specs=[smem_spec()] * 3 + [any_s...  19.1 us
    pallas_call x3, Pallas kernels, spread(): pl.pallas_call(kernel, in_specs=[smem_spec()] * 3 + [any_spec()] * len(pi...  14.2 us
    pallas_call x1, Pallas kernels, place_weights(): pl.pallas_call(kernel, in_specs=[smem_spec()] * 4, out_specs=smem_spec(),...  8.73 us
    pallas_call x1, Pallas kernels, pack_relay(): pl.pallas_call(kernel, grid=(steps + 1,), in_specs=[smem_spec(), pl.Block...  8.4 us
  transfers between devices with their start and end apart: 25, of which 9 were waited for; matrix products, arithmetic and copies ran while one was open for 4% of the time, Pallas kernels for 11%

profile of v2, /device:TPU:1, one launch (start us, length us, event | category | flops | bytes accessed | tf_op | source)
XLA Modules:
  0.0 277.0 jit_solution(697721302938136046)
XLA Ops:
  6.6 3.3 %scatter_custom_fusion = s32[4096]{0:T(1024)S(1)} fusion(s32[512]{0:T(512)S(1)} %compare_select_fusion.1, s32[512]{0:T(512)S(1)} %broadcast.509, s32[]{:T(128)} %constant.153.clone.1), kind=kCustom, calls=%fused_computation.61 | custom fusion | flops 512 | bytes 16388 | tf_op jit(solution)/shard_map/scatter-add | solution.py:521
  10.9 15.6 %all-to-all-start.1 = ((s32[256,1,48]{2,1,0:T(1,128)}), s32[256,1,48]{2,1,0:T(1,128)S(1)}, u32[]{:S(2)}, u32[]{:S(2)}) async-start(s32[256,1,48]{2,1,0:T(1,128)} %bitcast.9), calls=%async_computation.1 | async-start | bytes 262144 | tf_op jit(solution)/shard_map/all_to_all | solution.py:486
  26.5 8.4 %pack_relay.1 = (s32[896,128]{1,0:T(8,128)}, s32[1408,128]{1,0:T(8,128)}, s32[1152,128]{1,0:T(8,128)}, s32[1152,128]{1,0:T(8,128)}, s32[896,128]{1,0:T(8,128)}, ...) custom-call(s32[704]{0:T(1024)} %select_reduce_fusion.source_ref, ...), custom_call_target="tpu_custom_call" | custom-call | tf_op jit(solution)/shard_map/pack_relay/pallas_call | solution.py:259
  34.9 1.6 collective-permute-start
  36.5 2.9 %collective-permute-start.4 = (s32[896,128]{1,0:T(8,128)}, s32[896,128]{1,0:T(8,128)S(1)}, u32[]{:S(2)}, u32[]{:S(2)}) collective-permute-start(s32[896,128]{1,0:T(8,128)} %get-tuple-element.78), channel_id=1, source_target_pairs={{0,56},{8,0},{16,8},{24,16},{32,24},{40,32},{48,40},{56,48},{1,57}... | collective-permute-start | bytes 1376264 | tf_op jit(solution)/shard_map/ppermute | solution.py:491
  39.4 2.7 collective-permute-start.5
  42.9 6.7 %collective-permute-done.rest_1_ = s32[896,128]{1,0:T(8,128)S(1)} collective-permute-done((s32[896,128]{1,0:T(8,128)}, s32[896,128]{1,0:T(8,128)S(1)}, u32[]{:S(2)}, u32[]{:S(2)}) %collective-permute-start) | collective-permute-done | bytes 458784 | tf_op jit(solution)/shard_map/ppermute | solution.py:491
  51.2 1.9 collective-permute-start.6
  53.1 9.2 %collective-permute-done.2.rest_3_ = s32[1152,128]{1,0:T(8,128)S(1)} collective-permute-done((s32[1152,128]{1,0:T(8,128)}, s32[1152,128]{1,0:T(8,128)S(1)}, u32[]{:S(2)}, u32[]{:S(2)}) %collective-permute-start.2) | collective-permute-done | bytes 589856 | tf_op jit(solution)/shard_map/ppermute | solution.py:491
  62.3 1.6 collective-permute-start.7
  63.9 2.4 scatter_custom_fusion.1
  67.1 12.9 %all-to-all-start.2 = ((s32[256,1,20]{2,1,0:T(1,128)}), s32[256,1,20]{2,1,0:T(1,128)S(1)}, u32[]{:S(2)}, u32[]{:S(2)}) async-start(s32[256,1,20]{2,1,0:T(1,128)} %bitcast.14), calls=%async_computation.2 | async-start | bytes 262144 | tf_op jit(solution)/shard_map/all_to_all | solution.py:486
  81.9 8.5 %collective-permute-done.3.rest_4_ = s32[1152,128]{1,0:T(8,128)} collective-permute-done((s32[1152,128]{1,0:T(8,128)}, s32[1152,128]{1,0:T(8,128)}, u32[]{:S(2)}, u32[]{:S(2)}) %collective-permute-start.3) | collective-permute-done | bytes 589856 | tf_op jit(solution)/shard_map/ppermute | solution.py:491
  91.8 5.4 %shard_map.67 = s32[6144,128]{1,0:T(8,128)} custom-call(s32[2]{0:T(128)S(1)} %pad_add_fusion.3.place_ref, s32[256]{0:T(256)} %reshape.271.counts_ref, s32[256]{0:T(256)} %reshape.273.befores_ref, s32[2048,128]{1,0:T(8,128)} %get-tuple-element.73.rest_0_, s32[896,128]{1,0:T(8,128)} %copy-done.9, s32[1408,128]{1,0:T(8,128)} %copy-done, s32[1152,128]{1,0:T(8,128)} %copy-done.2, ...), custom_call_target="tpu_custom_call" | custom-call | tf_op jit(solution)/shard_map/pallas_call | solution.py:349
  97.1 2.6 all-to-all-done.2
  99.7 7.0 %all-to-all-start.3 = ((s32[32,12,16,128]{3,2,1,0:T(8,128)}), s32[32,12,16,128]{3,2,1,0:T(8,128)S(1)}, u32[]{:S(2)}, u32[]{:S(2)}) async-start(s32[32,12,16,128]{3,2,1,0:T(8,128)} %bitcast.33), calls=%async_computation.3 | async-start | bytes 6291456 | tf_op jit(solution)/shard_map/all_to_all | solution.py:486
  108.9 1.8 collective-permute-start.14
  110.7 2.4 collective-permute-start.18
  113.4 7.8 %collective-permute-done.8.rest_0_ = s32[896,128]{1,0:T(8,128)} collective-permute-done((s32[896,128]{1,0:T(8,128)}, s32[896,128]{1,0:T(8,128)}, u32[]{:S(2)}, u32[]{:S(2)}) %collective-permute-start.8) | collective-permute-done | bytes 458784 | tf_op jit(solution)/shard_map/ppermute | solution.py:491
  122.4 29.2 %collective-permute-done.12.rest_3_ = s32[896,128]{1,0:T(8,128)} collective-permute-done((s32[896,128]{1,0:T(8,128)}, s32[896,128]{1,0:T(8,128)}, u32[]{:S(2)}, u32[]{:S(2)}) %collective-permute-start.12) | collective-permute-done | bytes 458784 | tf_op jit(solution)/shard_map/ppermute | solution.py:491
  151.6 4.2 %shard_map.69 = s32[4096,128]{1,0:T(8,128)} custom-call(s32[2]{0:T(128)S(1)} %pad_add_fusion.3.place_ref, s32[256]{0:T(256)} %reshape.271.counts_ref, s32[256]{0:T(256)} %reshape.273.befores_ref, s32[896,128]{1,0:T(8,128)} %collective-permute-done.8.rest_0_, s32[1408,128]{1,0:T(8,128)} %collective-permute-done.10.rest_1_, ...), custom_call_target="tpu_custom_call" | custom-call | tf_op jit(solution)/shard_map/pallas_call | solution.py:349
  155.9 8.4 %all-to-all-start.4 = ((s32[32,8,16,128]{3,2,1,0:T(8,128)}), s32[32,8,16,128]{3,2,1,0:T(8,128)}, u32[]{:S(2)}, u32[]{:S(2)}) async-start(s32[32,8,16,128]{3,2,1,0:T(8,128)} %bitcast.37), calls=%async_computation.4 | async-start | bytes 4194304 | tf_op jit(solution)/shard_map/all_to_all | solution.py:486
  167.3 2.4 collective-permute-start.15
  169.7 7.9 %collective-permute-done.9.rest_0_ = s32[896,128]{1,0:T(8,128)S(1)} collective-permute-done((s32[896,128]{1,0:T(8,128)}, s32[896,128]{1,0:T(8,128)S(1)}, u32[]{:S(2)}, u32[]{:S(2)}) %collective-permute-start.9) | collective-permute-done | bytes 458784 | tf_op jit(solution)/shard_map/ppermute | solution.py:491
  178.7 2.4 collective-permute-start.17
  181.1 21.7 %collective-permute-done.16.rest_4_ = s32[896,128]{1,0:T(8,128)S(1)} collective-permute-done((s32[896,128]{1,0:T(8,128)S(1)}, s32[896,128]{1,0:T(8,128)S(1)}, u32[]{:S(2)}, u32[]{:S(2)}) %collective-permute-start.16) | collective-permute-done | bytes 458784 | tf_op jit(solution)/shard_map/ppermute | solution.py:491
  204.4 4.6 %shard_map.68 = s32[6144,128]{1,0:T(8,128)} custom-call(s32[2]{0:T(128)S(1)} %pad_add_fusion.3.place_ref, s32[256]{0:T(256)} %reshape.271.counts_ref, s32[256]{0:T(256)} %reshape.273.befores_ref, s32[896,128]{1,0:T(8,128)} %copy-done.4, s32[1408,128]{1,0:T(8,128)} %collective-permute-done.11.rest_1_, s32[896,128]{1,0:T(8,128)} %copy-done.5, ...), custom_call_target="tpu_custom_call" | custom-call | tf_op jit(solution)/shard_map/pallas_call | solution.py:349
  209.0 8.2 %all-to-all-start.5 = ((s32[32,12,16,128]{3,2,1,0:T(8,128)}), s32[32,12,16,128]{3,2,1,0:T(8,128)}, u32[]{:S(2)}, u32[]{:S(2)}) async-start(s32[32,12,16,128]{3,2,1,0:T(8,128)} %bitcast.34), calls=%async_computation.5 | async-start | bytes 6291456 | tf_op jit(solution)/shard_map/all_to_all | solution.py:486
  223.8 8.7 %place_weights.1 = f32[1024]{0:T(1024)} custom-call(s32[256]{0:T(256)S(1)} %dynamic-slice_reduce_fusion.counts_ref, s32[1]{0:T(128)} %bitcast.6.member_ref, s32[1024]{0:T(1024)} %reshape.281.keys_ref, f32[4096]{0:T(1024)} %copy-done.11), custom_call_target="tpu_custom_call" | custom-call | tf_op jit(solution)/shard_map/place_weights/pallas_call | solution.py:140
  234.5 22.6 %all-to-all-done.5 = s32[32,12,16,128]{3,2,1,0:T(8,128)} async-done(((s32[32,12,16,128]{3,2,1,0:T(8,128)}), s32[32,12,16,128]{3,2,1,0:T(8,128)}, u32[]{:S(2)}, u32[]{:S(2)}) %all-to-all-start.5) | async-done | bytes 3145760 | tf_op jit(solution)/shard_map/all_to_all | solution.py:486
  257.1 19.7 %conditional.1 = (s32[1024,2048]{1,0:T(8,128)}) conditional(s32[]{:T(128)} %convert_element_type.36, (s32[]{:T(128)}, s32[1]{0:T(128)}, s32[32]{0:T(128)S(1)}, s32[512]{0:T(512)S(1)}, s32[512]{0:T(512)S(1)}, /*index=5*/s32[512,2048]{1,0:T(8,128)}, s32[256]{0:T(256)S(1)}) %tuple.51, (s32[256,32]{0,1:T(8,128)S(1)}, s32[]{:T(128)}, ...), branch_computations={%region_27.28_spmd, %region_28.29_spmd} | conditional | flops 33 | bytes 16777488 | solution.py:585
  257.7 19.1 %unpack_relay.1 = s32[1024,2048]{1,0:T(8,128)} custom-call(s32[2]{0:T(128)S(1)} %get-tuple-element.43.place_ref, s32[256]{0:T(256)S(1)} %get-tuple-element.44.counts_ref, s32[256]{0:T(256)} %bitcast.52, s32[6144,128]{1,0:T(8,128)S(1)} %get-tuple-element.47.rest_0_, s32[4096,128]{1,0:T(8,128)} %get-tuple-element.48.rest_1_, s32[6144,128]{1,0:T(8,128)} %bitcast.4.rest_2_), custom_call_target="tpu_custom_call" | custom-call | tf_op jit(solution)/shard_map/cond/branch_1_fun/unpack_relay/pallas_call | solution.py:424
  (110 shorter events, 27.5 us)
Async XLA Ops:
  0.6 42.1 %copy-start.12 = (s32[512]{0:T(512)S(1)}, s32[512]{0:T(512)}, u32[]{:S(2)}) copy-start(s32[512]{0:T(512)} %param.6) | copy-start | bytes 6148
  0.6 42.1 %copy-start.13 = (s32[512,1]{0,1:T(1,128)S(1)}, s32[512,1]{0,1:T(1,128)}, u32[]{:S(2)}) copy-start(s32[512,1]{0,1:T(1,128)} %param.8) | copy-start | bytes 6148
  10.9 31.3 %all-to-all-start.1 = ((s32[256,1,48]{2,1,0:T(1,128)}), s32[256,1,48]{2,1,0:T(1,128)S(1)}, u32[]{:S(2)}, u32[]{:S(2)}) async-start(s32[256,1,48]{2,1,0:T(1,128)} %bitcast.9), calls=%async_computation.1 | async-start | bytes 262144 | tf_op jit(solution)/shard_map/all_to_all | solution.py:486
  34.9 14.7 %collective-permute-start = (s32[896,128]{1,0:T(8,128)}, s32[896,128]{1,0:T(8,128)S(1)}, u32[]{:S(2)}, u32[]{:S(2)}) collective-permute-start(s32[896,128]{1,0:T(8,128)} %get-tuple-element.74), channel_id=1, source_target_pairs={{0,8},{8,16},{16,24},{24,32},{32,40},{40,48},{48,56},{56,0},{1,9},... | collective-permute-start | bytes 1376264 | tf_op jit(solution)/shard_map/ppermute | solution.py:491
  36.5 13.2 %collective-permute-start.4 = (s32[896,128]{1,0:T(8,128)}, s32[896,128]{1,0:T(8,128)S(1)}, u32[]{:S(2)}, u32[]{:S(2)}) collective-permute-start(s32[896,128]{1,0:T(8,128)} %get-tuple-element.78), channel_id=1, source_target_pairs={{0,56},{8,0},{16,8},{24,16},{32,24},{40,32},{48,40},{56,48},{1,57}... | collective-permute-start | bytes 1376264 | tf_op jit(solution)/shard_map/ppermute | solution.py:491
  39.4 22.9 %collective-permute-start.2 = (s32[1152,128]{1,0:T(8,128)}, s32[1152,128]{1,0:T(8,128)S(1)}, u32[]{:S(2)}, u32[]{:S(2)}) collective-permute-start(s32[1152,128]{1,0:T(8,128)} %get-tuple-element.76), channel_id=1, source_target_pairs={{0,8},{8,16},{16,24},{24,32},{32,40},{40,48},{48,56},{56,0},{1,9},... | collective-permute-start | bytes 1769480 | tf_op jit(solution)/shard_map/ppermute | solution.py:491
  39.4 51.1 %collective-permute-start.1 = (s32[1408,128]{1,0:T(8,128)}, s32[1408,128]{1,0:T(8,128)S(1)}, u32[]{:S(2)}, u32[]{:S(2)}) collective-permute-start(s32[1408,128]{1,0:T(8,128)} %get-tuple-element.75), channel_id=1, source_target_pairs={{0,8},{8,16},{16,24},{24,32},{32,40},{40,48},{48,56},{56,0},{1,9},... | collective-permute-start | bytes 2162696 | tf_op jit(solution)/shard_map/ppermute | solution.py:491
  39.4 51.1 %collective-permute-start.5 = (s32[1408,128]{1,0:T(8,128)}, s32[1408,128]{1,0:T(8,128)S(1)}, u32[]{:S(2)}, u32[]{:S(2)}) collective-permute-start(s32[1408,128]{1,0:T(8,128)} %get-tuple-element.79), channel_id=1, source_target_pairs={{0,56},{8,0},{16,8},{24,16},{32,24},{40,32},{48,40},{56,48},{1,57}... | collective-permute-start | bytes 2162696 | tf_op jit(solution)/shard_map/ppermute | solution.py:491
  49.6 40.8 %collective-permute-start.3 = (s32[1152,128]{1,0:T(8,128)}, s32[1152,128]{1,0:T(8,128)}, u32[]{:S(2)}, u32[]{:S(2)}) collective-permute-start(s32[1152,128]{1,0:T(8,128)} %get-tuple-element.77), channel_id=1, source_target_pairs={{0,8},{8,16},{16,24},{24,32},{32,40},{40,48},{48,56},{56,0},{1,9},... | collective-permute-start | bytes 1769480 | tf_op jit(solution)/shard_map/ppermute | solution.py:491
  51.2 39.3 %collective-permute-start.6 = (s32[1152,128]{1,0:T(8,128)}, s32[1152,128]{1,0:T(8,128)S(1)}, u32[]{:S(2)}, u32[]{:S(2)}) collective-permute-start(s32[1152,128]{1,0:T(8,128)} %get-tuple-element.80), channel_id=1, source_target_pairs={{0,56},{8,0},{16,8},{24,16},{32,24},{40,32},{48,40},{56,48},{1,57}... | collective-permute-start | bytes 1769480 | tf_op jit(solution)/shard_map/ppermute | solution.py:491
  62.3 28.2 %copy-start.2 = (s32[1152,128]{1,0:T(8,128)}, s32[1152,128]{1,0:T(8,128)S(1)}, u32[]{:S(2)}) copy-start(s32[1152,128]{1,0:T(8,128)S(1)} %collective-permute-done.2.rest_3_) | copy-start | bytes 1769476
  62.3 28.2 %collective-permute-start.7 = (s32[1152,128]{1,0:T(8,128)}, s32[1152,128]{1,0:T(8,128)}, u32[]{:S(2)}, u32[]{:S(2)}) collective-permute-start(s32[1152,128]{1,0:T(8,128)} %get-tuple-element.81), channel_id=1, source_target_pairs={{0,56},{8,0},{16,8},{24,16},{32,24},{40,32},{48,40},{56,48},{1,57}... | collective-permute-start | bytes 1769480 | tf_op jit(solution)/shard_map/ppermute | solution.py:491
  67.1 32.6 %all-to-all-start.2 = ((s32[256,1,20]{2,1,0:T(1,128)}), s32[256,1,20]{2,1,0:T(1,128)S(1)}, u32[]{:S(2)}, u32[]{:S(2)}) async-start(s32[256,1,20]{2,1,0:T(1,128)} %bitcast.14), calls=%async_computation.2 | async-start | bytes 262144 | tf_op jit(solution)/shard_map/all_to_all | solution.py:486
  90.5 1.1 copy-start
  90.5 1.3 copy-start.1
  99.7 56.1 %all-to-all-start.3 = ((s32[32,12,16,128]{3,2,1,0:T(8,128)}), s32[32,12,16,128]{3,2,1,0:T(8,128)S(1)}, u32[]{:S(2)}, u32[]{:S(2)}) async-start(s32[32,12,16,128]{3,2,1,0:T(8,128)} %bitcast.33), calls=%async_computation.3 | async-start | bytes 6291456 | tf_op jit(solution)/shard_map/all_to_all | solution.py:486
  106.7 14.5 %collective-permute-start.8 = (s32[896,128]{1,0:T(8,128)}, s32[896,128]{1,0:T(8,128)}, u32[]{:S(2)}, u32[]{:S(2)}) collective-permute-start(s32[896,128]{1,0:T(8,128)} %copy-done.9), channel_id=1, source_target_pairs={{0,8},{8,16},{16,24},{24,32},{32,40},{40,48},{48,56},{56,0},{1,9},... | collective-permute-start | bytes 1376264 | tf_op jit(solution)/shard_map/ppermute | solution.py:491
  108.0 43.6 %collective-permute-start.10 = (s32[1408,128]{1,0:T(8,128)}, s32[1408,128]{1,0:T(8,128)}, u32[]{:S(2)}, u32[]{:S(2)}) collective-permute-start(s32[1408,128]{1,0:T(8,128)} %copy-done), channel_id=1, source_target_pairs={{0,8},{8,16},{16,24},{24,32},{32,40},{40,48},{48,56},{56,0},{1,9},... | collective-permute-start | bytes 2162696 | tf_op jit(solution)/shard_map/ppermute | solution.py:491
  108.9 42.7 %collective-permute-start.14 = (s32[1408,128]{1,0:T(8,128)}, s32[1408,128]{1,0:T(8,128)}, u32[]{:S(2)}, u32[]{:S(2)}) collective-permute-start(s32[1408,128]{1,0:T(8,128)} %copy-done.1), channel_id=1, source_target_pairs={{0,56},{8,0},{16,8},{24,16},{32,24},{40,32},{48,40},{56,48},{1,57}... | collective-permute-start | bytes 2162696 | tf_op jit(solution)/shard_map/ppermute | solution.py:491
  110.7 40.9 %collective-permute-start.18 = (s32[1152,128]{1,0:T(8,128)}, s32[1152,128]{1,0:T(8,128)}, u32[]{:S(2)}, u32[]{:S(2)}) collective-permute-start(s32[1152,128]{1,0:T(8,128)} %copy-done.2), channel_id=1, source_target_pairs={{0,8},{8,16},{16,24},{24,32},{32,40},{40,48},{48,56},{56,0},{1,9},... | collective-permute-start | bytes 1769480 | tf_op jit(solution)/shard_map/ppermute | solution.py:491
  113.1 38.5 %collective-permute-start.19 = (s32[1152,128]{1,0:T(8,128)}, s32[1152,128]{1,0:T(8,128)}, u32[]{:S(2)}, u32[]{:S(2)}) collective-permute-start(s32[1152,128]{1,0:T(8,128)} %copy-done.3), channel_id=1, source_target_pairs={{0,56},{8,0},{16,8},{24,16},{32,24},{40,32},{48,40},{56,48},{1,57}... | collective-permute-start | bytes 1769480 | tf_op jit(solution)/shard_map/ppermute | solution.py:491
  121.2 30.4 %collective-permute-start.12 = (s32[896,128]{1,0:T(8,128)}, s32[896,128]{1,0:T(8,128)}, u32[]{:S(2)}, u32[]{:S(2)}) collective-permute-start(s32[896,128]{1,0:T(8,128)} %copy-done.8), channel_id=1, source_target_pairs={{0,56},{8,0},{16,8},{24,16},{32,24},{40,32},{48,40},{56,48},{1,57}... | collective-permute-start | bytes 1376264 | tf_op jit(solution)/shard_map/ppermute | solution.py:491
  155.9 53.2 %all-to-all-start.4 = ((s32[32,8,16,128]{3,2,1,0:T(8,128)}), s32[32,8,16,128]{3,2,1,0:T(8,128)}, u32[]{:S(2)}, u32[]{:S(2)}) async-start(s32[32,8,16,128]{3,2,1,0:T(8,128)} %bitcast.37), calls=%async_computation.4 | async-start | bytes 4194304 | tf_op jit(solution)/shard_map/all_to_all | solution.py:486
  164.3 13.4 %collective-permute-start.9 = (s32[896,128]{1,0:T(8,128)}, s32[896,128]{1,0:T(8,128)S(1)}, u32[]{:S(2)}, u32[]{:S(2)}) collective-permute-start(s32[896,128]{1,0:T(8,128)} %collective-permute-done.8.rest_0_), channel_id=1, source_target_pairs={{0,8},{8,16},{16,24},{24,32},{32,40},{40,48},{48,56},{56,0},{1,9},... | collective-permute-start | bytes 1376264 | tf_op jit(solution)/shard_map/ppermute | solution.py:491
  165.8 12.9 %collective-permute-start.13 = (s32[896,128]{1,0:T(8,128)}, s32[896,128]{1,0:T(8,128)S(1)}, u32[]{:S(2)}, u32[]{:S(2)}) collective-permute-start(s32[896,128]{1,0:T(8,128)} %collective-permute-done.12.rest_3_), channel_id=1, source_target_pairs={{0,56},{8,0},{16,8},{24,16},{32,24},{40,32},{48,40},{56,48},{1,57}... | collective-permute-start | bytes 1376264 | tf_op jit(solution)/shard_map/ppermute | solution.py:491
  167.1 36.6 %collective-permute-start.11 = (s32[1408,128]{1,0:T(8,128)}, s32[1408,128]{1,0:T(8,128)}, u32[]{:S(2)}, u32[]{:S(2)}) collective-permute-start(s32[1408,128]{1,0:T(8,128)} %collective-permute-done.10.rest_1_), channel_id=1, source_target_pairs={{0,8},{8,16},{16,24},{24,32},{32,40},{40,48},{48,56},{56,0},{1,9},... | collective-permute-start | bytes 2162696 | tf_op jit(solution)/shard_map/ppermute | solution.py:491
  167.3 37.1 %collective-permute-start.15 = (s32[1408,128]{1,0:T(8,128)}, s32[1408,128]{1,0:T(8,128)}, u32[]{:S(2)}, u32[]{:S(2)}) collective-permute-start(s32[1408,128]{1,0:T(8,128)} %collective-permute-done.14.rest_4_), channel_id=1, source_target_pairs={{0,56},{8,0},{16,8},{24,16},{32,24},{40,32},{48,40},{56,48},{1,57}... | collective-permute-start | bytes 2162696 | tf_op jit(solution)/shard_map/ppermute | solution.py:491
  178.5 24.4 %collective-permute-start.16 = (s32[896,128]{1,0:T(8,128)S(1)}, s32[896,128]{1,0:T(8,128)S(1)}, u32[]{:S(2)}, u32[]{:S(2)}) collective-permute-start(s32[896,128]{1,0:T(8,128)S(1)} %collective-permute-done.9.rest_0_), channel_id=1, source_target_pairs={{0,8},{8,16},{16,24},{24,32},{32,40},{40,48},{48,56},{56,0},{1,9},... | collective-permute-start | bytes 1376264 | tf_op jit(solution)/shard_map/ppermute | solution.py:491
  178.7 24.2 %copy-start.5 = (s32[896,128]{1,0:T(8,128)}, s32[896,128]{1,0:T(8,128)S(1)}, u32[]{:S(2)}) copy-start(s32[896,128]{1,0:T(8,128)S(1)} %collective-permute-done.13.rest_2_) | copy-start | bytes 1376260
  178.7 24.2 %collective-permute-start.17 = (s32[896,128]{1,0:T(8,128)S(1)}, s32[896,128]{1,0:T(8,128)S(1)}, u32[]{:S(2)}, u32[]{:S(2)}) collective-permute-start(s32[896,128]{1,0:T(8,128)S(1)} %collective-permute-done.13.rest_2_), channel_id=1, source_target_pairs={{0,56},{8,0},{16,8},{24,16},{32,24},{40,32},{48,40},{56,48},{1,57}... | collective-permute-start | bytes 1376264 | tf_op jit(solution)/shard_map/ppermute | solution.py:491
  209.0 48.1 %all-to-all-start.5 = ((s32[32,12,16,128]{3,2,1,0:T(8,128)}), s32[32,12,16,128]{3,2,1,0:T(8,128)}, u32[]{:S(2)}, u32[]{:S(2)}) async-start(s32[32,12,16,128]{3,2,1,0:T(8,128)} %bitcast.34), calls=%async_computation.5 | async-start | bytes 6291456 | tf_op jit(solution)/shard_map/all_to_all | solution.py:486
  222.4 34.7 %copy-start.10 = (s32[4096]{0:T(1024)}, s32[4096]{0:T(1024)S(1)}, u32[]{:S(2)}) copy-start(s32[4096]{0:T(1024)S(1)} %reshape.276) | copy-start | bytes 49156
  (7 other events, 5.3 us)

commit v3 on v2

v3 whole, which is shorter than its diff:
```python
import jax
import jax.numpy as jnp
from jax import lax
from jax.experimental import pallas as pl
from jax.experimental.pallas import tpu as pltpu
from jax.sharding import Mesh
from jax.sharding import PartitionSpec as P


BINS = 4096
KEY_SHIFT = 18
DP = ("dp_0", "dp_1")
GROUP = ("group_0", "group_1")
DP_GROUP = ("dp_0", "dp_1", "group_0", "group_1")
LANES = 128
STEP = 64

SMEM = pltpu.MemorySpace.SMEM


def smem_spec():
    return pl.BlockSpec(memory_space=SMEM)


def any_spec():
    return pl.BlockSpec(memory_space=pltpu.MemorySpace.HBM)


def pack_rows(keys, dest, info, tokens, n_dev, n_member, slots):
    examples, width = tokens.shape
    tiles = width // LANES
    steps = examples // STEP
    n_owner = n_dev // n_member

    def kernel(keys_ref, dest_ref, info_ref, tok_ref, rows_ref, meta_ref, buf, seen, sent, sem):
        g = pl.program_id(0)

        @pl.when(g == 0)
        def _():
            sent[0] = 0
            for o in range(n_owner):
                seen[o] = 0

        @pl.when(g < steps)
        def _():
            for r in range(STEP // 8):
                for k in range(tiles):
                    at = (g * STEP + r * 8) * tiles + k
                    buf[pl.ds(at, 8, stride=tiles), :] = tok_ref[r * 8 : r * 8 + 8, k * LANES : (k + 1) * LANES]

        @pl.when(g > 0)
        def _():
            lowest = info_ref[0] << KEY_SHIFT

            def row(i, total):
                key = keys_ref[i]
                kept = key >= lowest

                @pl.when(kept)
                def _():
                    o = dest_ref[i]
                    local = seen[o]
                    seen[o] = local + 1
                    member = (info_ref[1 + o] + local) & (n_member - 1)
                    to = (o * n_member + member) * slots + local // n_member
                    meta_ref[to] = key
                    pltpu.make_async_copy(
                        buf.at[pl.ds(pl.multiple_of(i * tiles, tiles), tiles)],
                        rows_ref.at[pl.ds(pl.multiple_of(to * tiles, tiles), tiles)],
                        sem,
                    ).start()

                return total + kept.astype(jnp.int32)

            start = (g - 1) * STEP
            sent[0] = lax.fori_loop(start, start + STEP, row, sent[0])

        @pl.when(g == steps)
        def _():
            def drain(i, carry):
                pltpu.make_async_copy(buf.at[pl.ds(0, tiles)], rows_ref.at[pl.ds(0, tiles)], sem).wait()
                return carry

            lax.fori_loop(0, sent[0], drain, 0)

    return pl.pallas_call(
        kernel,
        grid=(steps + 1,),
        in_specs=[
            smem_spec(),
            smem_spec(),
            smem_spec(),
            pl.BlockSpec((STEP, width), lambda g: (jnp.minimum(g, steps - 1), 0)),
        ],
        out_specs=[any_spec(), smem_spec()],
        out_shape=[
            jax.ShapeDtypeStruct((n_dev * slots * tiles, LANES), tokens.dtype),
            jax.ShapeDtypeStruct((n_dev * slots,), keys.dtype),
        ],
        scratch_shapes=[
            pltpu.VMEM((examples * tiles, LANES), tokens.dtype),
            pltpu.SMEM((n_owner,), jnp.int32),
            pltpu.SMEM((1,), jnp.int32),
            pltpu.SemaphoreType.DMA,
        ],
        name="pack_rows",
    )(keys, dest, info, tokens)


def incoming(counts_ref, member, n_dev, n_member, visit, carry):
    def source(s, state):
        before, carry = state
        count = counts_ref[s]
        first = (member - before) & (n_member - 1)
        rows = (count - first + n_member - 1) >> 3
        carry = visit(s, (before + first) >> 3, rows, carry)
        return before + count, carry

    return lax.fori_loop(0, n_dev, source, (0, carry))


def place_bins(counts, member, got_keys, n_dev, n_member, slots, capacity):
    def kernel(counts_ref, member_ref, keys_ref, out_ref):
        def clear(i, carry):
            for j in range(8):
                out_ref[i * 8 + j] = -1
            return carry

        lax.fori_loop(0, capacity // 8, clear, 0)

        def visit(s, slot, rows, carry):
            at = s * (slots * n_member) + ((member_ref[0] - carry) & (n_member - 1))

            def one(q, c):
                out_ref[slot + q] = keys_ref[at + q * n_member] >> KEY_SHIFT
                return c

            lax.fori_loop(0, rows, one, 0)
            return carry + counts_ref[s]

        incoming(counts_ref, member_ref[0], n_dev, n_member, visit, 0)

    return pl.pallas_call(
        kernel,
        in_specs=[smem_spec()] * 3,
        out_specs=smem_spec(),
        out_shape=jax.ShapeDtypeStruct((capacity,), jnp.int32),
        name="place_bins",
    )(counts, member, got_keys)


def unpack_rows(counts, member, got, n_dev, n_member, slots, capacity, width):
    tiles = width // LANES
    steps = capacity // STEP

    def kernel(counts_ref, member_ref, got_ref, out_ref, buf, pending, filled, sems):
        g = pl.program_id(0)

        @pl.when(g == 0)
        def _():
            for b in range(steps):
                pending[b] = 0

            def visit(s, slot, rows, carry):
                b = slot // STEP

                @pl.when(rows > 0)
                def _():
                    pending[b] = pending[b] + rows

                for n in range(1, slots + 1):

                    @pl.when(rows == n)
                    def _(n=n):
                        pltpu.make_async_copy(
                            got_ref.at[pl.ds(pl.multiple_of(s * (slots * tiles), tiles), n * tiles)],
                            buf.at[pl.ds(pl.multiple_of(slot * tiles, tiles), n * tiles)],
                            sems.at[b],
                        ).start()

                return carry

            total, _ = incoming(counts_ref, member_ref[0], n_dev, n_member, visit, 0)
            filled[0] = (total - member_ref[0] + n_member - 1) >> 3

        def drain(i, carry):
            pltpu.make_async_copy(got_ref.at[pl.ds(0, tiles)], buf.at[pl.ds(0, tiles)], sems.at[g]).wait()
            return carry

        lax.fori_loop(0, pending[g], drain, 0)
        index = g * STEP + lax.broadcasted_iota(jnp.int32, (8, LANES), 0)
        for r in range(STEP // 8):
            real = index + r * 8 < filled[0]
            for k in range(tiles):
                at = (g * STEP + r * 8) * tiles + k
                rows = buf[pl.ds(at, 8, stride=tiles), :]
                out_ref[r * 8 : r * 8 + 8, k * LANES : (k + 1) * LANES] = jnp.where(real, rows, 0)

    return pl.pallas_call(
        kernel,
        grid=(steps,),
        in_specs=[smem_spec(), smem_spec(), any_spec()],
        out_specs=pl.BlockSpec((STEP, width), lambda g: (g, 0)),
        out_shape=jax.ShapeDtypeStruct((capacity, width), got.dtype),
        scratch_shapes=[
            pltpu.VMEM((capacity * tiles, LANES), got.dtype),
            pltpu.SMEM((steps,), jnp.int32),
            pltpu.SMEM((1,), jnp.int32),
            pltpu.SemaphoreType.DMA((steps,)),
        ],
        name="unpack_rows",
    )(counts, member, got)


NEAR = 112
EDGES = (0, 56, 144, 216)
OWN = 128
PLACES = 2 * (NEAR + EDGES[-1]) + OWN


def segments(hop):
    return [(EDGES[j], EDGES[j + 1] - EDGES[j]) for j in range(min(3, 5 - hop))]


def pack_relay(source, tokens, offset, sizes):
    examples, width = tokens.shape
    tiles = width // LANES
    tiled = tokens.reshape(examples // 8, 8, tiles, LANES).transpose(0, 2, 1, 3)[..., None, :]
    parts = 4

    def kernel(source_ref, tok_ref, *rest):
        outs, (buf, sem_in, sem_out) = rest[: len(sizes)], rest[len(sizes) :]
        each = examples // 8 // parts
        loads = [
            pltpu.make_async_copy(tok_ref.at[pl.ds(i * each, each)], buf.at[pl.ds(i * each, each)], sem_in)
            for i in range(parts)
        ]
        for load in loads:
            load.start()
        for load in loads:
            load.wait()
        start = offset
        for out, size in zip(outs, sizes):

            def some(i, carry, out=out, start=start):
                for j in range(8):
                    row = source_ref[start + i * 8 + j]
                    pltpu.make_async_copy(slot_of(buf, row), out.at[i * 8 + j], sem_out).start()
                return carry

            lax.fori_loop(0, size // 8, some, 0)
            start += size
        for out in outs:
            pltpu.make_async_copy(out, out, sem_out).wait()

    packed = pl.pallas_call(
        kernel,
        in_specs=[smem_spec(), any_spec()],
        out_specs=[any_spec()] * len(sizes),
        out_shape=[jax.ShapeDtypeStruct((n, tiles, 1, LANES), tokens.dtype) for n in sizes],
        scratch_shapes=[
            pltpu.VMEM((examples // 8, tiles, 8, 1, LANES), tokens.dtype),
            pltpu.SemaphoreType.DMA,
            pltpu.SemaphoreType.DMA,
        ],
    )(source, tiled)
    return [rows.reshape(-1, LANES) for rows in packed]


ROUNDS = ((0, 1), (2,), (3, 4))


def lanes_of(hop):
    if hop == 0:
        return [((0,), 4)]
    if hop == 4:
        return [((0, 1), 4)]
    return [((0,), 4), ((1,), 4)]


def slot_map():
    found = {}
    for n, hops in enumerate(ROUNDS):
        skip = 0
        for hop in hops:
            for sides, slots in lanes_of(hop):
                for side in sides:
                    found[hop if side == 0 else (8 - hop) % 8] = (n, skip)
                skip += slots
        for d, (m, at) in list(found.items()):
            if m == n and not isinstance(at, tuple):
                found[d] = (m, (at, skip))
    return {d: (n, rows, at) for d, (n, (at, rows)) in found.items()}


def spread(n, place, counts, befores, pieces, n_member, tiles, onto=None):
    slots = slot_map()
    width = next(rows for m, rows, _ in slots.values() if m == n)
    total = 4 * n_member * width * tiles
    origins, held = {}, 0
    for hop, side, start, rows, _ in pieces:
        if (hop, side) not in origins:
            rows_in = (OWN, NEAR, EDGES[3], EDGES[2], EDGES[1])[hop]
            origins[hop, side] = (held, rows_in)
            held += rows_in + 32
    arrays = [array for *_, array in pieces]
    laid = sum(4 * (16 if hop == 4 else 32) for hop, _ in origins)
    base_of = [] if onto is None else [onto]

    def kernel(place_ref, counts_ref, befores_ref, *rest):
        rest = rest[len(base_of) :]
        ins, (out, buf, sem_in, sem_out) = rest[: len(pieces)], rest[len(pieces) :]
        loads = []
        for (hop, side, start, rows, _), ref in zip(pieces, ins):
            at = (origins[hop, side][0] + start) * tiles
            loads.append(pltpu.make_async_copy(ref, buf.at[pl.ds(at, rows * tiles)], sem_in))
        for load in loads:
            load.start()
        z = place_ref[0]
        todo = []
        for (hop, side), (base, rows_in) in origins.items():
            sign = 1 - 2 * side
            origin = (z - sign * hop) & 7

            def share(y, k, origin=origin, sign=sign, side=side):
                count = counts_ref[origin * 32 + y * 8 + ((origin + sign * k) & 7)]
                return (count + 1 - side) >> 1 if k == 4 else count

            at = 0
            if hop > 1:
                for k in range(hop + 1, 5):
                    for y in range(4):
                        at += share(y, k)
            for y in range(4):
                todo.append((hop, side, y, base + jnp.minimum(at, rows_in), befores_ref[origin * 32 + y * 8 + z]))
                at += share(y, hop)
        for load in loads:
            load.wait()
        for hop, side, y, first, before in todo:
            skip = slots[hop if side == 0 else (8 - hop) % 8][2]
            for j in range(16 if hop == 4 else 32):
                local = 2 * j + side if hop == 4 else j
                member = (before + local) & (n_member - 1)
                to = (y * n_member + member) * width + skip + local // n_member
                pltpu.make_async_copy(
                    buf.at[pl.ds(pl.multiple_of((first + j) * tiles, tiles), tiles)],
                    out.at[pl.ds(pl.multiple_of(to * tiles, tiles), tiles)],
                    sem_out,
                ).start()
        whole = out.at[pl.ds(0, laid * tiles)]
        pltpu.make_async_copy(whole, whole, sem_out).wait()

    return pl.pallas_call(
        kernel,
        in_specs=[smem_spec()] * 3 + [any_spec()] * (len(base_of) + len(pieces)),
        out_specs=any_spec(),
        out_shape=jax.ShapeDtypeStruct((total, LANES), arrays[0].dtype),
        input_output_aliases={3: 0} if base_of else {},
        scratch_shapes=[
            pltpu.VMEM((held * tiles, LANES), arrays[0].dtype),
            pltpu.SemaphoreType.DMA,
            pltpu.SemaphoreType.DMA,
        ],
    )(place, counts, befores, *base_of, *arrays)


def copy_senders(d, slots_of, place_ref, counts_ref, befores_ref, n_member, start):
    _, rows_each, skip = slots_of[d]
    member = place_ref[1]
    origin = (place_ref[0] - d) & 7

    def sender(i, total):
        s = ((i >> 3) * 8 + origin) * n_member + (i & 7)
        before = befores_ref[s]
        first = (member - before) & (n_member - 1)
        rows = (counts_ref[s] - first + n_member - 1) >> 3
        slot = (before + first) >> 3
        for q in range(4):

            @pl.when(q < rows)
            def _(q=q):
                start(i * rows_each + skip + q, slot + q)

        return total + rows

    return lax.fori_loop(0, 4 * n_member, sender, 0)


def slot_of(ref, slot):
    return ref.at[slot >> 3, :, slot & 7]


def unpack_early(place, counts, befores, got, n_member, capacity, tiles):
    slots_of = slot_map()
    groups = capacity // 8

    def kernel(place_ref, counts_ref, befores_ref, *rest):
        ins, (out_ref, buf, zero, sem_in, sem_out) = rest[: len(got)], rest[len(got) :]
        zero[...] = jnp.zeros(zero.shape, zero.dtype)
        moved = 0
        for d in range(8):
            n = slots_of[d][0]
            if n < len(got):

                def start(row, slot, n=n):
                    pltpu.make_async_copy(ins[n].at[row], slot_of(buf, slot), sem_in).start()

                moved += copy_senders(d, slots_of, place_ref, counts_ref, befores_ref, n_member, start)

        def drain(i, carry):
            pltpu.make_async_copy(ins[0].at[0], buf.at[0, :, 0], sem_in).wait()
            return carry

        lax.fori_loop(0, moved, drain, 0)
        end = 32 * n_member - 1
        filled = (befores_ref[end] + counts_ref[end] - place_ref[1] + n_member - 1) >> 3
        whole, extra = filled >> 3, filled & 7

        def group(g, carry):
            @pl.when(g < whole)
            def _():
                pltpu.make_async_copy(buf.at[g], out_ref.at[g], sem_out).start()

            @pl.when((g > whole) | ((g == whole) & (extra == 0)))
            def _():
                pltpu.make_async_copy(zero, out_ref.at[g], sem_out).start()

            @pl.when((g == whole) & (extra > 0))
            def _():
                for k in range(8):

                    @pl.when(k < extra)
                    def _(k=k):
                        pltpu.make_async_copy(buf.at[g, :, k], out_ref.at[g, :, k], sem_out).start()

                    @pl.when(k >= extra)
                    def _(k=k):
                        pltpu.make_async_copy(zero.at[:, k], out_ref.at[g, :, k], sem_out).start()

            return carry

        lax.fori_loop(0, groups, group, 0)
        pltpu.make_async_copy(buf, out_ref, sem_out).wait()

    return pl.pallas_call(
        kernel,
        in_specs=[smem_spec()] * 3 + [any_spec()] * len(got),
        out_specs=any_spec(),
        out_shape=jax.ShapeDtypeStruct((groups, tiles, 8, 1, LANES), got[0].dtype),
        scratch_shapes=[
            pltpu.VMEM((groups, tiles, 8, 1, LANES), got[0].dtype),
            pltpu.VMEM((tiles, 8, 1, LANES), got[0].dtype),
            pltpu.SemaphoreType.DMA,
            pltpu.SemaphoreType.DMA,
        ],
        name="unpack_early",
    )(place, counts, befores, *got)


def unpack_last(place, counts, befores, early, last, n_member):
    slots_of = slot_map()
    late = [d for d in range(8) if slots_of[d][0] == len(ROUNDS) - 1]
    last = pltpu.with_memory_space_constraint(last, pltpu.MemorySpace.VMEM)

    def kernel(place_ref, counts_ref, befores_ref, early_ref, buf, out_ref, sem_out):

        def start(row, slot):
            pltpu.make_async_copy(buf.at[row], slot_of(out_ref, slot), sem_out).start()

        moved = 0
        for d in late:
            moved += copy_senders(d, slots_of, place_ref, counts_ref, befores_ref, n_member, start)

        def drain(i, carry):
            pltpu.make_async_copy(buf.at[0], out_ref.at[0, :, 0], sem_out).wait()
            return carry

        lax.fori_loop(0, moved, drain, 0)

    return pl.pallas_call(
        kernel,
        in_specs=[smem_spec()] * 3 + [any_spec(), pl.BlockSpec(memory_space=pltpu.MemorySpace.VMEM)],
        out_specs=any_spec(),
        out_shape=jax.ShapeDtypeStruct(early.shape, early.dtype),
        input_output_aliases={3: 0},
        scratch_shapes=[pltpu.SemaphoreType.DMA],
        name="unpack_last",
    )(place, counts, befores, early, last)


def relay_source(counts, local_rank, onehot, z):
    owner = jnp.arange(32, dtype=jnp.int32)
    y, d = owner // 8, (owner - z) % 8
    dist = jnp.minimum(d, 8 - d)
    earlier = (((4 - dist) * 4 + y)[None, :] < ((4 - dist) * 4 + y)[:, None]) & ((dist > 1)[None, :] == (dist > 1)[:, None])

    def start(members, sizes):
        return jnp.sum(jnp.where(earlier & members[None, :], sizes[None, :], 0), axis=1)

    ahead, back = (d >= 1) & (d <= 4), d >= 4
    start_ahead = start(ahead, jnp.where(d == 4, (counts + 1) >> 1, counts))
    start_back = start(back, jnp.where(d == 4, counts >> 1, counts))
    far_ahead, far_back, mine = 2 * NEAR, 2 * NEAR + EDGES[-1], 2 * NEAR + 2 * EDGES[-1]
    first = jnp.where(d == 0, mine, jnp.where(ahead, jnp.where(d == 1, 0, far_ahead), jnp.where(d == 7, NEAR, far_back)))
    base = first + jnp.where(d == 0, start(d == 0, counts), jnp.where(ahead, start_ahead, start_back))
    other = far_back + start_back
    limit = first + jnp.where(d == 0, OWN, jnp.where(dist == 1, NEAR, EDGES[-1]))

    def pick(values):
        return jnp.sum(onehot * values[None, :], axis=1)

    four = pick((d == 4).astype(jnp.int32)) == 1
    odd = four & ((local_rank & 1) == 1)
    position = jnp.where(odd, pick(other), pick(base)) + jnp.where(four, local_rank >> 1, local_rank)
    bound = jnp.where(odd, mine, pick(limit))
    position = jnp.where((jnp.sum(onehot, axis=1) == 1) & (position < bound), position, -1)
    example = jnp.arange(onehot.shape[0], dtype=jnp.int32)
    places = jnp.arange(PLACES, dtype=jnp.int32)
    return jnp.sum(jnp.where(position[None, :] == places[:, None], example[None, :], 0), axis=1)


def by_owner(values, position, size):
    places = jnp.arange(size, dtype=jnp.int32)
    return jnp.sum(jnp.where(position[None, :] == places[:, None], values[None, :], 0), axis=1)


def relay_fits(table):
    n_dev = table.shape[0]
    z = (jnp.arange(n_dev, dtype=jnp.int32)[:, None] // 8) % 8
    d = (jnp.arange(32, dtype=jnp.int32)[None, :] - z) % 8
    plus = jnp.where(d == 4, (table + 1) >> 1, table)
    minus = jnp.where(d == 4, table >> 1, table)
    over = jnp.zeros((), jnp.int32)
    for least, most, cap in ((1, 1, NEAR), (2, 4, EDGES[3]), (3, 4, EDGES[2]), (4, 4, EDGES[1])):
        ahead = jnp.sum(jnp.where((d >= least) & (d <= most), plus, 0), axis=1)
        back = jnp.sum(jnp.where((d <= 8 - least) & (d >= 8 - most), minus, 0), axis=1)
        over = jnp.maximum(over, jnp.max(jnp.maximum(ahead, back)) - cap)
    return over <= 0


def exchange(value, axes=DP_GROUP):
    return lax.all_to_all(value, axes, split_axis=0, concat_axis=0, tiled=True)


def hop_on(value, step, axis="dp_1"):
    count = lax.axis_size(axis)
    return lax.ppermute(value, axis, [(i, (i + step) % count) for i in range(count)])


DOUBLING = (
    ("group_1", 1), ("group_0", 1), ("group_0", 2), ("dp_0", 1), ("dp_0", 2), ("dp_1", 1), ("dp_1", 2), ("dp_1", 4),
)


def program(keys, cut, owner, tokens):
    examples = keys.shape[0]
    width = tokens.shape[1]
    tiles = width // LANES
    n_owner = lax.axis_size(DP)
    n_member = lax.axis_size(GROUP)
    n_dev = n_owner * n_member
    slots = 2 * examples // n_dev
    capacity = 2 * examples
    most = slots * n_member
    me = lax.axis_index(DP_GROUP)
    member = lax.axis_index(GROUP)
    y, z = lax.axis_index("dp_0"), lax.axis_index("dp_1")
    bins_of = keys >> KEY_SHIFT
    dest = owner[:, 0]
    kept = bins_of >= cut[0]
    owners = jnp.arange(n_owner, dtype=jnp.int32)
    onehot = ((dest[:, None] == owners[None, :]) & kept[:, None]).astype(jnp.int32)
    counts = jnp.sum(onehot, axis=0)
    index = jnp.arange(examples, dtype=jnp.int32)
    lower = (index[None, :] < index[:, None]).astype(jnp.bfloat16)
    running = jnp.dot(lower, onehot.astype(jnp.bfloat16), preferred_element_type=jnp.float32).astype(jnp.int32)
    local_rank = jnp.sum(running * onehot, axis=1)
    source = relay_source(counts, local_rank, onehot, z)
    near = pack_relay(source, tokens, 0, [NEAR] * 2)
    *far, own = pack_relay(source, tokens, 2 * NEAR, [n for _, n in segments(1)] * 2 + [OWN])
    plus, minus = far[:3], far[3:]

    hist = jnp.zeros((BINS,), jnp.int32).at[bins_of].add(1)
    for axis, step in DOUBLING:
        hist = hist + hop_on(hist, step, axis)
    own_keys = by_owner(keys, jnp.where(kept, dest * most + local_rank, -1), n_owner * most).reshape(n_owner, 1, most)
    own_keys = jnp.broadcast_to(own_keys, (n_owner, n_member, most)).reshape(n_dev, most)
    first = jnp.concatenate([jnp.broadcast_to(counts[None, :], (n_dev, n_owner)), own_keys], axis=1)
    first, _ = lax.optimization_barrier((first, source))
    first = exchange(first)
    table = first[:, :n_owner]
    got_keys = first[:, n_owner:].reshape(-1)
    device = jnp.arange(n_dev, dtype=jnp.int32)
    below = (device[None, :] < device[:, None]).astype(jnp.bfloat16)
    befores = jnp.dot(below, table.astype(jnp.bfloat16), preferred_element_type=jnp.float32).astype(jnp.int32)
    before = lax.dynamic_slice_in_dim(befores, me, 1, axis=0)[0]

    def column(values):
        return lax.dynamic_slice_in_dim(values, me // n_member, 1, axis=1)[:, 0]

    def line(values):
        return lax.dynamic_slice(values.reshape(4, 8, n_member, n_owner), (y, 0, member, 0), (1, 8, 1, n_owner)).reshape(-1)

    mine, mine_before = column(table), column(befores)
    line_counts, line_befores = line(table), line(befores)
    fits = relay_fits(table)
    place = jnp.stack([z, member]).astype(jnp.int32)

    slot_bins = place_bins(mine, member[None], got_keys, n_dev, n_member, slots, capacity)

    arrived = {0: [(0, 0, 0, OWN, own)]}
    near = [hop_on(near[0], 1), hop_on(near[1], -1)]
    arrived[1] = [(1, i, 0, NEAR, v) for i, v in enumerate(near)]
    for k in range(1, 5):
        spans = segments(k)
        plus = [hop_on(v, 1) for v in plus[: len(spans)]]
        minus = [hop_on(v, -1) for v in minus[: len(spans)]]
        if k > 1:
            arrived[k] = [(k, i, *span, v) for i, side in enumerate((plus, minus)) for span, v in zip(spans, side)]
    got = []
    for n, hops in enumerate(ROUNDS):
        calls = [[k] for k in hops] if hops[-1] == 4 else [hops]
        laid = None
        for ks in calls:
            laid = spread(n, place, line_counts, line_befores, [p for k in ks for p in arrived[k]], n_member, tiles, laid)
        laid = laid.reshape(n_owner, -1, tiles, LANES)
        if n > 0:
            laid, got[-1] = lax.optimization_barrier((laid, got[-1]))
        got.append(exchange(laid, ("dp_0",) + GROUP).reshape(-1, tiles, 1, LANES))

    early = unpack_early(place, mine, mine_before, got[:-1], n_member, capacity, tiles)
    packed = unpack_last(place, mine, mine_before, early, got[-1], n_member)
    packed = packed.reshape(capacity // 8, tiles, 8, LANES).transpose(0, 2, 1, 3).reshape(capacity, width)

    def direct(state):
        info = jnp.concatenate([cut, before])
        send_rows, _ = pack_rows(keys, dest, info, tokens, n_dev, n_member, slots)
        rows = exchange(send_rows.reshape(n_dev, slots, tiles, LANES)).reshape(-1, LANES)
        return jnp.ones((), jnp.bool_), unpack_rows(mine, member[None], rows, n_dev, n_member, slots, capacity, width)

    _, packed = lax.while_loop(lambda state: ~state[0], direct, (fits, packed))

    suffix = jnp.cumsum(hist.astype(jnp.float32)[::-1])[::-1]
    total = jnp.maximum(suffix[cut[0]], 1.0)
    weights = jnp.where(slot_bins >= 0, suffix[jnp.maximum(slot_bins, 0)] / total, 0.0)
    return (hist, packed, weights)


def solution(mesh):
    torus = Mesh(mesh.devices.reshape(4, 8, 4, 2), ("dp_0", "dp_1", "group_0", "group_1"))
    placed = (P(DP_GROUP), P(), P(DP_GROUP, None), P(DP_GROUP, None))
    return jax.shard_map(
        program,
        mesh=torus,
        in_specs=placed,
        out_specs=(P(), P(DP_GROUP, None), P(DP_GROUP)),
        check_vma=False,
    )
```

time: 280 us -> 311 us (1.11)
  the two profiles are of different devices: /device:TPU:1 before, /device:TPU:22 now
where the time goes in v3:
time: 311 us; the launch traced here: 310 us
  waiting for transfers between devices  157 us (50%)
  starting transfers between devices  70.2 us (23%)
  Pallas kernels  51.8 us (17%)
  other arithmetic  13.3 us (4%)
  local copies, waits for them, and re-layouts  11.4 us (4%)
  between operations  5.01 us (2%)
    ppermute x28, waiting for transfers between devices, hop_on(): lax.ppermute(value, axis, [(i, (i + step) % count) for i in range(count)])  147 us
    ppermute x28, starting transfers between devices, hop_on(): lax.ppermute(value, axis, [(i, (i + step) % count) for i in range(count)])  37.4 us
    all_to_all x4, starting transfers between devices, exchange(): return lax.all_to_all(value, axes, split_axis=0, concat_axis=0, tiled=True)  32.8 us
    pallas_call x4, Pallas kernels, spread(): pl.pallas_call(kernel, in_specs=[smem_spec()] * 3 + [any_spec()] * (len(b...  15.6 us
    pallas_call x1, Pallas kernels, place_bins(): pl.pallas_call(kernel, in_specs=[smem_spec()] * 3, out_specs=smem_spec(),...  11.3 us
    pallas_call x1, Pallas kernels, unpack_early(): pl.pallas_call(kernel, in_specs=[smem_spec()] * 3 + [any_spec()] * len(go...  10.4 us
    pallas_call x2, Pallas kernels, pack_relay(): pl.pallas_call(kernel, in_specs=[smem_spec(), any_spec()], out_specs=[any...  9.9 us
    all_to_all x4, waiting for transfers between devices, exchange(): return lax.all_to_all(value, axes, split_axis=0, concat_axis=0, tiled=True)  9.54 us
  transfers between devices with their start and end apart: 32, of which 17 were waited for; matrix products, arithmetic and copies ran while one was open for 6% of the time, Pallas kernels for 12%

profile of v3, /device:TPU:22, one launch (start us, length us, event | category | flops | bytes accessed | tf_op | source)
XLA Modules:
  0.0 309.6 jit_solution(5887833243418844104)
XLA Ops:
  6.6 4.3 %shard_map.69 = (s32[112,16,1,128]{3,2,1,0:T(1,128)}, s32[112,16,1,128]{3,2,1,0:T(1,128)}) custom-call(s32[784]{0:T(1024)} %select_reduce_fusion.1.source_ref, s32[64,16,8,1,128]{4,3,2,1,0:T(1,128)} %bitcast.50), custom_call_target="tpu_custom_call" | custom-call | tf_op jit(solution)/shard_map/pallas_call | solution.py:256
  10.9 5.9 %collective-permute-start.21 = (s32[1792,128]{1,0:T(8,128)}, s32[1792,128]{1,0:T(8,128)S(1)}, u32[]{:S(2)}, u32[]{:S(2)}) collective-permute-start(s32[1792,128]{1,0:T(8,128)} %bitcast.71), channel_id=1, source_target_pairs={{0,56},{8,0},{16,8},{24,16},{32,24},{40,32},{48,40},{56,48},{1,57}... | collective-permute-start | bytes 2752520 | tf_op jit(solution)/shard_map/ppermute | solution.py:547
  18.0 10.6 %all-to-all-start.1 = ((s32[256,1,64]{2,1,0:T(1,128)}), s32[256,1,64]{2,1,0:T(1,128)S(1)}, u32[]{:S(2)}, u32[]{:S(2)}) async-start(s32[256,1,64]{2,1,0:T(1,128)} %bitcast.6), calls=%async_computation.1 | async-start | bytes 262144 | tf_op jit(solution)/shard_map/all_to_all | solution.py:542
  29.2 5.6 %shard_map.67 = (s32[56,16,1,128]{3,2,1,0:T(1,128)}, s32[88,16,1,128]{3,2,1,0:T(1,128)}, s32[72,16,1,128]{3,2,1,0:T(1,128)}, s32[56,16,1,128]{3,2,1,0:T(1,128)},...) custom-call(s32[784]{0:T(1024)} %select_reduce_fusion.1.source_ref, ...), custom_call_target="tpu_custom_call" | custom-call | tf_op jit(solution)/shard_map/pallas_call | solution.py:256
  34.8 9.5 %all-to-all-done.1 = s32[256,1,64]{2,1,0:T(1,128)S(1)} async-done(((s32[256,1,64]{2,1,0:T(1,128)}), s32[256,1,64]{2,1,0:T(1,128)S(1)}, u32[]{:S(2)}, u32[]{:S(2)}) %all-to-all-start.1) | async-done | bytes 65568 | tf_op jit(solution)/shard_map/all_to_all | solution.py:542
  47.7 4.5 %shard_map.70 = s32[6144,128]{1,0:T(8,128)} custom-call(s32[2]{0:T(128)} %pad_add_fusion.2.place_ref, s32[256]{0:T(256)} %reshape.313.counts_ref, s32[256]{0:T(256)} %reshape.315.befores_ref, s32[2048,128]{1,0:T(8,128)} %bitcast.59, s32[1792,128]{1,0:T(8,128)} %copy-done.2, s32[1792,128]{1,0:T(8,128)} %copy-done.1), custom_call_target="tpu_custom_call" | custom-call | tf_op jit(solution)/shard_map/pallas_call | solution.py:353
  52.3 7.4 %all-to-all-start.2 = ((s32[32,12,16,128]{3,2,1,0:T(8,128)}), s32[32,12,16,128]{3,2,1,0:T(8,128)S(1)}, u32[]{:S(2)}, u32[]{:S(2)}) async-start(s32[32,12,16,128]{3,2,1,0:T(8,128)} %bitcast.54), calls=%async_computation.2 | async-start | bytes 6291456 | tf_op jit(solution)/shard_map/all_to_all | solution.py:542
  66.8 7.7 %collective-permute-done.8 = s32[896,128]{1,0:T(8,128)S(1)} collective-permute-done((s32[896,128]{1,0:T(8,128)}, s32[896,128]{1,0:T(8,128)S(1)}, u32[]{:S(2)}, u32[]{:S(2)}) %collective-permute-start.8) | collective-permute-done | bytes 458784 | tf_op jit(solution)/shard_map/ppermute | solution.py:547
  74.6 17.3 %collective-permute-done.14 = s32[896,128]{1,0:T(8,128)S(1)} collective-permute-done((s32[896,128]{1,0:T(8,128)}, s32[896,128]{1,0:T(8,128)S(1)}, u32[]{:S(2)}, u32[]{:S(2)}) %collective-permute-start.14) | collective-permute-done | bytes 458784 | tf_op jit(solution)/shard_map/ppermute | solution.py:547
  95.2 7.5 %collective-permute-done.12 = s32[1152,128]{1,0:T(8,128)S(1)} collective-permute-done((s32[1152,128]{1,0:T(8,128)}, s32[1152,128]{1,0:T(8,128)S(1)}, u32[]{:S(2)}, u32[]{:S(2)}) %collective-permute-start.12) | collective-permute-done | bytes 589856 | tf_op jit(solution)/shard_map/ppermute | solution.py:547
  104.5 3.2 %collective-permute-start.19 = (s32[1152,128]{1,0:T(8,128)S(1)}, s32[1152,128]{1,0:T(8,128)}, u32[]{:S(2)}, u32[]{:S(2)}) collective-permute-start(s32[1152,128]{1,0:T(8,128)S(1)} %collective-permute-done.18), channel_id=1, source_target_pairs={{0,56},{8,0},{16,8},{24,16},{32,24},{40,32},{48,40},{56,48},{1,57}... | collective-permute-start | bytes 1769480 | tf_op jit(solution)/shard_map/ppermute | solution.py:547
  107.7 4.9 %collective-permute-done.9.rest_0_ = s32[896,128]{1,0:T(8,128)} collective-permute-done((s32[896,128]{1,0:T(8,128)S(1)}, s32[896,128]{1,0:T(8,128)}, u32[]{:S(2)}, u32[]{:S(2)}) %collective-permute-start.9) | collective-permute-done | bytes 458784 | tf_op jit(solution)/shard_map/ppermute | solution.py:547
  112.6 28.5 %collective-permute-done.15.rest_3_ = s32[896,128]{1,0:T(8,128)} collective-permute-done((s32[896,128]{1,0:T(8,128)S(1)}, s32[896,128]{1,0:T(8,128)}, u32[]{:S(2)}, u32[]{:S(2)}) %collective-permute-start.15) | collective-permute-done | bytes 458784 | tf_op jit(solution)/shard_map/ppermute | solution.py:547
  141.1 4.2 %shard_map.68 = s32[4096,128]{1,0:T(8,128)} custom-call(s32[2]{0:T(128)} %pad_add_fusion.2.place_ref, s32[256]{0:T(256)} %reshape.313.counts_ref, s32[256]{0:T(256)} %reshape.315.befores_ref, s32[896,128]{1,0:T(8,128)} %collective-permute-done.9.rest_0_, s32[1408,128]{1,0:T(8,128)} %collective-permute-done.11.rest_1_, ...), custom_call_target="tpu_custom_call" | custom-call | tf_op jit(solution)/shard_map/pallas_call | solution.py:353
  145.4 7.4 %all-to-all-start.3 = ((s32[32,8,16,128]{3,2,1,0:T(8,128)}), s32[32,8,16,128]{3,2,1,0:T(8,128)}, u32[]{:S(2)}, u32[]{:S(2)}) async-start(s32[32,8,16,128]{3,2,1,0:T(8,128)} %bitcast.56), calls=%async_computation.3 | async-start | bytes 4194304 | tf_op jit(solution)/shard_map/all_to_all | solution.py:542
  156.2 3.2 %collective-permute-start.25 = (s32[1408,128]{1,0:T(8,128)}, s32[1408,128]{1,0:T(8,128)}, u32[]{:S(2)}, u32[]{:S(2)}) collective-permute-start(s32[1408,128]{1,0:T(8,128)} %collective-permute-done.17.rest_4_), channel_id=1, source_target_pairs={{0,56},{8,0},{16,8},{24,16},{32,24},{40,32},{48,40},{56,48},{1,57}... | collective-permute-start | bytes 2162696 | tf_op jit(solution)/shard_map/ppermute | solution.py:547
  159.5 8.4 %collective-permute-done.22.rest_0_ = s32[896,128]{1,0:T(8,128)} collective-permute-done((s32[896,128]{1,0:T(8,128)}, s32[896,128]{1,0:T(8,128)}, u32[]{:S(2)}, u32[]{:S(2)}) %collective-permute-start.22) | collective-permute-done | bytes 458784 | tf_op jit(solution)/shard_map/ppermute | solution.py:547
  167.9 3.3 %collective-permute-start.27 = (s32[896,128]{1,0:T(8,128)}, s32[896,128]{1,0:T(8,128)}, u32[]{:S(2)}, u32[]{:S(2)}) collective-permute-start(s32[896,128]{1,0:T(8,128)} %collective-permute-done.24.rest_2_), channel_id=1, source_target_pairs={{0,56},{8,0},{16,8},{24,16},{32,24},{40,32},{48,40},{56,48},{1,57}... | collective-permute-start | bytes 1376264 | tf_op jit(solution)/shard_map/ppermute | solution.py:547
  171.1 12.2 %collective-permute-done.23.rest_1_ = s32[1408,128]{1,0:T(8,128)} collective-permute-done((s32[1408,128]{1,0:T(8,128)}, s32[1408,128]{1,0:T(8,128)}, u32[]{:S(2)}, u32[]{:S(2)}) %collective-permute-start.23) | collective-permute-done | bytes 720928 | tf_op jit(solution)/shard_map/ppermute | solution.py:547
  183.3 3.9 %shard_map.71.rest_0_ = s32[6144,128]{1,0:T(8,128)} custom-call(s32[2]{0:T(128)} %pad_add_fusion.2.place_ref, s32[256]{0:T(256)} %reshape.313.counts_ref, s32[256]{0:T(256)} %reshape.315.befores_ref, s32[896,128]{1,0:T(8,128)} %collective-permute-done.22.rest_0_, s32[1408,128]{1,0:T(8,128)} %collective-permute-done.23.rest_1_, ...), custom_call_target="tpu_custom_call" | custom-call | tf_op jit(solution)/shard_map/pallas_call | solution.py:353
  187.2 5.3 %collective-permute-done.26.rest_1_ = s32[896,128]{1,0:T(8,128)} collective-permute-done((s32[896,128]{1,0:T(8,128)}, s32[896,128]{1,0:T(8,128)}, u32[]{:S(2)}, u32[]{:S(2)}) %collective-permute-start.26) | collective-permute-done | bytes 458784 | tf_op jit(solution)/shard_map/ppermute | solution.py:547
  195.5 7.4 %all-to-all-start.4 = ((s32[32,12,16,128]{3,2,1,0:T(8,128)}), s32[32,12,16,128]{3,2,1,0:T(8,128)S(1)}, u32[]{:S(2)}, u32[]{:S(2)}) async-start(s32[32,12,16,128]{3,2,1,0:T(8,128)} %bitcast.53), calls=%async_computation.4 | async-start | bytes 6291456 | tf_op jit(solution)/shard_map/all_to_all | solution.py:542
  202.9 3.3 %scatter_custom_fusion = s32[4096]{0:T(1024)S(1)} fusion(s32[512]{0:T(512)S(1)} %compare_select_fusion, s32[512]{0:T(512)S(1)} %broadcast.590, s32[]{:T(128)} %constant.134.clone.1), kind=kCustom, calls=%fused_computation.56 | custom fusion | flops 512 | bytes 16388 | tf_op jit(solution)/shard_map/scatter-add | solution.py:583
  208.2 32.4 %collective-permute-done.1 = s32[4096]{0:T(1024)S(1)} collective-permute-done((s32[4096]{0:T(1024)S(1)}, s32[4096]{0:T(1024)S(1)}, u32[]{:S(2)}, u32[]{:S(2)}) %collective-permute-start.1) | collective-permute-done | bytes 16416 | tf_op jit(solution)/shard_map/ppermute | solution.py:547
  241.3 4.7 %collective-permute-done.2 = s32[4096]{0:T(1024)S(1)} collective-permute-done((s32[4096]{0:T(1024)S(1)}, s32[4096]{0:T(1024)S(1)}, u32[]{:S(2)}, u32[]{:S(2)}) %collective-permute-start.2) | collective-permute-done | bytes 16416 | tf_op jit(solution)/shard_map/ppermute | solution.py:547
  251.7 3.2 %collective-permute-done.4 = s32[4096]{0:T(1024)S(1)} collective-permute-done((s32[4096]{0:T(1024)S(1)}, s32[4096]{0:T(1024)S(1)}, u32[]{:S(2)}, u32[]{:S(2)}) %collective-permute-start.4) | collective-permute-done | bytes 16416 | tf_op jit(solution)/shard_map/ppermute | solution.py:547
  255.0 4.9 %collective-permute-done.5 = s32[4096]{0:T(1024)S(1)} collective-permute-done((s32[4096]{0:T(1024)S(1)}, s32[4096]{0:T(1024)S(1)}, u32[]{:S(2)}, u32[]{:S(2)}) %collective-permute-start.5) | collective-permute-done | bytes 16416 | tf_op jit(solution)/shard_map/ppermute | solution.py:547
  259.9 5.8 %collective-permute-done.6 = s32[4096]{0:T(1024)S(1)} collective-permute-done((s32[4096]{0:T(1024)S(1)}, s32[4096]{0:T(1024)S(1)}, u32[]{:S(2)}, u32[]{:S(2)}) %collective-permute-start.6) | collective-permute-done | bytes 16416 | tf_op jit(solution)/shard_map/ppermute | solution.py:547
  268.5 11.3 %place_bins.1 = s32[1024]{0:T(1024)} custom-call(s32[256]{0:T(256)S(1)} %dynamic-slice_reduce_fusion.counts_ref, s32[1]{0:T(128)} %bitcast.9.member_ref, s32[8192]{0:T(1024)} %reshape.334.keys_ref), custom_call_target="tpu_custom_call" | custom-call | tf_op jit(solution)/shard_map/place_bins/pallas_call | solution.py:143
  287.0 6.1 %gather_fusion = f32[1024]{0:T(1024)S(1)} fusion(f32[4096]{0:T(1024)S(1)} %rev.7, s32[1024]{0:T(1024)S(1)} %maximum_clamp_fusion), kind=kCustom, calls=%fused_computation | custom fusion | bytes 12288 | tf_op jit(solution)/shard_map/gather | solution.py:645
  294.4 10.4 %unpack_early.1.early_ref = s32[128,16,8,1,128]{4,3,2,1,0:T(1,128)} custom-call(s32[2]{0:T(128)} %pad_add_fusion.2.place_ref, s32[256]{0:T(256)S(1)} %dynamic-slice_reduce_fusion.counts_ref, s32[256]{0:T(256)} %bitcast.68, s32[384,16,1,128]{3,2,1,0:T(1,128)} %bitcast.55, s32[256,16,1,128]{3,2,1,0:T(1,128)} %bitcast.31.rest_1_), custom_call_target="tpu_custom_call" | custom-call | tf_op jit(solution)/shard_map/unpack_early/pallas_call | solution.py:445
  304.8 4.5 %unpack_last.1 = s32[128,16,8,1,128]{4,3,2,1,0:T(1,128)} custom-call(s32[2]{0:T(128)} %pad_add_fusion.2.place_ref, s32[256]{0:T(256)S(1)} %dynamic-slice_reduce_fusion.counts_ref, s32[256]{0:T(256)} %bitcast.69, s32[128,16,8,1,128]{4,3,2,1,0:T(1,128)} %unpack_early.1.early_ref, s32[384,16,1,128]{3,2,1,0:T(1,128)S(1)} %bitcast.48), custom_call_target="tpu_custom_call", output_to_operand_aliasing={{}: (3, {})} | custom-call | tf_op jit(solution)/shard_map/unpack_last/pallas_call | solution.py:480
  (111 shorter events, 45.6 us)
Async XLA Ops:
  10.9 35.6 %collective-permute-start.21 = (s32[1792,128]{1,0:T(8,128)}, s32[1792,128]{1,0:T(8,128)S(1)}, u32[]{:S(2)}, u32[]{:S(2)}) collective-permute-start(s32[1792,128]{1,0:T(8,128)} %bitcast.71), channel_id=1, source_target_pairs={{0,56},{8,0},{16,8},{24,16},{32,24},{40,32},{48,40},{56,48},{1,57}... | collective-permute-start | bytes 2752520 | tf_op jit(solution)/shard_map/ppermute | solution.py:547
  16.8 29.7 %collective-permute-start.20 = (s32[1792,128]{1,0:T(8,128)}, s32[1792,128]{1,0:T(8,128)S(1)}, u32[]{:S(2)}, u32[]{:S(2)}) collective-permute-start(s32[1792,128]{1,0:T(8,128)} %bitcast.70), channel_id=1, source_target_pairs={{0,8},{8,16},{16,24},{24,32},{32,40},{40,48},{48,56},{56,0},{1,9},... | collective-permute-start | bytes 2752520 | tf_op jit(solution)/shard_map/ppermute | solution.py:547
  18.0 26.3 %all-to-all-start.1 = ((s32[256,1,64]{2,1,0:T(1,128)}), s32[256,1,64]{2,1,0:T(1,128)S(1)}, u32[]{:S(2)}, u32[]{:S(2)}) async-start(s32[256,1,64]{2,1,0:T(1,128)} %bitcast.6), calls=%async_computation.1 | async-start | bytes 262144 | tf_op jit(solution)/shard_map/all_to_all | solution.py:542
  52.3 93.1 %all-to-all-start.2 = ((s32[32,12,16,128]{3,2,1,0:T(8,128)}), s32[32,12,16,128]{3,2,1,0:T(8,128)S(1)}, u32[]{:S(2)}, u32[]{:S(2)}) async-start(s32[32,12,16,128]{3,2,1,0:T(8,128)} %bitcast.54), calls=%async_computation.2 | async-start | bytes 6291456 | tf_op jit(solution)/shard_map/all_to_all | solution.py:542
  59.7 14.9 %collective-permute-start.8 = (s32[896,128]{1,0:T(8,128)}, s32[896,128]{1,0:T(8,128)S(1)}, u32[]{:S(2)}, u32[]{:S(2)}) collective-permute-start(s32[896,128]{1,0:T(8,128)} %bitcast.77), channel_id=1, source_target_pairs={{0,8},{8,16},{16,24},{24,32},{32,40},{40,48},{48,56},{56,0},{1,9},... | collective-permute-start | bytes 1376264 | tf_op jit(solution)/shard_map/ppermute | solution.py:547
  61.5 30.4 %collective-permute-start.10 = (s32[1408,128]{1,0:T(8,128)}, s32[1408,128]{1,0:T(8,128)S(1)}, u32[]{:S(2)}, u32[]{:S(2)}) collective-permute-start(s32[1408,128]{1,0:T(8,128)} %bitcast.73), channel_id=1, source_target_pairs={{0,8},{8,16},{16,24},{24,32},{32,40},{40,48},{48,56},{56,0},{1,9},... | collective-permute-start | bytes 2162696 | tf_op jit(solution)/shard_map/ppermute | solution.py:547
  62.8 29.3 %collective-permute-start.16 = (s32[1408,128]{1,0:T(8,128)}, s32[1408,128]{1,0:T(8,128)S(1)}, u32[]{:S(2)}, u32[]{:S(2)}) collective-permute-start(s32[1408,128]{1,0:T(8,128)} %bitcast.72), channel_id=1, source_target_pairs={{0,56},{8,0},{16,8},{24,16},{32,24},{40,32},{48,40},{56,48},{1,57}... | collective-permute-start | bytes 2162696 | tf_op jit(solution)/shard_map/ppermute | solution.py:547
  64.8 27.1 %collective-permute-start.14 = (s32[896,128]{1,0:T(8,128)}, s32[896,128]{1,0:T(8,128)S(1)}, u32[]{:S(2)}, u32[]{:S(2)}) collective-permute-start(s32[896,128]{1,0:T(8,128)} %bitcast.76), channel_id=1, source_target_pairs={{0,56},{8,0},{16,8},{24,16},{32,24},{40,32},{48,40},{56,48},{1,57}... | collective-permute-start | bytes 1376264 | tf_op jit(solution)/shard_map/ppermute | solution.py:547
  65.0 37.6 %collective-permute-start.12 = (s32[1152,128]{1,0:T(8,128)}, s32[1152,128]{1,0:T(8,128)S(1)}, u32[]{:S(2)}, u32[]{:S(2)}) collective-permute-start(s32[1152,128]{1,0:T(8,128)} %bitcast.75), channel_id=1, source_target_pairs={{0,8},{8,16},{16,24},{24,32},{32,40},{40,48},{48,56},{56,0},{1,9},... | collective-permute-start | bytes 1769480 | tf_op jit(solution)/shard_map/ppermute | solution.py:547
  74.6 29.9 %collective-permute-start.18 = (s32[1152,128]{1,0:T(8,128)}, s32[1152,128]{1,0:T(8,128)S(1)}, u32[]{:S(2)}, u32[]{:S(2)}) collective-permute-start(s32[1152,128]{1,0:T(8,128)} %bitcast.74), channel_id=1, source_target_pairs={{0,56},{8,0},{16,8},{24,16},{32,24},{40,32},{48,40},{56,48},{1,57}... | collective-permute-start | bytes 1769480 | tf_op jit(solution)/shard_map/ppermute | solution.py:547
  91.9 20.7 %collective-permute-start.9 = (s32[896,128]{1,0:T(8,128)S(1)}, s32[896,128]{1,0:T(8,128)}, u32[]{:S(2)}, u32[]{:S(2)}) collective-permute-start(s32[896,128]{1,0:T(8,128)S(1)} %collective-permute-done.8), channel_id=1, source_target_pairs={{0,8},{8,16},{16,24},{24,32},{32,40},{40,48},{48,56},{56,0},{1,9},... | collective-permute-start | bytes 1376264 | tf_op jit(solution)/shard_map/ppermute | solution.py:547
  92.0 49.2 %collective-permute-start.11 = (s32[1408,128]{1,0:T(8,128)S(1)}, s32[1408,128]{1,0:T(8,128)}, u32[]{:S(2)}, u32[]{:S(2)}) collective-permute-start(s32[1408,128]{1,0:T(8,128)S(1)} %collective-permute-done.10), channel_id=1, source_target_pairs={{0,8},{8,16},{16,24},{24,32},{32,40},{40,48},{48,56},{56,0},{1,9},... | collective-permute-start | bytes 2162696 | tf_op jit(solution)/shard_map/ppermute | solution.py:547
  92.2 49.0 %collective-permute-start.17 = (s32[1408,128]{1,0:T(8,128)S(1)}, s32[1408,128]{1,0:T(8,128)}, u32[]{:S(2)}, u32[]{:S(2)}) collective-permute-start(s32[1408,128]{1,0:T(8,128)S(1)} %collective-permute-done.16), channel_id=1, source_target_pairs={{0,56},{8,0},{16,8},{24,16},{32,24},{40,32},{48,40},{56,48},{1,57}... | collective-permute-start | bytes 2162696 | tf_op jit(solution)/shard_map/ppermute | solution.py:547
  102.6 38.5 %collective-permute-start.13 = (s32[1152,128]{1,0:T(8,128)S(1)}, s32[1152,128]{1,0:T(8,128)}, u32[]{:S(2)}, u32[]{:S(2)}) collective-permute-start(s32[1152,128]{1,0:T(8,128)S(1)} %collective-permute-done.12), channel_id=1, source_target_pairs={{0,8},{8,16},{16,24},{24,32},{32,40},{40,48},{48,56},{56,0},{1,9},... | collective-permute-start | bytes 1769480 | tf_op jit(solution)/shard_map/ppermute | solution.py:547
  104.5 36.6 %collective-permute-start.19 = (s32[1152,128]{1,0:T(8,128)S(1)}, s32[1152,128]{1,0:T(8,128)}, u32[]{:S(2)}, u32[]{:S(2)}) collective-permute-start(s32[1152,128]{1,0:T(8,128)S(1)} %collective-permute-done.18), channel_id=1, source_target_pairs={{0,56},{8,0},{16,8},{24,16},{32,24},{40,32},{48,40},{56,48},{1,57}... | collective-permute-start | bytes 1769480 | tf_op jit(solution)/shard_map/ppermute | solution.py:547
  112.6 28.5 %collective-permute-start.15 = (s32[896,128]{1,0:T(8,128)S(1)}, s32[896,128]{1,0:T(8,128)}, u32[]{:S(2)}, u32[]{:S(2)}) collective-permute-start(s32[896,128]{1,0:T(8,128)S(1)} %collective-permute-done.14), channel_id=1, source_target_pairs={{0,56},{8,0},{16,8},{24,16},{32,24},{40,32},{48,40},{56,48},{1,57}... | collective-permute-start | bytes 1376264 | tf_op jit(solution)/shard_map/ppermute | solution.py:547
  145.4 50.1 %all-to-all-start.3 = ((s32[32,8,16,128]{3,2,1,0:T(8,128)}), s32[32,8,16,128]{3,2,1,0:T(8,128)}, u32[]{:S(2)}, u32[]{:S(2)}) async-start(s32[32,8,16,128]{3,2,1,0:T(8,128)} %bitcast.56), calls=%async_computation.3 | async-start | bytes 4194304 | tf_op jit(solution)/shard_map/all_to_all | solution.py:542
  152.9 15.0 %collective-permute-start.22 = (s32[896,128]{1,0:T(8,128)}, s32[896,128]{1,0:T(8,128)}, u32[]{:S(2)}, u32[]{:S(2)}) collective-permute-start(s32[896,128]{1,0:T(8,128)} %collective-permute-done.9.rest_0_), channel_id=1, source_target_pairs={{0,8},{8,16},{16,24},{24,32},{32,40},{40,48},{48,56},{56,0},{1,9},... | collective-permute-start | bytes 1376264 | tf_op jit(solution)/shard_map/ppermute | solution.py:547
  153.3 14.6 %collective-permute-start.24 = (s32[896,128]{1,0:T(8,128)}, s32[896,128]{1,0:T(8,128)}, u32[]{:S(2)}, u32[]{:S(2)}) collective-permute-start(s32[896,128]{1,0:T(8,128)} %collective-permute-done.15.rest_3_), channel_id=1, source_target_pairs={{0,56},{8,0},{16,8},{24,16},{32,24},{40,32},{48,40},{56,48},{1,57}... | collective-permute-start | bytes 1376264 | tf_op jit(solution)/shard_map/ppermute | solution.py:547
  156.2 27.1 %collective-permute-start.23 = (s32[1408,128]{1,0:T(8,128)}, s32[1408,128]{1,0:T(8,128)}, u32[]{:S(2)}, u32[]{:S(2)}) collective-permute-start(s32[1408,128]{1,0:T(8,128)} %collective-permute-done.11.rest_1_), channel_id=1, source_target_pairs={{0,8},{8,16},{16,24},{24,32},{32,40},{40,48},{48,56},{56,0},{1,9},... | collective-permute-start | bytes 2162696 | tf_op jit(solution)/shard_map/ppermute | solution.py:547
  156.2 27.1 %collective-permute-start.25 = (s32[1408,128]{1,0:T(8,128)}, s32[1408,128]{1,0:T(8,128)}, u32[]{:S(2)}, u32[]{:S(2)}) collective-permute-start(s32[1408,128]{1,0:T(8,128)} %collective-permute-done.17.rest_4_), channel_id=1, source_target_pairs={{0,56},{8,0},{16,8},{24,16},{32,24},{40,32},{48,40},{56,48},{1,57}... | collective-permute-start | bytes 2162696 | tf_op jit(solution)/shard_map/ppermute | solution.py:547
  167.9 24.7 %collective-permute-start.26 = (s32[896,128]{1,0:T(8,128)}, s32[896,128]{1,0:T(8,128)}, u32[]{:S(2)}, u32[]{:S(2)}) collective-permute-start(s32[896,128]{1,0:T(8,128)} %collective-permute-done.22.rest_0_), channel_id=1, source_target_pairs={{0,8},{8,16},{16,24},{24,32},{32,40},{40,48},{48,56},{56,0},{1,9},... | collective-permute-start | bytes 1376264 | tf_op jit(solution)/shard_map/ppermute | solution.py:547
  167.9 24.7 %collective-permute-start.27 = (s32[896,128]{1,0:T(8,128)}, s32[896,128]{1,0:T(8,128)}, u32[]{:S(2)}, u32[]{:S(2)}) collective-permute-start(s32[896,128]{1,0:T(8,128)} %collective-permute-done.24.rest_2_), channel_id=1, source_target_pairs={{0,56},{8,0},{16,8},{24,16},{32,24},{40,32},{48,40},{56,48},{1,57}... | collective-permute-start | bytes 1376264 | tf_op jit(solution)/shard_map/ppermute | solution.py:547
  195.5 109.3 %all-to-all-start.4 = ((s32[32,12,16,128]{3,2,1,0:T(8,128)}), s32[32,12,16,128]{3,2,1,0:T(8,128)S(1)}, u32[]{:S(2)}, u32[]{:S(2)}) async-start(s32[32,12,16,128]{3,2,1,0:T(8,128)} %bitcast.53), calls=%async_computation.4 | async-start | bytes 6291456 | tf_op jit(solution)/shard_map/all_to_all | solution.py:542
  206.2 1.5 collective-permute-start
  207.7 33.0 %collective-permute-start.1 = (s32[4096]{0:T(1024)S(1)}, s32[4096]{0:T(1024)S(1)}, u32[]{:S(2)}, u32[]{:S(2)}) collective-permute-start(s32[4096]{0:T(1024)S(1)} %add.237), channel_id=1, source_target_pairs={{0,2},{2,4},{4,6},{6,0},{1,3},{3,5},{5,7},{7,1},{8,10},{10,12},{12... | collective-permute-start | bytes 49160 | tf_op jit(solution)/shard_map/ppermute | solution.py:547
  240.7 5.2 %collective-permute-start.2 = (s32[4096]{0:T(1024)S(1)}, s32[4096]{0:T(1024)S(1)}, u32[]{:S(2)}, u32[]{:S(2)}) collective-permute-start(s32[4096]{0:T(1024)S(1)} %add.238), channel_id=1, source_target_pairs={{0,4},{2,6},{4,0},{6,2},{1,5},{3,7},{5,1},{7,3},{8,12},{10,14},{12... | collective-permute-start | bytes 49160 | tf_op jit(solution)/shard_map/ppermute | solution.py:547
  245.9 3.7 %collective-permute-start.3 = (s32[4096]{0:T(1024)S(1)}, s32[4096]{0:T(1024)S(1)}, u32[]{:S(2)}, u32[]{:S(2)}) collective-permute-start(s32[4096]{0:T(1024)S(1)} %add.239), channel_id=1, source_target_pairs={{0,64},{64,128},{128,192},{192,0},{1,65},{65,129},{129,193},{193,1... | collective-permute-start | bytes 49160 | tf_op jit(solution)/shard_map/ppermute | solution.py:547
  249.7 5.2 %collective-permute-start.4 = (s32[4096]{0:T(1024)S(1)}, s32[4096]{0:T(1024)S(1)}, u32[]{:S(2)}, u32[]{:S(2)}) collective-permute-start(s32[4096]{0:T(1024)S(1)} %add.240), channel_id=1, source_target_pairs={{0,128},{64,192},{128,0},{192,64},{1,129},{65,193},{129,1},{193,65... | collective-permute-start | bytes 49160 | tf_op jit(solution)/shard_map/ppermute | solution.py:547
  254.9 4.9 %collective-permute-start.5 = (s32[4096]{0:T(1024)S(1)}, s32[4096]{0:T(1024)S(1)}, u32[]{:S(2)}, u32[]{:S(2)}) collective-permute-start(s32[4096]{0:T(1024)S(1)} %add.241), channel_id=1, source_target_pairs={{0,8},{8,16},{16,24},{24,32},{32,40},{40,48},{48,56},{56,0},{1,9},... | collective-permute-start | bytes 49160 | tf_op jit(solution)/shard_map/ppermute | solution.py:547
  259.9 5.9 %collective-permute-start.6 = (s32[4096]{0:T(1024)S(1)}, s32[4096]{0:T(1024)S(1)}, u32[]{:S(2)}, u32[]{:S(2)}) collective-permute-start(s32[4096]{0:T(1024)S(1)} %add.242), channel_id=1, source_target_pairs={{0,16},{8,24},{16,32},{24,40},{32,48},{40,56},{48,0},{56,8},{1,17}... | collective-permute-start | bytes 49160 | tf_op jit(solution)/shard_map/ppermute | solution.py:547
  265.7 19.3 %collective-permute-start.7 = (s32[4096]{0:T(1024)S(1)}, s32[4096]{0:T(1024)S(1)}, u32[]{:S(2)}, u32[]{:S(2)}) collective-permute-start(s32[4096]{0:T(1024)S(1)} %add.243), channel_id=1, source_target_pairs={{0,32},{8,40},{16,48},{24,56},{32,0},{40,8},{48,16},{56,24},{1,33}... | collective-permute-start | bytes 49160 | tf_op jit(solution)/shard_map/ppermute | solution.py:547
  (6 other events, 78.8 us)

commit v4 on v3

--- a/solution.py
+++ b/solution.py
@@ -16,6 +16,7 @@
 STEP = 64
 
 SMEM = pltpu.MemorySpace.SMEM
+VMEM = pltpu.MemorySpace.VMEM
 
 
 def smem_spec():
@@ -244,7 +245,7 @@
 
             def some(i, carry, out=out, start=start):
                 for j in range(8):
-                    row = source_ref[start + i * 8 + j]
+                    row = source_ref[0, start + i * 8 + j]
                     pltpu.make_async_copy(slot_of(buf, row), out.at[i * 8 + j], sem_out).start()
                 return carry
 
@@ -488,35 +489,79 @@
     )(place, counts, befores, early, last)
 
 
-def relay_source(counts, local_rank, onehot, z):
-    owner = jnp.arange(32, dtype=jnp.int32)
-    y, d = owner // 8, (owner - z) % 8
-    dist = jnp.minimum(d, 8 - d)
-    earlier = (((4 - dist) * 4 + y)[None, :] < ((4 - dist) * 4 + y)[:, None]) & ((dist > 1)[None, :] == (dist > 1)[:, None])
-
-    def start(members, sizes):
-        return jnp.sum(jnp.where(earlier & members[None, :], sizes[None, :], 0), axis=1)
-
-    ahead, back = (d >= 1) & (d <= 4), d >= 4
-    start_ahead = start(ahead, jnp.where(d == 4, (counts + 1) >> 1, counts))
-    start_back = start(back, jnp.where(d == 4, counts >> 1, counts))
-    far_ahead, far_back, mine = 2 * NEAR, 2 * NEAR + EDGES[-1], 2 * NEAR + 2 * EDGES[-1]
-    first = jnp.where(d == 0, mine, jnp.where(ahead, jnp.where(d == 1, 0, far_ahead), jnp.where(d == 7, NEAR, far_back)))
-    base = first + jnp.where(d == 0, start(d == 0, counts), jnp.where(ahead, start_ahead, start_back))
-    other = far_back + start_back
-    limit = first + jnp.where(d == 0, OWN, jnp.where(dist == 1, NEAR, EDGES[-1]))
-
-    def pick(values):
-        return jnp.sum(onehot * values[None, :], axis=1)
-
-    four = pick((d == 4).astype(jnp.int32)) == 1
-    odd = four & ((local_rank & 1) == 1)
-    position = jnp.where(odd, pick(other), pick(base)) + jnp.where(four, local_rank >> 1, local_rank)
-    bound = jnp.where(odd, mine, pick(limit))
-    position = jnp.where((jnp.sum(onehot, axis=1) == 1) & (position < bound), position, -1)
-    example = jnp.arange(onehot.shape[0], dtype=jnp.int32)
-    places = jnp.arange(PLACES, dtype=jnp.int32)
-    return jnp.sum(jnp.where(position[None, :] == places[:, None], example[None, :], 0), axis=1)
+def plan_relay(keys, dest, cut, z):
+    examples = keys.shape[1]
+    padded = -(-PLACES // LANES) * LANES
+
+    def across(left, right):
+        return lax.dot_general(left, right, (((1,), (1,)), ((), ())), preferred_element_type=jnp.float32)
+
+    def kernel(keys_ref, dest_ref, cut_ref, z_ref, plan_ref, rank_ref, counts_ref):
+        kept = (keys_ref[...] >> KEY_SHIFT) >= cut_ref[0]
+        owner = lax.broadcasted_iota(jnp.int32, (32, examples), 0)
+        hot = (dest_ref[...] == owner) & kept
+        ones = jnp.where(hot, 1.0, 0.0).astype(jnp.bfloat16)
+        row = lax.broadcasted_iota(jnp.int32, (examples, examples), 0)
+        col = lax.broadcasted_iota(jnp.int32, (examples, examples), 1)
+        before = jnp.where(row < col, 1.0, 0.0).astype(jnp.bfloat16)
+        running = jnp.dot(ones, before, preferred_element_type=jnp.float32).astype(jnp.int32)
+        counts = across(jnp.ones((8, examples), jnp.bfloat16), ones).astype(jnp.int32)[0:1, :]
+        counts_ref[...] = counts
+        rank_ref[...] = jnp.sum(jnp.where(hot, running, 0), axis=0, keepdims=True)
+
+        z = z_ref[0]
+
+        def about(axis):
+            o = lax.broadcasted_iota(jnp.int32, (32, 32), axis)
+            d = ((o & 7) - z) & 7
+            dist = jnp.minimum(d, 8 - d)
+            far = jnp.where(dist > 1, 1, 0)
+            return d, dist, far * 64 + (4 - dist) * 4 + (o >> 3), far
+
+        d, dist, order, far = about(0)
+        d_of, _, order_of, far_of = about(1)
+        earlier = (order_of < order) & (far_of == far)
+
+        def start(members, sizes):
+            return jnp.sum(jnp.where(earlier & members, sizes, 0), axis=1, keepdims=True)
+
+        start_ahead = start((d_of >= 1) & (d_of <= 4), jnp.where(d_of == 4, (counts + 1) >> 1, counts))
+        start_back = start(d_of >= 4, jnp.where(d_of == 4, counts >> 1, counts))
+        start_own = start(d_of == 0, jnp.broadcast_to(counts, (32, 32)))
+        d, dist = d[:, 0:1], dist[:, 0:1]
+        ahead = (d >= 1) & (d <= 4)
+        far_ahead, far_back, mine = 2 * NEAR, 2 * NEAR + EDGES[-1], 2 * NEAR + 2 * EDGES[-1]
+        first = jnp.where(
+            d == 0, mine, jnp.where(ahead, jnp.where(d == 1, 0, far_ahead), jnp.where(d == 7, NEAR, far_back))
+        )
+        base = first + jnp.where(d == 0, start_own, jnp.where(ahead, start_ahead, start_back))
+        other = far_back + start_back
+        limit = first + jnp.where(d == 0, OWN, jnp.where(dist == 1, NEAR, EDGES[-1]))
+        odd = (d == 4) & ((running & 1) == 1)
+        position = jnp.where(odd, other, base) + jnp.where(d == 4, running >> 1, running)
+        bound = jnp.where(odd, mine, limit)
+        position = jnp.sum(jnp.where(hot & (position < bound), position + 1, 0), axis=0, keepdims=True) - 1
+
+        place = lax.broadcasted_iota(jnp.int32, (padded, examples), 0)
+        here = jnp.where(place == position, 1.0, 0.0).astype(jnp.bfloat16)
+        part = lax.broadcasted_iota(jnp.int32, (8, examples), 0)
+        example = lax.broadcasted_iota(jnp.int32, (8, examples), 1)
+        parts = jnp.where(part == 0, example >> 4, jnp.where(part == 1, example & 15, 0))
+        found = across(parts.astype(jnp.float32).astype(jnp.bfloat16), here).astype(jnp.int32)
+        plan_ref[...] = found[0:1, :] * 16 + found[1:2, :]
+
+    whole = pl.BlockSpec(memory_space=VMEM)
+    return pl.pallas_call(
+        kernel,
+        in_specs=[whole, whole, smem_spec(), smem_spec()],
+        out_specs=[whole] * 3,
+        out_shape=[
+            jax.ShapeDtypeStruct((1, padded), jnp.int32),
+            jax.ShapeDtypeStruct((1, examples), jnp.int32),
+            jax.ShapeDtypeStruct((1, 32), jnp.int32),
+        ],
+        name="plan_relay",
+    )(keys, dest, cut, z)
 
 
 def by_owner(values, position, size):
@@ -568,14 +613,8 @@
     bins_of = keys >> KEY_SHIFT
     dest = owner[:, 0]
     kept = bins_of >= cut[0]
-    owners = jnp.arange(n_owner, dtype=jnp.int32)
-    onehot = ((dest[:, None] == owners[None, :]) & kept[:, None]).astype(jnp.int32)
-    counts = jnp.sum(onehot, axis=0)
-    index = jnp.arange(examples, dtype=jnp.int32)
-    lower = (index[None, :] < index[:, None]).astype(jnp.bfloat16)
-    running = jnp.dot(lower, onehot.astype(jnp.bfloat16), preferred_element_type=jnp.float32).astype(jnp.int32)
-    local_rank = jnp.sum(running * onehot, axis=1)
-    source = relay_source(counts, local_rank, onehot, z)
+    source, local_rank, counts = plan_relay(keys[None, :], owner.reshape(1, -1), cut, z[None].astype(jnp.int32))
+    local_rank, counts = local_rank[0], counts[0]
     near = pack_relay(source, tokens, 0, [NEAR] * 2)
     *far, own = pack_relay(source, tokens, 2 * NEAR, [n for _, n in segments(1)] * 2 + [OWN])
     plus, minus = far[:3], far[3:]

time: 311 us -> 307 us (0.987)
  other arithmetic: 13.3 us -> 9.08 us
  transfers between devices with their start and end apart: 32 -> 32, of which waited for: 17 -> 17; matrix products, arithmetic and copies ran while one was open for 6% -> 6% of each run, Pallas kernels for 12% -> 13%
where the time goes in v4:
time: 307 us; the launch traced here: 306 us
  waiting for transfers between devices  157 us (51%)
  starting transfers between devices  70 us (23%)
  Pallas kernels  53.8 us (18%)
  local copies, waits for them, and re-layouts  11.4 us (4%)
  other arithmetic  9.08 us (3%)
  between operations  4.99 us (2%)
    ppermute x28, waiting for transfers between devices, hop_on(): lax.ppermute(value, axis, [(i, (i + step) % count) for i in range(count)])  147 us
    ppermute x28, starting transfers between devices, hop_on(): lax.ppermute(value, axis, [(i, (i + step) % count) for i in range(count)])  37.2 us
    all_to_all x4, starting transfers between devices, exchange(): return lax.all_to_all(value, axes, split_axis=0, concat_axis=0, tiled=True)  32.8 us
    pallas_call x4, Pallas kernels, spread(): pl.pallas_call(kernel, in_specs=[smem_spec()] * 3 + [any_spec()] * (len(b...  15.6 us
    pallas_call x1, Pallas kernels, place_bins(): pl.pallas_call(kernel, in_specs=[smem_spec()] * 3, out_specs=smem_spec(),...  11.3 us
    pallas_call x1, Pallas kernels, unpack_early(): pl.pallas_call(kernel, in_specs=[smem_spec()] * 3 + [any_spec()] * len(go...  10.4 us
    pallas_call x2, Pallas kernels, pack_relay(): pl.pallas_call(kernel, in_specs=[smem_spec(), any_spec()], out_specs=[any...  10 us
    all_to_all x4, waiting for transfers between devices, exchange(): return lax.all_to_all(value, axes, split_axis=0, concat_axis=0, tiled=True)  9.52 us
  transfers between devices with their start and end apart: 32, of which 17 were waited for; matrix products, arithmetic and copies ran while one was open for 6% of the time, Pallas kernels for 13%

profile of v4, /device:TPU:22, one launch (start us, length us, event | category | flops | bytes accessed | tf_op | source)
XLA Modules:
  0.0 306.4 jit_solution(17111835957114683860)
XLA Ops:
  3.3 4.5 %shard_map.69 = (s32[112,16,1,128]{3,2,1,0:T(1,128)}, s32[112,16,1,128]{3,2,1,0:T(1,128)}) custom-call(s32[1,896]{1,0:T(1,128)} %get-tuple-element.68.source_ref, s32[64,16,8,1,128]{4,3,2,1,0:T(1,128)} %bitcast.53), custom_call_target="tpu_custom_call" | custom-call | tf_op jit(solution)/shard_map/pallas_call | solution.py:257
  7.8 5.9 %collective-permute-start.21 = (s32[1792,128]{1,0:T(8,128)}, s32[1792,128]{1,0:T(8,128)S(1)}, u32[]{:S(2)}, u32[]{:S(2)}) collective-permute-start(s32[1792,128]{1,0:T(8,128)} %bitcast.74), channel_id=1, source_target_pairs={{0,56},{8,0},{16,8},{24,16},{32,24},{40,32},{48,40},{56,48},{1,57}... | collective-permute-start | bytes 2752520 | tf_op jit(solution)/shard_map/ppermute | solution.py:592
  14.9 10.6 %all-to-all-start.1 = ((s32[256,1,64]{2,1,0:T(1,128)}), s32[256,1,64]{2,1,0:T(1,128)S(1)}, u32[]{:S(2)}, u32[]{:S(2)}) async-start(s32[256,1,64]{2,1,0:T(1,128)} %bitcast.11), calls=%async_computation.1 | async-start | bytes 262144 | tf_op jit(solution)/shard_map/all_to_all | solution.py:587
  26.1 5.6 %shard_map.67 = (s32[56,16,1,128]{3,2,1,0:T(1,128)}, s32[88,16,1,128]{3,2,1,0:T(1,128)}, s32[72,16,1,128]{3,2,1,0:T(1,128)}, s32[56,16,1,128]{3,2,1,0:T(1,128)},...) custom-call(s32[1,896]{1,0:T(1,128)} %get-tuple-element.68.source_ref, ...), custom_call_target="tpu_custom_call" | custom-call | tf_op jit(solution)/shard_map/pallas_call | solution.py:257
  31.7 9.5 %all-to-all-done.1 = s32[256,1,64]{2,1,0:T(1,128)S(1)} async-done(((s32[256,1,64]{2,1,0:T(1,128)}), s32[256,1,64]{2,1,0:T(1,128)S(1)}, u32[]{:S(2)}, u32[]{:S(2)}) %all-to-all-start.1) | async-done | bytes 65568 | tf_op jit(solution)/shard_map/all_to_all | solution.py:587
  44.6 4.5 %shard_map.70 = s32[6144,128]{1,0:T(8,128)} custom-call(s32[2]{0:T(128)} %pad_add_fusion.2.place_ref, s32[256]{0:T(256)} %reshape.167.counts_ref, s32[256]{0:T(256)} %reshape.169.befores_ref, s32[2048,128]{1,0:T(8,128)} %bitcast.62, s32[1792,128]{1,0:T(8,128)} %copy-done.2, s32[1792,128]{1,0:T(8,128)} %copy-done.1), custom_call_target="tpu_custom_call" | custom-call | tf_op jit(solution)/shard_map/pallas_call | solution.py:354
  49.1 7.4 %all-to-all-start.2 = ((s32[32,12,16,128]{3,2,1,0:T(8,128)}), s32[32,12,16,128]{3,2,1,0:T(8,128)S(1)}, u32[]{:S(2)}, u32[]{:S(2)}) async-start(s32[32,12,16,128]{3,2,1,0:T(8,128)} %bitcast.57), calls=%async_computation.2 | async-start | bytes 6291456 | tf_op jit(solution)/shard_map/all_to_all | solution.py:587
  63.7 7.7 %collective-permute-done.8 = s32[896,128]{1,0:T(8,128)S(1)} collective-permute-done((s32[896,128]{1,0:T(8,128)}, s32[896,128]{1,0:T(8,128)S(1)}, u32[]{:S(2)}, u32[]{:S(2)}) %collective-permute-start.8) | collective-permute-done | bytes 458784 | tf_op jit(solution)/shard_map/ppermute | solution.py:592
  71.4 17.3 %collective-permute-done.14 = s32[896,128]{1,0:T(8,128)S(1)} collective-permute-done((s32[896,128]{1,0:T(8,128)}, s32[896,128]{1,0:T(8,128)S(1)}, u32[]{:S(2)}, u32[]{:S(2)}) %collective-permute-start.14) | collective-permute-done | bytes 458784 | tf_op jit(solution)/shard_map/ppermute | solution.py:592
  92.1 7.5 %collective-permute-done.12 = s32[1152,128]{1,0:T(8,128)S(1)} collective-permute-done((s32[1152,128]{1,0:T(8,128)}, s32[1152,128]{1,0:T(8,128)S(1)}, u32[]{:S(2)}, u32[]{:S(2)}) %collective-permute-start.12) | collective-permute-done | bytes 589856 | tf_op jit(solution)/shard_map/ppermute | solution.py:592
  101.4 3.2 %collective-permute-start.19 = (s32[1152,128]{1,0:T(8,128)S(1)}, s32[1152,128]{1,0:T(8,128)}, u32[]{:S(2)}, u32[]{:S(2)}) collective-permute-start(s32[1152,128]{1,0:T(8,128)S(1)} %collective-permute-done.18), channel_id=1, source_target_pairs={{0,56},{8,0},{16,8},{24,16},{32,24},{40,32},{48,40},{56,48},{1,57}... | collective-permute-start | bytes 1769480 | tf_op jit(solution)/shard_map/ppermute | solution.py:592
  104.6 4.9 %collective-permute-done.9.rest_0_ = s32[896,128]{1,0:T(8,128)} collective-permute-done((s32[896,128]{1,0:T(8,128)S(1)}, s32[896,128]{1,0:T(8,128)}, u32[]{:S(2)}, u32[]{:S(2)}) %collective-permute-start.9) | collective-permute-done | bytes 458784 | tf_op jit(solution)/shard_map/ppermute | solution.py:592
  109.5 28.5 %collective-permute-done.15.rest_3_ = s32[896,128]{1,0:T(8,128)} collective-permute-done((s32[896,128]{1,0:T(8,128)S(1)}, s32[896,128]{1,0:T(8,128)}, u32[]{:S(2)}, u32[]{:S(2)}) %collective-permute-start.15) | collective-permute-done | bytes 458784 | tf_op jit(solution)/shard_map/ppermute | solution.py:592
  138.0 4.2 %shard_map.68 = s32[4096,128]{1,0:T(8,128)} custom-call(s32[2]{0:T(128)} %pad_add_fusion.2.place_ref, s32[256]{0:T(256)} %reshape.167.counts_ref, s32[256]{0:T(256)} %reshape.169.befores_ref, s32[896,128]{1,0:T(8,128)} %collective-permute-done.9.rest_0_, s32[1408,128]{1,0:T(8,128)} %collective-permute-done.11.rest_1_, ...), custom_call_target="tpu_custom_call" | custom-call | tf_op jit(solution)/shard_map/pallas_call | solution.py:354
  142.3 7.4 %all-to-all-start.3 = ((s32[32,8,16,128]{3,2,1,0:T(8,128)}), s32[32,8,16,128]{3,2,1,0:T(8,128)}, u32[]{:S(2)}, u32[]{:S(2)}) async-start(s32[32,8,16,128]{3,2,1,0:T(8,128)} %bitcast.59), calls=%async_computation.3 | async-start | bytes 4194304 | tf_op jit(solution)/shard_map/all_to_all | solution.py:587
  153.1 3.2 %collective-permute-start.25 = (s32[1408,128]{1,0:T(8,128)}, s32[1408,128]{1,0:T(8,128)}, u32[]{:S(2)}, u32[]{:S(2)}) collective-permute-start(s32[1408,128]{1,0:T(8,128)} %collective-permute-done.17.rest_4_), channel_id=1, source_target_pairs={{0,56},{8,0},{16,8},{24,16},{32,24},{40,32},{48,40},{56,48},{1,57}... | collective-permute-start | bytes 2162696 | tf_op jit(solution)/shard_map/ppermute | solution.py:592
  156.3 8.4 %collective-permute-done.22.rest_0_ = s32[896,128]{1,0:T(8,128)} collective-permute-done((s32[896,128]{1,0:T(8,128)}, s32[896,128]{1,0:T(8,128)}, u32[]{:S(2)}, u32[]{:S(2)}) %collective-permute-start.22) | collective-permute-done | bytes 458784 | tf_op jit(solution)/shard_map/ppermute | solution.py:592
  164.7 3.3 %collective-permute-start.27 = (s32[896,128]{1,0:T(8,128)}, s32[896,128]{1,0:T(8,128)}, u32[]{:S(2)}, u32[]{:S(2)}) collective-permute-start(s32[896,128]{1,0:T(8,128)} %collective-permute-done.24.rest_2_), channel_id=1, source_target_pairs={{0,56},{8,0},{16,8},{24,16},{32,24},{40,32},{48,40},{56,48},{1,57}... | collective-permute-start | bytes 1376264 | tf_op jit(solution)/shard_map/ppermute | solution.py:592
  168.0 12.2 %collective-permute-done.23.rest_1_ = s32[1408,128]{1,0:T(8,128)} collective-permute-done((s32[1408,128]{1,0:T(8,128)}, s32[1408,128]{1,0:T(8,128)}, u32[]{:S(2)}, u32[]{:S(2)}) %collective-permute-start.23) | collective-permute-done | bytes 720928 | tf_op jit(solution)/shard_map/ppermute | solution.py:592
  180.2 3.9 %shard_map.71.rest_0_ = s32[6144,128]{1,0:T(8,128)} custom-call(s32[2]{0:T(128)} %pad_add_fusion.2.place_ref, s32[256]{0:T(256)} %reshape.167.counts_ref, s32[256]{0:T(256)} %reshape.169.befores_ref, s32[896,128]{1,0:T(8,128)} %collective-permute-done.22.rest_0_, s32[1408,128]{1,0:T(8,128)} %collective-permute-done.23.rest_1_, ...), custom_call_target="tpu_custom_call" | custom-call | tf_op jit(solution)/shard_map/pallas_call | solution.py:354
  184.1 5.3 %collective-permute-done.26.rest_1_ = s32[896,128]{1,0:T(8,128)} collective-permute-done((s32[896,128]{1,0:T(8,128)}, s32[896,128]{1,0:T(8,128)}, u32[]{:S(2)}, u32[]{:S(2)}) %collective-permute-start.26) | collective-permute-done | bytes 458784 | tf_op jit(solution)/shard_map/ppermute | solution.py:592
  192.4 7.4 %all-to-all-start.4 = ((s32[32,12,16,128]{3,2,1,0:T(8,128)}), s32[32,12,16,128]{3,2,1,0:T(8,128)S(1)}, u32[]{:S(2)}, u32[]{:S(2)}) async-start(s32[32,12,16,128]{3,2,1,0:T(8,128)} %bitcast.56), calls=%async_computation.4 | async-start | bytes 6291456 | tf_op jit(solution)/shard_map/all_to_all | solution.py:587
  199.8 3.3 %scatter_custom_fusion = s32[4096]{0:T(1024)S(1)} fusion(s32[512]{0:T(512)S(1)} %get-tuple-element.115, s32[512]{0:T(512)S(1)} %broadcast.95, s32[]{:T(128)} %constant.96.clone.1), kind=kCustom, calls=%fused_computation.35 | custom fusion | flops 512 | bytes 16388 | tf_op jit(solution)/shard_map/scatter-add | solution.py:622
  204.9 32.7 %collective-permute-done.1 = s32[4096]{0:T(1024)S(1)} collective-permute-done((s32[4096]{0:T(1024)S(1)}, s32[4096]{0:T(1024)S(1)}, u32[]{:S(2)}, u32[]{:S(2)}) %collective-permute-start.1) | collective-permute-done | bytes 16416 | tf_op jit(solution)/shard_map/ppermute | solution.py:592
  238.1 4.7 %collective-permute-done.2 = s32[4096]{0:T(1024)S(1)} collective-permute-done((s32[4096]{0:T(1024)S(1)}, s32[4096]{0:T(1024)S(1)}, u32[]{:S(2)}, u32[]{:S(2)}) %collective-permute-start.2) | collective-permute-done | bytes 16416 | tf_op jit(solution)/shard_map/ppermute | solution.py:592
  248.5 3.2 %collective-permute-done.4 = s32[4096]{0:T(1024)S(1)} collective-permute-done((s32[4096]{0:T(1024)S(1)}, s32[4096]{0:T(1024)S(1)}, u32[]{:S(2)}, u32[]{:S(2)}) %collective-permute-start.4) | collective-permute-done | bytes 16416 | tf_op jit(solution)/shard_map/ppermute | solution.py:592
  251.9 4.9 %collective-permute-done.5 = s32[4096]{0:T(1024)S(1)} collective-permute-done((s32[4096]{0:T(1024)S(1)}, s32[4096]{0:T(1024)S(1)}, u32[]{:S(2)}, u32[]{:S(2)}) %collective-permute-start.5) | collective-permute-done | bytes 16416 | tf_op jit(solution)/shard_map/ppermute | solution.py:592
  256.8 5.8 %collective-permute-done.6 = s32[4096]{0:T(1024)S(1)} collective-permute-done((s32[4096]{0:T(1024)S(1)}, s32[4096]{0:T(1024)S(1)}, u32[]{:S(2)}, u32[]{:S(2)}) %collective-permute-start.6) | collective-permute-done | bytes 16416 | tf_op jit(solution)/shard_map/ppermute | solution.py:592
  265.4 11.3 %place_bins.1 = s32[1024]{0:T(1024)} custom-call(s32[256]{0:T(256)S(1)} %dynamic-slice_reduce_fusion.counts_ref, s32[1]{0:T(128)} %bitcast.13.member_ref, s32[8192]{0:T(1024)} %reshape.188.keys_ref), custom_call_target="tpu_custom_call" | custom-call | tf_op jit(solution)/shard_map/place_bins/pallas_call | solution.py:144
  283.9 6.1 %gather_fusion = f32[1024]{0:T(1024)S(1)} fusion(f32[4096]{0:T(1024)S(1)} %rev.7, s32[1024]{0:T(1024)S(1)} %maximum_clamp_fusion), kind=kCustom, calls=%fused_computation | custom fusion | bytes 12288 | tf_op jit(solution)/shard_map/gather | solution.py:684
  291.3 10.4 %unpack_early.1.early_ref = s32[128,16,8,1,128]{4,3,2,1,0:T(1,128)} custom-call(s32[2]{0:T(128)} %pad_add_fusion.2.place_ref, s32[256]{0:T(256)S(1)} %dynamic-slice_reduce_fusion.counts_ref, s32[256]{0:T(256)} %bitcast.70, s32[384,16,1,128]{3,2,1,0:T(1,128)} %bitcast.58, s32[256,16,1,128]{3,2,1,0:T(1,128)} %bitcast.35.rest_1_), custom_call_target="tpu_custom_call" | custom-call | tf_op jit(solution)/shard_map/unpack_early/pallas_call | solution.py:446
  301.7 4.5 %unpack_last.1 = s32[128,16,8,1,128]{4,3,2,1,0:T(1,128)} custom-call(s32[2]{0:T(128)} %pad_add_fusion.2.place_ref, s32[256]{0:T(256)S(1)} %dynamic-slice_reduce_fusion.counts_ref, s32[256]{0:T(256)} %bitcast.71, s32[128,16,8,1,128]{4,3,2,1,0:T(1,128)} %unpack_early.1.early_ref, s32[384,16,1,128]{3,2,1,0:T(1,128)S(1)} %bitcast.51), custom_call_target="tpu_custom_call", output_to_operand_aliasing={{}: (3, {})} | custom-call | tf_op jit(solution)/shard_map/unpack_last/pallas_call | solution.py:481
  (100 shorter events, 42.1 us)
Async XLA Ops:
  7.8 35.6 %collective-permute-start.21 = (s32[1792,128]{1,0:T(8,128)}, s32[1792,128]{1,0:T(8,128)S(1)}, u32[]{:S(2)}, u32[]{:S(2)}) collective-permute-start(s32[1792,128]{1,0:T(8,128)} %bitcast.74), channel_id=1, source_target_pairs={{0,56},{8,0},{16,8},{24,16},{32,24},{40,32},{48,40},{56,48},{1,57}... | collective-permute-start | bytes 2752520 | tf_op jit(solution)/shard_map/ppermute | solution.py:592
  13.7 29.7 %collective-permute-start.20 = (s32[1792,128]{1,0:T(8,128)}, s32[1792,128]{1,0:T(8,128)S(1)}, u32[]{:S(2)}, u32[]{:S(2)}) collective-permute-start(s32[1792,128]{1,0:T(8,128)} %bitcast.73), channel_id=1, source_target_pairs={{0,8},{8,16},{16,24},{24,32},{32,40},{40,48},{48,56},{56,0},{1,9},... | collective-permute-start | bytes 2752520 | tf_op jit(solution)/shard_map/ppermute | solution.py:592
  14.9 26.3 %all-to-all-start.1 = ((s32[256,1,64]{2,1,0:T(1,128)}), s32[256,1,64]{2,1,0:T(1,128)S(1)}, u32[]{:S(2)}, u32[]{:S(2)}) async-start(s32[256,1,64]{2,1,0:T(1,128)} %bitcast.11), calls=%async_computation.1 | async-start | bytes 262144 | tf_op jit(solution)/shard_map/all_to_all | solution.py:587
  49.1 93.1 %all-to-all-start.2 = ((s32[32,12,16,128]{3,2,1,0:T(8,128)}), s32[32,12,16,128]{3,2,1,0:T(8,128)S(1)}, u32[]{:S(2)}, u32[]{:S(2)}) async-start(s32[32,12,16,128]{3,2,1,0:T(8,128)} %bitcast.57), calls=%async_computation.2 | async-start | bytes 6291456 | tf_op jit(solution)/shard_map/all_to_all | solution.py:587
  56.5 14.9 %collective-permute-start.8 = (s32[896,128]{1,0:T(8,128)}, s32[896,128]{1,0:T(8,128)S(1)}, u32[]{:S(2)}, u32[]{:S(2)}) collective-permute-start(s32[896,128]{1,0:T(8,128)} %bitcast.80), channel_id=1, source_target_pairs={{0,8},{8,16},{16,24},{24,32},{32,40},{40,48},{48,56},{56,0},{1,9},... | collective-permute-start | bytes 1376264 | tf_op jit(solution)/shard_map/ppermute | solution.py:592
  58.4 30.4 %collective-permute-start.10 = (s32[1408,128]{1,0:T(8,128)}, s32[1408,128]{1,0:T(8,128)S(1)}, u32[]{:S(2)}, u32[]{:S(2)}) collective-permute-start(s32[1408,128]{1,0:T(8,128)} %bitcast.76), channel_id=1, source_target_pairs={{0,8},{8,16},{16,24},{24,32},{32,40},{40,48},{48,56},{56,0},{1,9},... | collective-permute-start | bytes 2162696 | tf_op jit(solution)/shard_map/ppermute | solution.py:592
  59.7 29.3 %collective-permute-start.16 = (s32[1408,128]{1,0:T(8,128)}, s32[1408,128]{1,0:T(8,128)S(1)}, u32[]{:S(2)}, u32[]{:S(2)}) collective-permute-start(s32[1408,128]{1,0:T(8,128)} %bitcast.75), channel_id=1, source_target_pairs={{0,56},{8,0},{16,8},{24,16},{32,24},{40,32},{48,40},{56,48},{1,57}... | collective-permute-start | bytes 2162696 | tf_op jit(solution)/shard_map/ppermute | solution.py:592
  61.7 27.1 %collective-permute-start.14 = (s32[896,128]{1,0:T(8,128)}, s32[896,128]{1,0:T(8,128)S(1)}, u32[]{:S(2)}, u32[]{:S(2)}) collective-permute-start(s32[896,128]{1,0:T(8,128)} %bitcast.79), channel_id=1, source_target_pairs={{0,56},{8,0},{16,8},{24,16},{32,24},{40,32},{48,40},{56,48},{1,57}... | collective-permute-start | bytes 1376264 | tf_op jit(solution)/shard_map/ppermute | solution.py:592
  61.9 37.6 %collective-permute-start.12 = (s32[1152,128]{1,0:T(8,128)}, s32[1152,128]{1,0:T(8,128)S(1)}, u32[]{:S(2)}, u32[]{:S(2)}) collective-permute-start(s32[1152,128]{1,0:T(8,128)} %bitcast.78), channel_id=1, source_target_pairs={{0,8},{8,16},{16,24},{24,32},{32,40},{40,48},{48,56},{56,0},{1,9},... | collective-permute-start | bytes 1769480 | tf_op jit(solution)/shard_map/ppermute | solution.py:592
  71.4 29.9 %collective-permute-start.18 = (s32[1152,128]{1,0:T(8,128)}, s32[1152,128]{1,0:T(8,128)S(1)}, u32[]{:S(2)}, u32[]{:S(2)}) collective-permute-start(s32[1152,128]{1,0:T(8,128)} %bitcast.77), channel_id=1, source_target_pairs={{0,56},{8,0},{16,8},{24,16},{32,24},{40,32},{48,40},{56,48},{1,57}... | collective-permute-start | bytes 1769480 | tf_op jit(solution)/shard_map/ppermute | solution.py:592
  88.7 20.7 %collective-permute-start.9 = (s32[896,128]{1,0:T(8,128)S(1)}, s32[896,128]{1,0:T(8,128)}, u32[]{:S(2)}, u32[]{:S(2)}) collective-permute-start(s32[896,128]{1,0:T(8,128)S(1)} %collective-permute-done.8), channel_id=1, source_target_pairs={{0,8},{8,16},{16,24},{24,32},{32,40},{40,48},{48,56},{56,0},{1,9},... | collective-permute-start | bytes 1376264 | tf_op jit(solution)/shard_map/ppermute | solution.py:592
  88.8 49.2 %collective-permute-start.11 = (s32[1408,128]{1,0:T(8,128)S(1)}, s32[1408,128]{1,0:T(8,128)}, u32[]{:S(2)}, u32[]{:S(2)}) collective-permute-start(s32[1408,128]{1,0:T(8,128)S(1)} %collective-permute-done.10), channel_id=1, source_target_pairs={{0,8},{8,16},{16,24},{24,32},{32,40},{40,48},{48,56},{56,0},{1,9},... | collective-permute-start | bytes 2162696 | tf_op jit(solution)/shard_map/ppermute | solution.py:592
  89.0 49.0 %collective-permute-start.17 = (s32[1408,128]{1,0:T(8,128)S(1)}, s32[1408,128]{1,0:T(8,128)}, u32[]{:S(2)}, u32[]{:S(2)}) collective-permute-start(s32[1408,128]{1,0:T(8,128)S(1)} %collective-permute-done.16), channel_id=1, source_target_pairs={{0,56},{8,0},{16,8},{24,16},{32,24},{40,32},{48,40},{56,48},{1,57}... | collective-permute-start | bytes 2162696 | tf_op jit(solution)/shard_map/ppermute | solution.py:592
  99.5 38.5 %collective-permute-start.13 = (s32[1152,128]{1,0:T(8,128)S(1)}, s32[1152,128]{1,0:T(8,128)}, u32[]{:S(2)}, u32[]{:S(2)}) collective-permute-start(s32[1152,128]{1,0:T(8,128)S(1)} %collective-permute-done.12), channel_id=1, source_target_pairs={{0,8},{8,16},{16,24},{24,32},{32,40},{40,48},{48,56},{56,0},{1,9},... | collective-permute-start | bytes 1769480 | tf_op jit(solution)/shard_map/ppermute | solution.py:592
  101.4 36.6 %collective-permute-start.19 = (s32[1152,128]{1,0:T(8,128)S(1)}, s32[1152,128]{1,0:T(8,128)}, u32[]{:S(2)}, u32[]{:S(2)}) collective-permute-start(s32[1152,128]{1,0:T(8,128)S(1)} %collective-permute-done.18), channel_id=1, source_target_pairs={{0,56},{8,0},{16,8},{24,16},{32,24},{40,32},{48,40},{56,48},{1,57}... | collective-permute-start | bytes 1769480 | tf_op jit(solution)/shard_map/ppermute | solution.py:592
  109.5 28.5 %collective-permute-start.15 = (s32[896,128]{1,0:T(8,128)S(1)}, s32[896,128]{1,0:T(8,128)}, u32[]{:S(2)}, u32[]{:S(2)}) collective-permute-start(s32[896,128]{1,0:T(8,128)S(1)} %collective-permute-done.14), channel_id=1, source_target_pairs={{0,56},{8,0},{16,8},{24,16},{32,24},{40,32},{48,40},{56,48},{1,57}... | collective-permute-start | bytes 1376264 | tf_op jit(solution)/shard_map/ppermute | solution.py:592
  142.3 50.1 %all-to-all-start.3 = ((s32[32,8,16,128]{3,2,1,0:T(8,128)}), s32[32,8,16,128]{3,2,1,0:T(8,128)}, u32[]{:S(2)}, u32[]{:S(2)}) async-start(s32[32,8,16,128]{3,2,1,0:T(8,128)} %bitcast.59), calls=%async_computation.3 | async-start | bytes 4194304 | tf_op jit(solution)/shard_map/all_to_all | solution.py:587
  149.7 15.0 %collective-permute-start.22 = (s32[896,128]{1,0:T(8,128)}, s32[896,128]{1,0:T(8,128)}, u32[]{:S(2)}, u32[]{:S(2)}) collective-permute-start(s32[896,128]{1,0:T(8,128)} %collective-permute-done.9.rest_0_), channel_id=1, source_target_pairs={{0,8},{8,16},{16,24},{24,32},{32,40},{40,48},{48,56},{56,0},{1,9},... | collective-permute-start | bytes 1376264 | tf_op jit(solution)/shard_map/ppermute | solution.py:592
  150.2 14.6 %collective-permute-start.24 = (s32[896,128]{1,0:T(8,128)}, s32[896,128]{1,0:T(8,128)}, u32[]{:S(2)}, u32[]{:S(2)}) collective-permute-start(s32[896,128]{1,0:T(8,128)} %collective-permute-done.15.rest_3_), channel_id=1, source_target_pairs={{0,56},{8,0},{16,8},{24,16},{32,24},{40,32},{48,40},{56,48},{1,57}... | collective-permute-start | bytes 1376264 | tf_op jit(solution)/shard_map/ppermute | solution.py:592
  153.1 27.1 %collective-permute-start.23 = (s32[1408,128]{1,0:T(8,128)}, s32[1408,128]{1,0:T(8,128)}, u32[]{:S(2)}, u32[]{:S(2)}) collective-permute-start(s32[1408,128]{1,0:T(8,128)} %collective-permute-done.11.rest_1_), channel_id=1, source_target_pairs={{0,8},{8,16},{16,24},{24,32},{32,40},{40,48},{48,56},{56,0},{1,9},... | collective-permute-start | bytes 2162696 | tf_op jit(solution)/shard_map/ppermute | solution.py:592
  153.1 27.1 %collective-permute-start.25 = (s32[1408,128]{1,0:T(8,128)}, s32[1408,128]{1,0:T(8,128)}, u32[]{:S(2)}, u32[]{:S(2)}) collective-permute-start(s32[1408,128]{1,0:T(8,128)} %collective-permute-done.17.rest_4_), channel_id=1, source_target_pairs={{0,56},{8,0},{16,8},{24,16},{32,24},{40,32},{48,40},{56,48},{1,57}... | collective-permute-start | bytes 2162696 | tf_op jit(solution)/shard_map/ppermute | solution.py:592
  164.7 24.7 %collective-permute-start.26 = (s32[896,128]{1,0:T(8,128)}, s32[896,128]{1,0:T(8,128)}, u32[]{:S(2)}, u32[]{:S(2)}) collective-permute-start(s32[896,128]{1,0:T(8,128)} %collective-permute-done.22.rest_0_), channel_id=1, source_target_pairs={{0,8},{8,16},{16,24},{24,32},{32,40},{40,48},{48,56},{56,0},{1,9},... | collective-permute-start | bytes 1376264 | tf_op jit(solution)/shard_map/ppermute | solution.py:592
  164.7 24.7 %collective-permute-start.27 = (s32[896,128]{1,0:T(8,128)}, s32[896,128]{1,0:T(8,128)}, u32[]{:S(2)}, u32[]{:S(2)}) collective-permute-start(s32[896,128]{1,0:T(8,128)} %collective-permute-done.24.rest_2_), channel_id=1, source_target_pairs={{0,56},{8,0},{16,8},{24,16},{32,24},{40,32},{48,40},{56,48},{1,57}... | collective-permute-start | bytes 1376264 | tf_op jit(solution)/shard_map/ppermute | solution.py:592
  192.4 109.3 %all-to-all-start.4 = ((s32[32,12,16,128]{3,2,1,0:T(8,128)}), s32[32,12,16,128]{3,2,1,0:T(8,128)S(1)}, u32[]{:S(2)}, u32[]{:S(2)}) async-start(s32[32,12,16,128]{3,2,1,0:T(8,128)} %bitcast.56), calls=%async_computation.4 | async-start | bytes 6291456 | tf_op jit(solution)/shard_map/all_to_all | solution.py:587
  203.1 1.3 collective-permute-start
  204.3 33.2 %collective-permute-start.1 = (s32[4096]{0:T(1024)S(1)}, s32[4096]{0:T(1024)S(1)}, u32[]{:S(2)}, u32[]{:S(2)}) collective-permute-start(s32[4096]{0:T(1024)S(1)} %add.134), channel_id=1, source_target_pairs={{0,2},{2,4},{4,6},{6,0},{1,3},{3,5},{5,7},{7,1},{8,10},{10,12},{12... | collective-permute-start | bytes 49160 | tf_op jit(solution)/shard_map/ppermute | solution.py:592
  237.5 5.2 %collective-permute-start.2 = (s32[4096]{0:T(1024)S(1)}, s32[4096]{0:T(1024)S(1)}, u32[]{:S(2)}, u32[]{:S(2)}) collective-permute-start(s32[4096]{0:T(1024)S(1)} %add.135), channel_id=1, source_target_pairs={{0,4},{2,6},{4,0},{6,2},{1,5},{3,7},{5,1},{7,3},{8,12},{10,14},{12... | collective-permute-start | bytes 49160 | tf_op jit(solution)/shard_map/ppermute | solution.py:592
  242.8 3.7 %collective-permute-start.3 = (s32[4096]{0:T(1024)S(1)}, s32[4096]{0:T(1024)S(1)}, u32[]{:S(2)}, u32[]{:S(2)}) collective-permute-start(s32[4096]{0:T(1024)S(1)} %add.136), channel_id=1, source_target_pairs={{0,64},{64,128},{128,192},{192,0},{1,65},{65,129},{129,193},{193,1... | collective-permute-start | bytes 49160 | tf_op jit(solution)/shard_map/ppermute | solution.py:592
  246.5 5.2 %collective-permute-start.4 = (s32[4096]{0:T(1024)S(1)}, s32[4096]{0:T(1024)S(1)}, u32[]{:S(2)}, u32[]{:S(2)}) collective-permute-start(s32[4096]{0:T(1024)S(1)} %add.137), channel_id=1, source_target_pairs={{0,128},{64,192},{128,0},{192,64},{1,129},{65,193},{129,1},{193,65... | collective-permute-start | bytes 49160 | tf_op jit(solution)/shard_map/ppermute | solution.py:592
  251.8 4.9 %collective-permute-start.5 = (s32[4096]{0:T(1024)S(1)}, s32[4096]{0:T(1024)S(1)}, u32[]{:S(2)}, u32[]{:S(2)}) collective-permute-start(s32[4096]{0:T(1024)S(1)} %add.138), channel_id=1, source_target_pairs={{0,8},{8,16},{16,24},{24,32},{32,40},{40,48},{48,56},{56,0},{1,9},... | collective-permute-start | bytes 49160 | tf_op jit(solution)/shard_map/ppermute | solution.py:592
  256.7 5.9 %collective-permute-start.6 = (s32[4096]{0:T(1024)S(1)}, s32[4096]{0:T(1024)S(1)}, u32[]{:S(2)}, u32[]{:S(2)}) collective-permute-start(s32[4096]{0:T(1024)S(1)} %add.139), channel_id=1, source_target_pairs={{0,16},{8,24},{16,32},{24,40},{32,48},{40,56},{48,0},{56,8},{1,17}... | collective-permute-start | bytes 49160 | tf_op jit(solution)/shard_map/ppermute | solution.py:592
  262.6 19.3 %collective-permute-start.7 = (s32[4096]{0:T(1024)S(1)}, s32[4096]{0:T(1024)S(1)}, u32[]{:S(2)}, u32[]{:S(2)}) collective-permute-start(s32[4096]{0:T(1024)S(1)} %add.140), channel_id=1, source_target_pairs={{0,32},{8,40},{16,48},{24,56},{32,0},{40,8},{48,16},{56,24},{1,33}... | collective-permute-start | bytes 49160 | tf_op jit(solution)/shard_map/ppermute | solution.py:592
  (8 other events, 105.4 us)

commit v5 on v4

--- a/solution.py
+++ b/solution.py
@@ -489,14 +489,21 @@
     )(place, counts, befores, early, last)
 
 
-def plan_relay(keys, dest, cut, z):
+def plan_relay(keys, dest, cut, z, tokens):
     examples = keys.shape[1]
     padded = -(-PLACES // LANES) * LANES
+    tiles = tokens.shape[1] // LANES
+    tiled = tokens.reshape(examples // 8, 8, tiles, LANES).transpose(0, 2, 1, 3)[..., None, :]
 
     def across(left, right):
         return lax.dot_general(left, right, (((1,), (1,)), ((), ())), preferred_element_type=jnp.float32)
 
-    def kernel(keys_ref, dest_ref, cut_ref, z_ref, plan_ref, rank_ref, counts_ref):
+    def kernel(
+        keys_ref, dest_ref, cut_ref, z_ref, tok_ref, plan_ref, rank_ref, counts_ref, up_ref, down_ref,
+        buf, source, sem_in, sem_plan, sem_out,
+    ):
+        load = pltpu.make_async_copy(tok_ref, buf, sem_in)
+        load.start()
         kept = (keys_ref[...] >> KEY_SHIFT) >= cut_ref[0]
         owner = lax.broadcasted_iota(jnp.int32, (32, examples), 0)
         hot = (dest_ref[...] == owner) & kept
@@ -549,19 +556,40 @@
         parts = jnp.where(part == 0, example >> 4, jnp.where(part == 1, example & 15, 0))
         found = across(parts.astype(jnp.float32).astype(jnp.bfloat16), here).astype(jnp.int32)
         plan_ref[...] = found[0:1, :] * 16 + found[1:2, :]
+        load.wait()
+        move = pltpu.make_async_copy(plan_ref, source, sem_plan)
+        move.start()
+        move.wait()
+        for out, start in ((up_ref, 0), (down_ref, NEAR)):
+
+            def some(i, carry, out=out, start=start):
+                for j in range(8):
+                    row = source[0, start + i * 8 + j]
+                    pltpu.make_async_copy(slot_of(buf, row), out.at[i * 8 + j], sem_out).start()
+                return carry
+
+            lax.fori_loop(0, NEAR // 8, some, 0)
+        for out in (up_ref, down_ref):
+            pltpu.make_async_copy(out, out, sem_out).wait()
 
     whole = pl.BlockSpec(memory_space=VMEM)
     return pl.pallas_call(
         kernel,
-        in_specs=[whole, whole, smem_spec(), smem_spec()],
-        out_specs=[whole] * 3,
+        in_specs=[whole, whole, smem_spec(), smem_spec(), any_spec()],
+        out_specs=[whole] * 3 + [any_spec()] * 2,
         out_shape=[
             jax.ShapeDtypeStruct((1, padded), jnp.int32),
             jax.ShapeDtypeStruct((1, examples), jnp.int32),
             jax.ShapeDtypeStruct((1, 32), jnp.int32),
+            *[jax.ShapeDtypeStruct((NEAR, tiles, 1, LANES), tokens.dtype)] * 2,
+        ],
+        scratch_shapes=[
+            pltpu.VMEM(tiled.shape, tokens.dtype),
+            pltpu.SMEM((1, padded), jnp.int32),
+            *[pltpu.SemaphoreType.DMA] * 3,
         ],
         name="plan_relay",
-    )(keys, dest, cut, z)
+    )(keys, dest, cut, z, tiled)
 
 
 def by_owner(values, position, size):
@@ -613,9 +641,11 @@
     bins_of = keys >> KEY_SHIFT
     dest = owner[:, 0]
     kept = bins_of >= cut[0]
-    source, local_rank, counts = plan_relay(keys[None, :], owner.reshape(1, -1), cut, z[None].astype(jnp.int32))
+    source, local_rank, counts, *near = plan_relay(
+        keys[None, :], owner.reshape(1, -1), cut, z[None].astype(jnp.int32), tokens
+    )
+    near = [rows.reshape(-1, LANES) for rows in near]
     local_rank, counts = local_rank[0], counts[0]
-    near = pack_relay(source, tokens, 0, [NEAR] * 2)
     *far, own = pack_relay(source, tokens, 2 * NEAR, [n for _, n in segments(1)] * 2 + [OWN])
     plus, minus = far[:3], far[3:]
 

time: 307 us -> 307 us (level)
  waiting for transfers between devices: 157 us -> 149 us
  starting transfers between devices: 70 us -> 77.1 us
    ppermute x28, starting transfers between devices: 37.2 us -> 42.5 us  [hop_on(): lax.ppermute(value, axis, [(i, (i + step) % count) for i in range(count)])]
    pallas_call x2 -> x1, Pallas kernels: 10 us -> 5.58 us  [pack_relay(): pl.pallas_call(kernel, in_specs=[smem_spec(), any_spec()], out_specs=[any...]
    all_to_all x4, waiting for transfers between devices: 9.52 us -> 5.11 us  [exchange(): return lax.all_to_all(value, axes, split_axis=0, concat_axis=0, tiled=True)]
    ppermute x28, waiting for transfers between devices: 147 us -> 143 us  [hop_on(): lax.ppermute(value, axis, [(i, (i + step) % count) for i in range(count)])]
    pallas_call x1, Pallas kernels: 2 us -> 5.61 us  [plan_relay(): pl.pallas_call(kernel, in_specs=[whole, whole, smem_spec(), smem_spec(),...]
  transfers between devices with their start and end apart: 32 -> 32, of which waited for: 17 -> 17; matrix products, arithmetic and copies ran while one was open for 6% -> 7% of each run, Pallas kernels for 13% -> 13%
where the time goes in v5:
time: 307 us; the launch traced here: 306 us
  waiting for transfers between devices  149 us (49%)
  starting transfers between devices  77.1 us (25%)
  Pallas kernels  53 us (17%)
  local copies, waits for them, and re-layouts  12.1 us (4%)
  other arithmetic  9.76 us (3%)
  between operations  4.98 us (2%)
    ppermute x28, waiting for transfers between devices, hop_on(): lax.ppermute(value, axis, [(i, (i + step) % count) for i in range(count)])  143 us
    ppermute x28, starting transfers between devices, hop_on(): lax.ppermute(value, axis, [(i, (i + step) % count) for i in range(count)])  42.5 us
    all_to_all x4, starting transfers between devices, exchange(): return lax.all_to_all(value, axes, split_axis=0, concat_axis=0, tiled=True)  34.6 us
    pallas_call x4, Pallas kernels, spread(): pl.pallas_call(kernel, in_specs=[smem_spec()] * 3 + [any_spec()] * (len(b...  15.6 us
    pallas_call x1, Pallas kernels, place_bins(): pl.pallas_call(kernel, in_specs=[smem_spec()] * 3, out_specs=smem_spec(),...  11.3 us
    pallas_call x1, Pallas kernels, unpack_early(): pl.pallas_call(kernel, in_specs=[smem_spec()] * 3 + [any_spec()] * len(go...  10.4 us
    gather x1, local copies, waits for them, and re-layouts, program(): suffix[jnp.maximum(slot_bins, 0)] / total  6.14 us
  transfers between devices with their start and end apart: 32, of which 17 were waited for; matrix products, arithmetic and copies ran while one was open for 7% of the time, Pallas kernels for 13%

profile of v5, /device:TPU:22, one launch (start us, length us, event | category | flops | bytes accessed | tf_op | source)
XLA Modules:
  0.0 305.7 jit_solution(15428734863438342850)
XLA Ops:
  1.3 5.6 %plan_relay.1 = (s32[1,896]{1,0:T(1,128)}, s32[1,512]{1,0:T(1,128)}, s32[1,32]{1,0:T(1,128)}, s32[112,16,1,128]{3,2,1,0:T(1,128)}, s32[112,16,1,128]{3,2,1,0:T(1,128)}) custom-call(s32[1,512]{1,0:T(1,128)} %bitcast.65, s32[1,512]{1,0:T(1,128)} %bitcast.66, s32[1]{0:T(128)} %copy.21.cut_ref, s32[1]{0:T(128)} %bitcast.5.z_ref, s32[64,16,8,1,128]{4,3,2,1,0:T(1,128)} %bitcast.53), custom_call_target="tpu_custom_call" | custom-call | tf_op jit(solution)/shard_map/plan_relay/pallas_call | solution.py:576
  8.9 4.0 %collective-permute-start.21 = (s32[1792,128]{1,0:T(8,128)}, s32[1792,128]{1,0:T(8,128)S(1)}, u32[]{:S(2)}, u32[]{:S(2)}) collective-permute-start(s32[1792,128]{1,0:T(8,128)} %bitcast.73), channel_id=1, source_target_pairs={{0,56},{8,0},{16,8},{24,16},{32,24},{40,32},{48,40},{56,48},{1,57}... | collective-permute-start | bytes 2752520 | tf_op jit(solution)/shard_map/ppermute | solution.py:620
  15.5 11.7 %all-to-all-start.1 = ((s32[256,1,64]{2,1,0:T(1,128)}), s32[256,1,64]{2,1,0:T(1,128)S(1)}, u32[]{:S(2)}, u32[]{:S(2)}) async-start(s32[256,1,64]{2,1,0:T(1,128)} %bitcast.14), calls=%async_computation.1 | async-start | bytes 262144 | tf_op jit(solution)/shard_map/all_to_all | solution.py:615
  27.8 5.6 %shard_map.67 = (s32[56,16,1,128]{3,2,1,0:T(1,128)}, s32[88,16,1,128]{3,2,1,0:T(1,128)}, s32[72,16,1,128]{3,2,1,0:T(1,128)}, s32[56,16,1,128]{3,2,1,0:T(1,128)},...) custom-call(s32[1,896]{1,0:T(1,128)} %get-tuple-element.68.source_ref, ...), custom_call_target="tpu_custom_call" | custom-call | tf_op jit(solution)/shard_map/pallas_call | solution.py:257
  33.4 5.1 %all-to-all-done.1 = s32[256,1,64]{2,1,0:T(1,128)S(1)} async-done(((s32[256,1,64]{2,1,0:T(1,128)}), s32[256,1,64]{2,1,0:T(1,128)S(1)}, u32[]{:S(2)}, u32[]{:S(2)}) %all-to-all-start.1) | async-done | bytes 65568 | tf_op jit(solution)/shard_map/all_to_all | solution.py:615
  41.9 4.5 %shard_map.69 = s32[6144,128]{1,0:T(8,128)} custom-call(s32[2]{0:T(128)} %pad_add_fusion.2.place_ref, s32[256]{0:T(256)} %reshape.168.counts_ref, s32[256]{0:T(256)} %reshape.170.befores_ref, s32[2048,128]{1,0:T(8,128)} %bitcast.62, s32[1792,128]{1,0:T(8,128)} %copy-done.1, s32[1792,128]{1,0:T(8,128)} %copy-done.2), custom_call_target="tpu_custom_call" | custom-call | tf_op jit(solution)/shard_map/pallas_call | solution.py:354
  46.4 8.1 %all-to-all-start.2 = ((s32[32,12,16,128]{3,2,1,0:T(8,128)}), s32[32,12,16,128]{3,2,1,0:T(8,128)S(1)}, u32[]{:S(2)}, u32[]{:S(2)}) async-start(s32[32,12,16,128]{3,2,1,0:T(8,128)} %bitcast.57), calls=%async_computation.2 | async-start | bytes 6291456 | tf_op jit(solution)/shard_map/all_to_all | solution.py:615
  54.5 3.4 %collective-permute-start.8 = (s32[896,128]{1,0:T(8,128)}, s32[896,128]{1,0:T(8,128)S(1)}, u32[]{:S(2)}, u32[]{:S(2)}) collective-permute-start(s32[896,128]{1,0:T(8,128)} %bitcast.80), channel_id=1, source_target_pairs={{0,8},{8,16},{16,24},{24,32},{32,40},{40,48},{48,56},{56,0},{1,9},... | collective-permute-start | bytes 1376264 | tf_op jit(solution)/shard_map/ppermute | solution.py:620
  63.2 6.2 %collective-permute-done.8 = s32[896,128]{1,0:T(8,128)S(1)} collective-permute-done((s32[896,128]{1,0:T(8,128)}, s32[896,128]{1,0:T(8,128)S(1)}, u32[]{:S(2)}, u32[]{:S(2)}) %collective-permute-start.8) | collective-permute-done | bytes 458784 | tf_op jit(solution)/shard_map/ppermute | solution.py:620
  69.9 17.9 %collective-permute-done.14 = s32[896,128]{1,0:T(8,128)S(1)} collective-permute-done((s32[896,128]{1,0:T(8,128)}, s32[896,128]{1,0:T(8,128)S(1)}, u32[]{:S(2)}, u32[]{:S(2)}) %collective-permute-start.14) | collective-permute-done | bytes 458784 | tf_op jit(solution)/shard_map/ppermute | solution.py:620
  91.5 6.0 %collective-permute-done.12 = s32[1152,128]{1,0:T(8,128)S(1)} collective-permute-done((s32[1152,128]{1,0:T(8,128)}, s32[1152,128]{1,0:T(8,128)S(1)}, u32[]{:S(2)}, u32[]{:S(2)}) %collective-permute-start.12) | collective-permute-done | bytes 589856 | tf_op jit(solution)/shard_map/ppermute | solution.py:620
  100.5 3.6 %collective-permute-start.19 = (s32[1152,128]{1,0:T(8,128)S(1)}, s32[1152,128]{1,0:T(8,128)}, u32[]{:S(2)}, u32[]{:S(2)}) collective-permute-start(s32[1152,128]{1,0:T(8,128)S(1)} %collective-permute-done.18), channel_id=1, source_target_pairs={{0,56},{8,0},{16,8},{24,16},{32,24},{40,32},{48,40},{56,48},{1,57}... | collective-permute-start | bytes 1769480 | tf_op jit(solution)/shard_map/ppermute | solution.py:620
  104.0 3.4 %collective-permute-done.9.rest_0_ = s32[896,128]{1,0:T(8,128)} collective-permute-done((s32[896,128]{1,0:T(8,128)S(1)}, s32[896,128]{1,0:T(8,128)}, u32[]{:S(2)}, u32[]{:S(2)}) %collective-permute-start.9) | collective-permute-done | bytes 458784 | tf_op jit(solution)/shard_map/ppermute | solution.py:620
  108.0 28.9 %collective-permute-done.15.rest_3_ = s32[896,128]{1,0:T(8,128)} collective-permute-done((s32[896,128]{1,0:T(8,128)S(1)}, s32[896,128]{1,0:T(8,128)}, u32[]{:S(2)}, u32[]{:S(2)}) %collective-permute-start.15) | collective-permute-done | bytes 458784 | tf_op jit(solution)/shard_map/ppermute | solution.py:620
  136.9 4.2 %shard_map.68 = s32[4096,128]{1,0:T(8,128)} custom-call(s32[2]{0:T(128)} %pad_add_fusion.2.place_ref, s32[256]{0:T(256)} %reshape.168.counts_ref, s32[256]{0:T(256)} %reshape.170.befores_ref, s32[896,128]{1,0:T(8,128)} %collective-permute-done.9.rest_0_, s32[1408,128]{1,0:T(8,128)} %collective-permute-done.11.rest_1_, ...), custom_call_target="tpu_custom_call" | custom-call | tf_op jit(solution)/shard_map/pallas_call | solution.py:354
  141.2 7.4 %all-to-all-start.3 = ((s32[32,8,16,128]{3,2,1,0:T(8,128)}), s32[32,8,16,128]{3,2,1,0:T(8,128)}, u32[]{:S(2)}, u32[]{:S(2)}) async-start(s32[32,8,16,128]{3,2,1,0:T(8,128)} %bitcast.59), calls=%async_computation.3 | async-start | bytes 4194304 | tf_op jit(solution)/shard_map/all_to_all | solution.py:615
  149.3 3.3 %collective-permute-start.24 = (s32[896,128]{1,0:T(8,128)}, s32[896,128]{1,0:T(8,128)}, u32[]{:S(2)}, u32[]{:S(2)}) collective-permute-start(s32[896,128]{1,0:T(8,128)} %collective-permute-done.15.rest_3_), channel_id=1, source_target_pairs={{0,56},{8,0},{16,8},{24,16},{32,24},{40,32},{48,40},{56,48},{1,57}... | collective-permute-start | bytes 1376264 | tf_op jit(solution)/shard_map/ppermute | solution.py:620
  155.8 8.4 %collective-permute-done.22.rest_0_ = s32[896,128]{1,0:T(8,128)} collective-permute-done((s32[896,128]{1,0:T(8,128)}, s32[896,128]{1,0:T(8,128)}, u32[]{:S(2)}, u32[]{:S(2)}) %collective-permute-start.22) | collective-permute-done | bytes 458784 | tf_op jit(solution)/shard_map/ppermute | solution.py:620
  164.2 3.3 %collective-permute-start.27 = (s32[896,128]{1,0:T(8,128)}, s32[896,128]{1,0:T(8,128)}, u32[]{:S(2)}, u32[]{:S(2)}) collective-permute-start(s32[896,128]{1,0:T(8,128)} %collective-permute-done.24.rest_2_), channel_id=1, source_target_pairs={{0,56},{8,0},{16,8},{24,16},{32,24},{40,32},{48,40},{56,48},{1,57}... | collective-permute-start | bytes 1376264 | tf_op jit(solution)/shard_map/ppermute | solution.py:620
  167.5 12.1 %collective-permute-done.23.rest_1_ = s32[1408,128]{1,0:T(8,128)} collective-permute-done((s32[1408,128]{1,0:T(8,128)}, s32[1408,128]{1,0:T(8,128)}, u32[]{:S(2)}, u32[]{:S(2)}) %collective-permute-start.23) | collective-permute-done | bytes 720928 | tf_op jit(solution)/shard_map/ppermute | solution.py:620
  179.6 3.9 %shard_map.70.rest_0_ = s32[6144,128]{1,0:T(8,128)} custom-call(s32[2]{0:T(128)} %pad_add_fusion.2.place_ref, s32[256]{0:T(256)} %reshape.168.counts_ref, s32[256]{0:T(256)} %reshape.170.befores_ref, s32[896,128]{1,0:T(8,128)} %collective-permute-done.22.rest_0_, s32[1408,128]{1,0:T(8,128)} %collective-permute-done.23.rest_1_, ...), custom_call_target="tpu_custom_call" | custom-call | tf_op jit(solution)/shard_map/pallas_call | solution.py:354
  183.6 5.3 %collective-permute-done.26.rest_1_ = s32[896,128]{1,0:T(8,128)} collective-permute-done((s32[896,128]{1,0:T(8,128)}, s32[896,128]{1,0:T(8,128)}, u32[]{:S(2)}, u32[]{:S(2)}) %collective-permute-start.26) | collective-permute-done | bytes 458784 | tf_op jit(solution)/shard_map/ppermute | solution.py:620
  191.9 7.4 %all-to-all-start.4 = ((s32[32,12,16,128]{3,2,1,0:T(8,128)}), s32[32,12,16,128]{3,2,1,0:T(8,128)S(1)}, u32[]{:S(2)}, u32[]{:S(2)}) async-start(s32[32,12,16,128]{3,2,1,0:T(8,128)} %bitcast.56), calls=%async_computation.4 | async-start | bytes 6291456 | tf_op jit(solution)/shard_map/all_to_all | solution.py:615
  199.3 3.3 %scatter_custom_fusion = s32[4096]{0:T(1024)S(1)} fusion(s32[512]{0:T(512)S(1)} %get-tuple-element.115, s32[512]{0:T(512)S(1)} %broadcast.95, s32[]{:T(128)} %constant.96.clone.1), kind=kCustom, calls=%fused_computation.35 | custom fusion | flops 512 | bytes 16388 | tf_op jit(solution)/shard_map/scatter-add | solution.py:652
  204.4 32.7 %collective-permute-done.1 = s32[4096]{0:T(1024)S(1)} collective-permute-done((s32[4096]{0:T(1024)S(1)}, s32[4096]{0:T(1024)S(1)}, u32[]{:S(2)}, u32[]{:S(2)}) %collective-permute-start.1) | collective-permute-done | bytes 16416 | tf_op jit(solution)/shard_map/ppermute | solution.py:620
  237.6 4.7 %collective-permute-done.2 = s32[4096]{0:T(1024)S(1)} collective-permute-done((s32[4096]{0:T(1024)S(1)}, s32[4096]{0:T(1024)S(1)}, u32[]{:S(2)}, u32[]{:S(2)}) %collective-permute-start.2) | collective-permute-done | bytes 16416 | tf_op jit(solution)/shard_map/ppermute | solution.py:620
  251.3 4.9 %collective-permute-done.5 = s32[4096]{0:T(1024)S(1)} collective-permute-done((s32[4096]{0:T(1024)S(1)}, s32[4096]{0:T(1024)S(1)}, u32[]{:S(2)}, u32[]{:S(2)}) %collective-permute-start.5) | collective-permute-done | bytes 16416 | tf_op jit(solution)/shard_map/ppermute | solution.py:620
  256.3 5.8 %collective-permute-done.6 = s32[4096]{0:T(1024)S(1)} collective-permute-done((s32[4096]{0:T(1024)S(1)}, s32[4096]{0:T(1024)S(1)}, u32[]{:S(2)}, u32[]{:S(2)}) %collective-permute-start.6) | collective-permute-done | bytes 16416 | tf_op jit(solution)/shard_map/ppermute | solution.py:620
  264.7 11.3 %place_bins.1 = s32[1024]{0:T(1024)} custom-call(s32[256]{0:T(256)S(1)} %dynamic-slice_reduce_fusion.counts_ref, s32[1]{0:T(128)} %bitcast.16.member_ref, s32[8192]{0:T(1024)} %reshape.188.keys_ref), custom_call_target="tpu_custom_call" | custom-call | tf_op jit(solution)/shard_map/place_bins/pallas_call | solution.py:144
  283.2 6.1 %gather_fusion = f32[1024]{0:T(1024)S(1)} fusion(f32[4096]{0:T(1024)S(1)} %rev.7, s32[1024]{0:T(1024)S(1)} %maximum_clamp_fusion), kind=kCustom, calls=%fused_computation | custom fusion | bytes 12288 | tf_op jit(solution)/shard_map/gather | solution.py:714
  290.6 10.4 %unpack_early.1.early_ref = s32[128,16,8,1,128]{4,3,2,1,0:T(1,128)} custom-call(s32[2]{0:T(128)} %pad_add_fusion.2.place_ref, s32[256]{0:T(256)S(1)} %dynamic-slice_reduce_fusion.counts_ref, s32[256]{0:T(256)} %bitcast.70, s32[384,16,1,128]{3,2,1,0:T(1,128)} %bitcast.58, s32[256,16,1,128]{3,2,1,0:T(1,128)} %bitcast.35.rest_1_), custom_call_target="tpu_custom_call" | custom-call | tf_op jit(solution)/shard_map/unpack_early/pallas_call | solution.py:446
  301.0 4.5 %unpack_last.1 = s32[128,16,8,1,128]{4,3,2,1,0:T(1,128)} custom-call(s32[2]{0:T(128)} %pad_add_fusion.2.place_ref, s32[256]{0:T(256)S(1)} %dynamic-slice_reduce_fusion.counts_ref, s32[256]{0:T(256)} %bitcast.71, s32[128,16,8,1,128]{4,3,2,1,0:T(1,128)} %unpack_early.1.early_ref, s32[384,16,1,128]{3,2,1,0:T(1,128)S(1)} %bitcast.51), custom_call_target="tpu_custom_call", output_to_operand_aliasing={{}: (3, {})} | custom-call | tf_op jit(solution)/shard_map/unpack_last/pallas_call | solution.py:481
  (95 shorter events, 47.6 us)
Async XLA Ops:
  6.9 33.7 %collective-permute-start.20 = (s32[1792,128]{1,0:T(8,128)}, s32[1792,128]{1,0:T(8,128)S(1)}, u32[]{:S(2)}, u32[]{:S(2)}) collective-permute-start(s32[1792,128]{1,0:T(8,128)} %bitcast.74), channel_id=1, source_target_pairs={{0,8},{8,16},{16,24},{24,32},{32,40},{40,48},{48,56},{56,0},{1,9},... | collective-permute-start | bytes 2752520 | tf_op jit(solution)/shard_map/ppermute | solution.py:620
  8.9 31.7 %collective-permute-start.21 = (s32[1792,128]{1,0:T(8,128)}, s32[1792,128]{1,0:T(8,128)S(1)}, u32[]{:S(2)}, u32[]{:S(2)}) collective-permute-start(s32[1792,128]{1,0:T(8,128)} %bitcast.73), channel_id=1, source_target_pairs={{0,56},{8,0},{16,8},{24,16},{32,24},{40,32},{48,40},{56,48},{1,57}... | collective-permute-start | bytes 2752520 | tf_op jit(solution)/shard_map/ppermute | solution.py:620
  15.5 23.0 %all-to-all-start.1 = ((s32[256,1,64]{2,1,0:T(1,128)}), s32[256,1,64]{2,1,0:T(1,128)S(1)}, u32[]{:S(2)}, u32[]{:S(2)}) async-start(s32[256,1,64]{2,1,0:T(1,128)} %bitcast.14), calls=%async_computation.1 | async-start | bytes 262144 | tf_op jit(solution)/shard_map/all_to_all | solution.py:615
  46.4 94.7 %all-to-all-start.2 = ((s32[32,12,16,128]{3,2,1,0:T(8,128)}), s32[32,12,16,128]{3,2,1,0:T(8,128)S(1)}, u32[]{:S(2)}, u32[]{:S(2)}) async-start(s32[32,12,16,128]{3,2,1,0:T(8,128)} %bitcast.57), calls=%async_computation.2 | async-start | bytes 6291456 | tf_op jit(solution)/shard_map/all_to_all | solution.py:615
  54.5 14.9 %collective-permute-start.8 = (s32[896,128]{1,0:T(8,128)}, s32[896,128]{1,0:T(8,128)S(1)}, u32[]{:S(2)}, u32[]{:S(2)}) collective-permute-start(s32[896,128]{1,0:T(8,128)} %bitcast.80), channel_id=1, source_target_pairs={{0,8},{8,16},{16,24},{24,32},{32,40},{40,48},{48,56},{56,0},{1,9},... | collective-permute-start | bytes 1376264 | tf_op jit(solution)/shard_map/ppermute | solution.py:620
  57.9 30.3 %collective-permute-start.10 = (s32[1408,128]{1,0:T(8,128)}, s32[1408,128]{1,0:T(8,128)S(1)}, u32[]{:S(2)}, u32[]{:S(2)}) collective-permute-start(s32[1408,128]{1,0:T(8,128)} %bitcast.76), channel_id=1, source_target_pairs={{0,8},{8,16},{16,24},{24,32},{32,40},{40,48},{48,56},{56,0},{1,9},... | collective-permute-start | bytes 2162696 | tf_op jit(solution)/shard_map/ppermute | solution.py:620
  58.2 30.1 %collective-permute-start.16 = (s32[1408,128]{1,0:T(8,128)}, s32[1408,128]{1,0:T(8,128)S(1)}, u32[]{:S(2)}, u32[]{:S(2)}) collective-permute-start(s32[1408,128]{1,0:T(8,128)} %bitcast.75), channel_id=1, source_target_pairs={{0,56},{8,0},{16,8},{24,16},{32,24},{40,32},{48,40},{56,48},{1,57}... | collective-permute-start | bytes 2162696 | tf_op jit(solution)/shard_map/ppermute | solution.py:620
  61.1 26.7 %collective-permute-start.14 = (s32[896,128]{1,0:T(8,128)}, s32[896,128]{1,0:T(8,128)S(1)}, u32[]{:S(2)}, u32[]{:S(2)}) collective-permute-start(s32[896,128]{1,0:T(8,128)} %bitcast.79), channel_id=1, source_target_pairs={{0,56},{8,0},{16,8},{24,16},{32,24},{40,32},{48,40},{56,48},{1,57}... | collective-permute-start | bytes 1376264 | tf_op jit(solution)/shard_map/ppermute | solution.py:620
  61.2 36.3 %collective-permute-start.12 = (s32[1152,128]{1,0:T(8,128)}, s32[1152,128]{1,0:T(8,128)S(1)}, u32[]{:S(2)}, u32[]{:S(2)}) collective-permute-start(s32[1152,128]{1,0:T(8,128)} %bitcast.78), channel_id=1, source_target_pairs={{0,8},{8,16},{16,24},{24,32},{32,40},{40,48},{48,56},{56,0},{1,9},... | collective-permute-start | bytes 1769480 | tf_op jit(solution)/shard_map/ppermute | solution.py:620
  69.4 31.0 %collective-permute-start.18 = (s32[1152,128]{1,0:T(8,128)}, s32[1152,128]{1,0:T(8,128)S(1)}, u32[]{:S(2)}, u32[]{:S(2)}) collective-permute-start(s32[1152,128]{1,0:T(8,128)} %bitcast.77), channel_id=1, source_target_pairs={{0,56},{8,0},{16,8},{24,16},{32,24},{40,32},{48,40},{56,48},{1,57}... | collective-permute-start | bytes 1769480 | tf_op jit(solution)/shard_map/ppermute | solution.py:620
  87.8 19.6 %collective-permute-start.9 = (s32[896,128]{1,0:T(8,128)S(1)}, s32[896,128]{1,0:T(8,128)}, u32[]{:S(2)}, u32[]{:S(2)}) collective-permute-start(s32[896,128]{1,0:T(8,128)S(1)} %collective-permute-done.8), channel_id=1, source_target_pairs={{0,8},{8,16},{16,24},{24,32},{32,40},{40,48},{48,56},{56,0},{1,9},... | collective-permute-start | bytes 1376264 | tf_op jit(solution)/shard_map/ppermute | solution.py:620
  88.2 48.7 %collective-permute-start.11 = (s32[1408,128]{1,0:T(8,128)S(1)}, s32[1408,128]{1,0:T(8,128)}, u32[]{:S(2)}, u32[]{:S(2)}) collective-permute-start(s32[1408,128]{1,0:T(8,128)S(1)} %collective-permute-done.10), channel_id=1, source_target_pairs={{0,8},{8,16},{16,24},{24,32},{32,40},{40,48},{48,56},{56,0},{1,9},... | collective-permute-start | bytes 2162696 | tf_op jit(solution)/shard_map/ppermute | solution.py:620
  88.3 48.5 %collective-permute-start.17 = (s32[1408,128]{1,0:T(8,128)S(1)}, s32[1408,128]{1,0:T(8,128)}, u32[]{:S(2)}, u32[]{:S(2)}) collective-permute-start(s32[1408,128]{1,0:T(8,128)S(1)} %collective-permute-done.16), channel_id=1, source_target_pairs={{0,56},{8,0},{16,8},{24,16},{32,24},{40,32},{48,40},{56,48},{1,57}... | collective-permute-start | bytes 2162696 | tf_op jit(solution)/shard_map/ppermute | solution.py:620
  97.5 39.4 %collective-permute-start.13 = (s32[1152,128]{1,0:T(8,128)S(1)}, s32[1152,128]{1,0:T(8,128)}, u32[]{:S(2)}, u32[]{:S(2)}) collective-permute-start(s32[1152,128]{1,0:T(8,128)S(1)} %collective-permute-done.12), channel_id=1, source_target_pairs={{0,8},{8,16},{16,24},{24,32},{32,40},{40,48},{48,56},{56,0},{1,9},... | collective-permute-start | bytes 1769480 | tf_op jit(solution)/shard_map/ppermute | solution.py:620
  100.5 36.4 %collective-permute-start.19 = (s32[1152,128]{1,0:T(8,128)S(1)}, s32[1152,128]{1,0:T(8,128)}, u32[]{:S(2)}, u32[]{:S(2)}) collective-permute-start(s32[1152,128]{1,0:T(8,128)S(1)} %collective-permute-done.18), channel_id=1, source_target_pairs={{0,56},{8,0},{16,8},{24,16},{32,24},{40,32},{48,40},{56,48},{1,57}... | collective-permute-start | bytes 1769480 | tf_op jit(solution)/shard_map/ppermute | solution.py:620
  107.4 29.4 %collective-permute-start.15 = (s32[896,128]{1,0:T(8,128)S(1)}, s32[896,128]{1,0:T(8,128)}, u32[]{:S(2)}, u32[]{:S(2)}) collective-permute-start(s32[896,128]{1,0:T(8,128)S(1)} %collective-permute-done.14), channel_id=1, source_target_pairs={{0,56},{8,0},{16,8},{24,16},{32,24},{40,32},{48,40},{56,48},{1,57}... | collective-permute-start | bytes 1376264 | tf_op jit(solution)/shard_map/ppermute | solution.py:620
  141.2 50.7 %all-to-all-start.3 = ((s32[32,8,16,128]{3,2,1,0:T(8,128)}), s32[32,8,16,128]{3,2,1,0:T(8,128)}, u32[]{:S(2)}, u32[]{:S(2)}) async-start(s32[32,8,16,128]{3,2,1,0:T(8,128)} %bitcast.59), calls=%async_computation.3 | async-start | bytes 4194304 | tf_op jit(solution)/shard_map/all_to_all | solution.py:615
  148.6 15.6 %collective-permute-start.22 = (s32[896,128]{1,0:T(8,128)}, s32[896,128]{1,0:T(8,128)}, u32[]{:S(2)}, u32[]{:S(2)}) collective-permute-start(s32[896,128]{1,0:T(8,128)} %collective-permute-done.9.rest_0_), channel_id=1, source_target_pairs={{0,8},{8,16},{16,24},{24,32},{32,40},{40,48},{48,56},{56,0},{1,9},... | collective-permute-start | bytes 1376264 | tf_op jit(solution)/shard_map/ppermute | solution.py:620
  149.3 14.9 %collective-permute-start.24 = (s32[896,128]{1,0:T(8,128)}, s32[896,128]{1,0:T(8,128)}, u32[]{:S(2)}, u32[]{:S(2)}) collective-permute-start(s32[896,128]{1,0:T(8,128)} %collective-permute-done.15.rest_3_), channel_id=1, source_target_pairs={{0,56},{8,0},{16,8},{24,16},{32,24},{40,32},{48,40},{56,48},{1,57}... | collective-permute-start | bytes 1376264 | tf_op jit(solution)/shard_map/ppermute | solution.py:620
  152.6 27.0 %collective-permute-start.23 = (s32[1408,128]{1,0:T(8,128)}, s32[1408,128]{1,0:T(8,128)}, u32[]{:S(2)}, u32[]{:S(2)}) collective-permute-start(s32[1408,128]{1,0:T(8,128)} %collective-permute-done.11.rest_1_), channel_id=1, source_target_pairs={{0,8},{8,16},{16,24},{24,32},{32,40},{40,48},{48,56},{56,0},{1,9},... | collective-permute-start | bytes 2162696 | tf_op jit(solution)/shard_map/ppermute | solution.py:620
  152.6 27.0 %collective-permute-start.25 = (s32[1408,128]{1,0:T(8,128)}, s32[1408,128]{1,0:T(8,128)}, u32[]{:S(2)}, u32[]{:S(2)}) collective-permute-start(s32[1408,128]{1,0:T(8,128)} %collective-permute-done.17.rest_4_), channel_id=1, source_target_pairs={{0,56},{8,0},{16,8},{24,16},{32,24},{40,32},{48,40},{56,48},{1,57}... | collective-permute-start | bytes 2162696 | tf_op jit(solution)/shard_map/ppermute | solution.py:620
  164.2 24.7 %collective-permute-start.26 = (s32[896,128]{1,0:T(8,128)}, s32[896,128]{1,0:T(8,128)}, u32[]{:S(2)}, u32[]{:S(2)}) collective-permute-start(s32[896,128]{1,0:T(8,128)} %collective-permute-done.22.rest_0_), channel_id=1, source_target_pairs={{0,8},{8,16},{16,24},{24,32},{32,40},{40,48},{48,56},{56,0},{1,9},... | collective-permute-start | bytes 1376264 | tf_op jit(solution)/shard_map/ppermute | solution.py:620
  164.2 24.7 %collective-permute-start.27 = (s32[896,128]{1,0:T(8,128)}, s32[896,128]{1,0:T(8,128)}, u32[]{:S(2)}, u32[]{:S(2)}) collective-permute-start(s32[896,128]{1,0:T(8,128)} %collective-permute-done.24.rest_2_), channel_id=1, source_target_pairs={{0,56},{8,0},{16,8},{24,16},{32,24},{40,32},{48,40},{56,48},{1,57}... | collective-permute-start | bytes 1376264 | tf_op jit(solution)/shard_map/ppermute | solution.py:620
  191.9 109.1 %all-to-all-start.4 = ((s32[32,12,16,128]{3,2,1,0:T(8,128)}), s32[32,12,16,128]{3,2,1,0:T(8,128)S(1)}, u32[]{:S(2)}, u32[]{:S(2)}) async-start(s32[32,12,16,128]{3,2,1,0:T(8,128)} %bitcast.56), calls=%async_computation.4 | async-start | bytes 6291456 | tf_op jit(solution)/shard_map/all_to_all | solution.py:615
  202.5 1.3 collective-permute-start
  203.8 33.2 %collective-permute-start.1 = (s32[4096]{0:T(1024)S(1)}, s32[4096]{0:T(1024)S(1)}, u32[]{:S(2)}, u32[]{:S(2)}) collective-permute-start(s32[4096]{0:T(1024)S(1)} %add.134), channel_id=1, source_target_pairs={{0,2},{2,4},{4,6},{6,0},{1,3},{3,5},{5,7},{7,1},{8,10},{10,12},{12... | collective-permute-start | bytes 49160 | tf_op jit(solution)/shard_map/ppermute | solution.py:620
  237.0 5.2 %collective-permute-start.2 = (s32[4096]{0:T(1024)S(1)}, s32[4096]{0:T(1024)S(1)}, u32[]{:S(2)}, u32[]{:S(2)}) collective-permute-start(s32[4096]{0:T(1024)S(1)} %add.135), channel_id=1, source_target_pairs={{0,4},{2,6},{4,0},{6,2},{1,5},{3,7},{5,1},{7,3},{8,12},{10,14},{12... | collective-permute-start | bytes 49160 | tf_op jit(solution)/shard_map/ppermute | solution.py:620
  242.3 3.7 %collective-permute-start.3 = (s32[4096]{0:T(1024)S(1)}, s32[4096]{0:T(1024)S(1)}, u32[]{:S(2)}, u32[]{:S(2)}) collective-permute-start(s32[4096]{0:T(1024)S(1)} %add.136), channel_id=1, source_target_pairs={{0,64},{64,128},{128,192},{192,0},{1,65},{65,129},{129,193},{193,1... | collective-permute-start | bytes 49160 | tf_op jit(solution)/shard_map/ppermute | solution.py:620
  246.0 5.2 %collective-permute-start.4 = (s32[4096]{0:T(1024)S(1)}, s32[4096]{0:T(1024)S(1)}, u32[]{:S(2)}, u32[]{:S(2)}) collective-permute-start(s32[4096]{0:T(1024)S(1)} %add.137), channel_id=1, source_target_pairs={{0,128},{64,192},{128,0},{192,64},{1,129},{65,193},{129,1},{193,65... | collective-permute-start | bytes 49160 | tf_op jit(solution)/shard_map/ppermute | solution.py:620
  251.3 4.9 %collective-permute-start.5 = (s32[4096]{0:T(1024)S(1)}, s32[4096]{0:T(1024)S(1)}, u32[]{:S(2)}, u32[]{:S(2)}) collective-permute-start(s32[4096]{0:T(1024)S(1)} %add.138), channel_id=1, source_target_pairs={{0,8},{8,16},{16,24},{24,32},{32,40},{40,48},{48,56},{56,0},{1,9},... | collective-permute-start | bytes 49160 | tf_op jit(solution)/shard_map/ppermute | solution.py:620
  256.2 5.9 %collective-permute-start.6 = (s32[4096]{0:T(1024)S(1)}, s32[4096]{0:T(1024)S(1)}, u32[]{:S(2)}, u32[]{:S(2)}) collective-permute-start(s32[4096]{0:T(1024)S(1)} %add.139), channel_id=1, source_target_pairs={{0,16},{8,24},{16,32},{24,40},{32,48},{40,56},{48,0},{56,8},{1,17}... | collective-permute-start | bytes 49160 | tf_op jit(solution)/shard_map/ppermute | solution.py:620
  262.1 19.1 %collective-permute-start.7 = (s32[4096]{0:T(1024)S(1)}, s32[4096]{0:T(1024)S(1)}, u32[]{:S(2)}, u32[]{:S(2)}) collective-permute-start(s32[4096]{0:T(1024)S(1)} %add.140), channel_id=1, source_target_pairs={{0,32},{8,40},{16,48},{24,56},{32,0},{40,8},{48,16},{56,24},{1,33}... | collective-permute-start | bytes 49160 | tf_op jit(solution)/shard_map/ppermute | solution.py:620
  (6 other events, 83.2 us)
